TPU v7x, 512 devices: a whole 4x4x16 slice. The times are simulated.
512 devices in a mesh: mode: 128 (over y, z, core), cores: 4 (over x).
Axes of the slice: x: 4, y: 4, z: 16, core: 2. Of those that a mesh axis runs over, the one named last changes fastest.
Arguments:
- train_cores: bfloat16 [4, 400, 512, 400], P('cores', None, 'mode'), may hold values from -0.06187184 to 0.06187184
- sketch_cores: bfloat16 [4, 100, 512, 100], P('cores', None, 'mode'), may hold values from -0.3125 to 0.3125
- left_interface: float32 [100, 400], replicated, may hold values from -6 to 6
- right_sketch: bfloat16 [400, 100], replicated, may hold values from -6 to 6
Outputs:
- frames: bfloat16 [4, 100, 512, 100], P('cores', None, 'mode')
- interfaces: float32 [4, 100, 400], P('cores')
All inputs are finite; a program needn't handle non-finite values.
Results may differ from a plain program's by a relative error of at most 0.019.
Values may be sent and summed in bfloat16 or wider, within the bound.
No kernel may reach another device: no remote copies, remote signals or barrier semaphores. Data moves between devices by JAX's collectives and lax.ppermute only.
A program may use at most 64 MiB of HBM per device.

v0:
```python
import math

import jax
import jax.numpy as jnp
from jax import lax
from jax.sharding import Mesh
from jax.sharding import PartitionSpec as P

MODE = ("mode_0", "mode_1", "mode_2")


def padded_to(lines, size):
    spare = -lines.shape[0] % size
    if not spare:
        return lines
    return jnp.concatenate([lines, jnp.zeros((spare, *lines.shape[1:]), lines.dtype)])


def sent_to_all(shard, axis):
    copies = jnp.broadcast_to(shard, (lax.axis_size(axis), *shard.shape))
    return lax.all_to_all(copies, axis, split_axis=0, concat_axis=0, tiled=True)


def laid_out(tiles, dim):
    shape = list(tiles.shape[1:])
    shape[dim] *= tiles.shape[0]
    return jnp.moveaxis(tiles, 0, dim).reshape(shape)


def whole_of(shard, axes, dim):
    far, near = axes
    initial = sent_to_all(shard, far)
    tiles = jnp.swapaxes(sent_to_all(initial, near), 0, 1)
    return laid_out(tiles.reshape(-1, *shard.shape), dim)


def cut_along(shard, dim, size):
    shape = shard.shape
    tiles = shard.reshape(*shape[:dim], size, shape[dim] // size, *shape[dim + 1 :])
    return jnp.moveaxis(tiles, dim, 0)


def sum_at_owner(shard, axis, dim):
    tiles = cut_along(shard, dim, lax.axis_size(axis))
    arrived = lax.all_to_all(tiles, axis, split_axis=0, concat_axis=0, tiled=True)
    return arrived.sum(axis=0)


def summed_rows(shard, axes, dim):
    far, near = axes
    tiles = cut_along(shard, dim, lax.axis_size(far))
    nearer = sum_at_owner(tiles, near, dim + 1)
    arrived = lax.all_to_all(nearer, far, split_axis=0, concat_axis=0, tiled=True)
    return arrived.sum(axis=0)


def nested_sum(shard, axes):
    lines = shard.reshape(-1)
    padded = padded_to(lines, lax.axis_size(axes[0]) * lax.axis_size(axes[1]))
    whole = whole_of(summed_rows(padded, axes, 0), axes, 0)
    return lax.slice_in_dim(whole, 0, len(lines)).reshape(shard.shape)


def from_behind(shard, axis, by):
    size = lax.axis_size(axis)
    pairs = [(i, i + by) for i in range(size) if 0 <= i + by < size]
    return lax.ppermute(shard, axis, pairs)


def sent_and_summed(shard, axis, dim):
    tiles = cut_along(shard, dim, lax.axis_size(axis))
    arrived = lax.all_to_all(tiles, axis, split_axis=0, concat_axis=0, tiled=True)
    return arrived.astype(jnp.float32).sum(axis=0)


def sum_in_two_steps(shard, axes, dim):
    far, near = axes
    own = sent_and_summed(cut_along(shard, dim, lax.axis_size(far)), near, dim + 1)
    return jnp.sum(
        lax.all_to_all(own.astype(jnp.bfloat16), far, 0, 0, tiled=True).astype(jnp.float32), axis=0
    )


def nested_sum_2(shard, axes):
    lines = shard.reshape(-1)
    padded = padded_to(lines, lax.axis_size(axes[0]) * lax.axis_size(axes[1]))
    whole = whole_of(sum_in_two_steps(padded, axes, 0).astype(jnp.bfloat16), axes, 0)
    return lax.slice_in_dim(whole, 0, len(lines)).reshape(shard.shape).astype(jnp.float32)


def body(train_cores, sketch_cores, left_interface, right_sketch):
    my_core = train_cores[0]
    my_sketch = sketch_cores[0]
    rank_size = my_core.shape[0]
    mode_local = my_core.shape[1]
    sketch_size = my_sketch.shape[0]
    group_index = lax.axis_index("cores")
    group_count = lax.axis_size("cores")
    final_group = group_count - 1
    flat_core = my_core.reshape(rank_size * mode_local, rank_size)
    sketch_flat = my_sketch.reshape(sketch_size, mode_local * sketch_size)
    sketch = right_sketch
    for round_index in range(group_count - 1):
        partial_value = jnp.dot(flat_core, sketch, preferred_element_type=jnp.float32).astype(
            jnp.bfloat16
        )
        partial_value = partial_value.reshape(rank_size, mode_local * sketch_size)
        local_term = lax.dot_general(
            partial_value, sketch_flat, (((1,), (1,)), ((), ())), preferred_element_type=jnp.float32
        )
        summed = nested_sum(local_term, (("mode_0", "mode_1"), "mode_2"))
        received = from_behind(summed.astype(jnp.bfloat16), "cores", -1)
        sketch = jnp.where(group_index == final_group, right_sketch, received)
    frame_scale = math.sqrt(sketch_size * mode_local * lax.axis_size(MODE))
    wide_core = my_core.reshape(rank_size, mode_local * rank_size)
    interface = left_interface
    for round_index in range(group_count):
        carry_low = interface.astype(jnp.bfloat16)
        built = jnp.dot(carry_low, wide_core, preferred_element_type=jnp.float32)
        built = built.astype(jnp.bfloat16).reshape(sketch_size * mode_local, rank_size)
        images = jnp.dot(built, sketch, preferred_element_type=jnp.float32)
        core_local = lax.dot_general(
            built, built, (((0,), (0,)), ((), ())), preferred_element_type=jnp.float32
        )
        core_square = nested_sum_2(
            core_local.astype(jnp.bfloat16), (("mode_0", "mode_1"), "mode_2")
        )
        sketch_wide = sketch.astype(jnp.float32)
        projected = lax.dot_general(
            sketch_wide, core_square, (((0,), (0,)), ((), ())), precision=lax.Precision.HIGHEST
        )
        gram_matrix = jnp.dot(projected, sketch_wide, precision=lax.Precision.HIGHEST)
        chol_lower = jnp.linalg.cholesky(gram_matrix)
        frame_rows = lax.linalg.triangular_solve(chol_lower, images.T, left_side=True, lower=True)
        next_interface = lax.linalg.triangular_solve(
            chol_lower, projected, left_side=True, lower=True
        )
        frame_out = (frame_rows.T * frame_scale).astype(jnp.bfloat16)
        interface_out = next_interface
        if round_index < group_count - 1:
            passed = from_behind(next_interface.astype(jnp.bfloat16), "cores", 1)
            interface = jnp.where(group_index == 0, left_interface, passed.astype(jnp.float32))
    frames = frame_out.reshape(1, sketch_size, mode_local, sketch_size)
    interfaces = interface_out.reshape(1, sketch_size, rank_size)
    return (frames, interfaces)


def solution(mesh):
    split = Mesh(
        mesh.devices.reshape(4, 16, 2, mesh.shape["cores"]), ("mode_0", "mode_1", "mode_2", "cores")
    )
    placed = (P("cores", None, MODE, None), P("cores", None, MODE, None), P(), P())
    return jax.shard_map(
        body,
        mesh=split,
        in_specs=placed,
        out_specs=(P("cores", None, MODE, None), P("cores", None, None)),
        check_vma=False,
    )
```

profile of v0, /device:TPU:7, one launch (start us, length us, event | category | flops | bytes accessed | tf_op | source)
XLA Modules:
  0.0 535.2 jit_solution(12062699144036527548)
XLA Ops:
  10.1 32.0 %all_to_all.197 = f32[64,1,313]{2,1,0:T(1,128)S(1)} all-to-all(f32[64,1,313]{2,1,0:T(1,128)S(1)} %all_to_all.127), channel_id=1, replica_groups=mesh['mode_0'=4,'mode_1'=16,'mode_2'=2,'cores'=4] {'mode_0','mode_1'}, dimensions={0} | all-to-all | bytes 160256 | tf_op jit(solution)/shard_map/all_to_all | solution.py:53
  42.3 20.1 %all_to_all.198 = bf16[64,1,313]{2,1,0:T(2,128)(2,1)S(1)} all-to-all(bf16[64,1,313]{2,1,0:T(2,128)(2,1)S(1)} %broadcast_in_dim.43), channel_id=1, replica_groups=mesh['mode_0'=4,'mode_1'=16,'mode_2'=2,'cores'=4] {'mode_0','mode_1'}, dimensions={0} | all-to-all | bytes 80128 | tf_op jit(solution)/shard_map/all_to_all | solution.py:21
  89.6 10.3 %all-to-all-done.5 = f32[64,1,313]{2,1,0:T(1,128)S(1)} async-done(((f32[64,1,313]{2,1,0:T(1,128)}), f32[64,1,313]{2,1,0:T(1,128)S(1)}, u32[]{:S(2)}, u32[]{:S(2)}) %all-to-all-start.5) | async-done | bytes 80160 | tf_op jit(solution)/shard_map/all_to_all | solution.py:53
  110.6 10.4 %all-to-all-done.6 = bf16[64,1,313]{2,1,0:T(2,128)(2,1)S(1)} async-done(((bf16[64,1,313]{2,1,0:T(2,128)(2,1)}), bf16[64,1,313]{2,1,0:T(2,128)(2,1)S(1)}, u32[]{:S(2)}, u32[]{:S(2)}) %all-to-all-start.6) | async-done | bytes 40096 | tf_op jit(solution)/shard_map/all_to_all | solution.py:21
  161.1 11.5 %all-to-all-done.9 = f32[64,1,313]{2,1,0:T(1,128)S(1)} async-done(((f32[64,1,313]{2,1,0:T(1,128)}), f32[64,1,313]{2,1,0:T(1,128)S(1)}, u32[]{:S(2)}, u32[]{:S(2)}) %all-to-all-start.9) | async-done | bytes 80160 | tf_op jit(solution)/shard_map/all_to_all | solution.py:53
  179.2 15.0 %all-to-all-done.13 = bf16[64,2,625]{2,1,0:T(2,128)(2,1)S(1)} async-done(((bf16[64,2,625]{2,1,0:T(2,128)(2,1)}), bf16[64,2,625]{2,1,0:T(2,128)(2,1)S(1)}, u32[]{:S(2)}, u32[]{:S(2)}) %all-to-all-start.13) | async-done | bytes 160032 | tf_op jit(solution)/shard_map/all_to_all | solution.py:80
  194.9 7.4 %all-to-all-start.10 = ((bf16[64,1,313]{2,1,0:T(2,128)(2,1)}), bf16[64,1,313]{2,1,0:T(2,128)(2,1)S(1)}, u32[]{:S(2)}, u32[]{:S(2)}) async-start(bf16[64,1,313]{2,1,0:T(2,128)(2,1)} %broadcast_in_dim.47), calls=%async_computation.10 | async-start | bytes 196608 | tf_op jit(solution)/shard_map/all_to_all | solution.py:21
  205.6 10.5 %all-to-all-done.10 = bf16[64,1,313]{2,1,0:T(2,128)(2,1)S(1)} async-done(((bf16[64,1,313]{2,1,0:T(2,128)(2,1)}), bf16[64,1,313]{2,1,0:T(2,128)(2,1)S(1)}, u32[]{:S(2)}, u32[]{:S(2)}) %all-to-all-start.10) | async-done | bytes 40096 | tf_op jit(solution)/shard_map/all_to_all | solution.py:21
  230.4 12.6 %all-to-all-done.14 = bf16[64,2,625]{2,1,0:T(2,128)(2,1)S(1)} async-done(((bf16[64,2,625]{2,1,0:T(2,128)(2,1)}), bf16[64,2,625]{2,1,0:T(2,128)(2,1)S(1)}, u32[]{:S(2)}, u32[]{:S(2)}) %all-to-all-start.14) | async-done | bytes 160032 | tf_op jit(solution)/shard_map/all_to_all | solution.py:21
  251.1 9.1 %cholesky.74 = f32[100,100]{1,0:T(8,128)S(1)} custom-call(f32[100,100]{1,0:T(8,128)S(1)} %fusion.23), custom_call_target="Cholesky" | custom-call | tf_op jit(solution)/shard_map/jit(cholesky)/cholesky | solution.py:133
  261.6 7.7 %custom-call.9 = f32[1,100,100]{1,2,0:T(8,128)S(1)} custom-call(f32[1,100,100]{2,1,0:T(8,128)S(1)} %fusion.11), custom_call_target="InvertDiagBlocksLowerTriangular" | custom-call | tf_op jit(solution)/shard_map/triangular_solve/custom-call.0 | solution.py:135
  283.6 21.7 %all_to_all.206 = bf16[64,2,625]{2,1,0:T(2,128)(2,1)S(1)} all-to-all(bf16[64,2,625]{2,1,0:T(2,128)(2,1)S(1)} %reshape.134), channel_id=1, replica_groups=mesh['mode_0'=4,'mode_1'=16,'mode_2'=2,'cores'=4] {'mode_0','mode_1'}, dimensions={0} | all-to-all | bytes 320000 | tf_op jit(solution)/shard_map/all_to_all | solution.py:80
  308.0 21.9 %all_to_all.207 = bf16[64,2,625]{2,1,0:T(2,128)(2,1)S(1)} all-to-all(bf16[64,2,625]{2,1,0:T(2,128)(2,1)S(1)} %reshape.136), channel_id=1, replica_groups=mesh['mode_0'=4,'mode_1'=16,'mode_2'=2,'cores'=4] {'mode_0','mode_1'}, dimensions={0} | all-to-all | bytes 320000 | tf_op jit(solution)/shard_map/all_to_all | solution.py:21
  338.9 9.1 %cholesky.85 = f32[100,100]{1,0:T(8,128)S(1)} custom-call(f32[100,100]{1,0:T(8,128)S(1)} %fusion.21), custom_call_target="Cholesky" | custom-call | tf_op jit(solution)/shard_map/jit(cholesky)/cholesky | solution.py:133
  349.4 7.7 %custom-call.10 = f32[1,100,100]{1,2,0:T(8,128)S(1)} custom-call(f32[1,100,100]{2,1,0:T(8,128)S(1)} %fusion.12), custom_call_target="InvertDiagBlocksLowerTriangular" | custom-call | tf_op jit(solution)/shard_map/triangular_solve/custom-call.0 | solution.py:135
  371.4 21.3 %all_to_all.210 = bf16[64,2,625]{2,1,0:T(2,128)(2,1)S(1)} all-to-all(bf16[64,2,625]{2,1,0:T(2,128)(2,1)S(1)} %reshape.138), channel_id=1, replica_groups=mesh['mode_0'=4,'mode_1'=16,'mode_2'=2,'cores'=4] {'mode_0','mode_1'}, dimensions={0} | all-to-all | bytes 320000 | tf_op jit(solution)/shard_map/all_to_all | solution.py:80
  395.4 21.8 %all_to_all.211 = bf16[64,2,625]{2,1,0:T(2,128)(2,1)S(1)} all-to-all(bf16[64,2,625]{2,1,0:T(2,128)(2,1)S(1)} %reshape.140), channel_id=1, replica_groups=mesh['mode_0'=4,'mode_1'=16,'mode_2'=2,'cores'=4] {'mode_0','mode_1'}, dimensions={0} | all-to-all | bytes 320000 | tf_op jit(solution)/shard_map/all_to_all | solution.py:21
  426.2 9.1 %cholesky.96 = f32[100,100]{1,0:T(8,128)S(1)} custom-call(f32[100,100]{1,0:T(8,128)S(1)} %fusion.19), custom_call_target="Cholesky" | custom-call | tf_op jit(solution)/shard_map/jit(cholesky)/cholesky | solution.py:133
  436.7 7.7 %custom-call.11 = f32[1,100,100]{1,2,0:T(8,128)S(1)} custom-call(f32[1,100,100]{2,1,0:T(8,128)S(1)} %fusion.13), custom_call_target="InvertDiagBlocksLowerTriangular" | custom-call | tf_op jit(solution)/shard_map/triangular_solve/custom-call.0 | solution.py:135
  458.7 21.5 %all_to_all.214 = bf16[64,2,625]{2,1,0:T(2,128)(2,1)S(1)} all-to-all(bf16[64,2,625]{2,1,0:T(2,128)(2,1)S(1)} %reshape.142), channel_id=1, replica_groups=mesh['mode_0'=4,'mode_1'=16,'mode_2'=2,'cores'=4] {'mode_0','mode_1'}, dimensions={0} | all-to-all | bytes 320000 | tf_op jit(solution)/shard_map/all_to_all | solution.py:80
  483.5 7.0 %all-to-all-start.26 = ((bf16[64,2,625]{2,1,0:T(2,128)(2,1)}), bf16[64,2,625]{2,1,0:T(2,128)(2,1)S(1)}, u32[]{:S(2)}, u32[]{:S(2)}) async-start(bf16[64,2,625]{2,1,0:T(2,128)(2,1)} %reshape.144), calls=%async_computation.26 | async-start | bytes 327680 | tf_op jit(solution)/shard_map/all_to_all | solution.py:21
  490.8 14.7 %all-to-all-done.26 = bf16[64,2,625]{2,1,0:T(2,128)(2,1)S(1)} async-done(((bf16[64,2,625]{2,1,0:T(2,128)(2,1)}), bf16[64,2,625]{2,1,0:T(2,128)(2,1)S(1)}, u32[]{:S(2)}, u32[]{:S(2)}) %all-to-all-start.26) | async-done | bytes 160032 | tf_op jit(solution)/shard_map/all_to_all | solution.py:21
  514.5 9.1 %cholesky.107 = f32[100,100]{1,0:T(8,128)S(1)} custom-call(f32[100,100]{1,0:T(8,128)S(1)} %fusion.17), custom_call_target="Cholesky" | custom-call | tf_op jit(solution)/shard_map/jit(cholesky)/cholesky | solution.py:133
  525.0 7.7 %custom-call.12 = f32[1,100,100]{1,2,0:T(8,128)S(1)} custom-call(f32[1,100,100]{2,1,0:T(8,128)S(1)} %fusion.14), custom_call_target="InvertDiagBlocksLowerTriangular" | custom-call | tf_op jit(solution)/shard_map/triangular_solve/custom-call.0 | solution.py:134
  (201 shorter events, 206.3 us)
Async XLA Ops:
  0.6 2.9 copy-start.1
  3.5 1.2 copy-start.2
  69.3 4.3 collective-permute-start
  81.3 18.6 %all-to-all-start.5 = ((f32[64,1,313]{2,1,0:T(1,128)}), f32[64,1,313]{2,1,0:T(1,128)S(1)}, u32[]{:S(2)}, u32[]{:S(2)}) async-start(f32[64,1,313]{2,1,0:T(1,128)} %all_to_all.133), calls=%async_computation.5 | async-start | bytes 196608 | tf_op jit(solution)/shard_map/all_to_all | solution.py:53
  86.1 21.1 %copy-start = (f32[100,400]{0,1:T(8,128)S(1)}, f32[100,400]{0,1:T(8,128)}, u32[]{:S(2)}) copy-start(f32[100,400]{0,1:T(8,128)} %param.9) | copy-start | bytes 480004
  100.7 20.3 %all-to-all-start.6 = ((bf16[64,1,313]{2,1,0:T(2,128)(2,1)}), bf16[64,1,313]{2,1,0:T(2,128)(2,1)S(1)}, u32[]{:S(2)}, u32[]{:S(2)}) async-start(bf16[64,1,313]{2,1,0:T(2,128)(2,1)} %broadcast_in_dim.45), calls=%async_computation.6 | async-start | bytes 196608 | tf_op jit(solution)/shard_map/all_to_all | solution.py:21
  129.7 11.3 %collective-permute-start.1 = (bf16[400,100]{1,0:T(8,128)(2,1)S(1)}, bf16[400,100]{1,0:T(8,128)(2,1)}, u32[]{:S(2)}, u32[]{:S(2)}) collective-permute-start(bf16[400,100]{1,0:T(8,128)(2,1)S(1)} %convert_element_type.115), channel_id=1, source_target_pairs={{1,0},{2,1},{3,2},{5,4},{6,5},{7,6},{9,8},{10,9},{11,10},{13,12},{... | collective-permute-start | bytes 240008 | tf_op jit(solution)/shard_map/ppermute | solution.py:67
  149.0 5.0 all-to-all-start.12
  154.0 18.6 %all-to-all-start.9 = ((f32[64,1,313]{2,1,0:T(1,128)}), f32[64,1,313]{2,1,0:T(1,128)S(1)}, u32[]{:S(2)}, u32[]{:S(2)}) async-start(f32[64,1,313]{2,1,0:T(1,128)} %all_to_all.139), calls=%async_computation.9 | async-start | bytes 196608 | tf_op jit(solution)/shard_map/all_to_all | solution.py:53
  172.6 21.6 %all-to-all-start.13 = ((bf16[64,2,625]{2,1,0:T(2,128)(2,1)}), bf16[64,2,625]{2,1,0:T(2,128)(2,1)S(1)}, u32[]{:S(2)}, u32[]{:S(2)}) async-start(bf16[64,2,625]{2,1,0:T(2,128)(2,1)} %reshape.130), calls=%async_computation.13 | async-start | bytes 327680 | tf_op jit(solution)/shard_map/all_to_all | solution.py:80
  194.9 21.2 %all-to-all-start.10 = ((bf16[64,1,313]{2,1,0:T(2,128)(2,1)}), bf16[64,1,313]{2,1,0:T(2,128)(2,1)S(1)}, u32[]{:S(2)}, u32[]{:S(2)}) async-start(bf16[64,1,313]{2,1,0:T(2,128)(2,1)} %broadcast_in_dim.47), calls=%async_computation.10 | async-start | bytes 196608 | tf_op jit(solution)/shard_map/all_to_all | solution.py:21
  222.5 20.5 %all-to-all-start.14 = ((bf16[64,2,625]{2,1,0:T(2,128)(2,1)}), bf16[64,2,625]{2,1,0:T(2,128)(2,1)S(1)}, u32[]{:S(2)}, u32[]{:S(2)}) async-start(bf16[64,2,625]{2,1,0:T(2,128)(2,1)} %reshape.132), calls=%async_computation.14 | async-start | bytes 327680 | tf_op jit(solution)/shard_map/all_to_all | solution.py:21
  228.0 22.3 %collective-permute-start.2 = (bf16[400,100]{1,0:T(8,128)(2,1)S(1)}, bf16[400,100]{1,0:T(8,128)(2,1)S(1)}, u32[]{:S(2)}, u32[]{:S(2)}) collective-permute-start(bf16[400,100]{1,0:T(8,128)(2,1)S(1)} %convert_element_type.118), channel_id=1, source_target_pairs={{1,0},{2,1},{3,2},{5,4},{6,5},{7,6},{9,8},{10,9},{11,10},{13,12},{... | collective-permute-start | bytes 240008 | tf_op jit(solution)/shard_map/ppermute | solution.py:67
  269.6 6.0 %collective-permute-start.3 = (bf16[100,400]{0,1:T(8,128)(2,1)S(1)}, bf16[100,400]{0,1:T(8,128)(2,1)S(1)}, u32[]{:S(2)}, u32[]{:S(2)}) collective-permute-start(bf16[100,400]{0,1:T(8,128)(2,1)S(1)} %convolution_convert_fusion.13), channel_id=1, source_target_pairs={{0,1},{1,2},{2,3},{4,5},{5,6},{6,7},{8,9},{9,10},{10,11},{12,13},{... | collective-permute-start | bytes 240008 | tf_op jit(solution)/shard_map/ppermute | solution.py:67
  357.4 6.0 %collective-permute-start.4 = (bf16[100,400]{0,1:T(8,128)(2,1)S(1)}, bf16[100,400]{0,1:T(8,128)(2,1)S(1)}, u32[]{:S(2)}, u32[]{:S(2)}) collective-permute-start(bf16[100,400]{0,1:T(8,128)(2,1)S(1)} %convolution_convert_fusion.12), channel_id=1, source_target_pairs={{0,1},{1,2},{2,3},{4,5},{5,6},{6,7},{8,9},{9,10},{10,11},{12,13},{... | collective-permute-start | bytes 240008 | tf_op jit(solution)/shard_map/ppermute | solution.py:67
  444.7 6.0 %collective-permute-start.5 = (bf16[100,400]{0,1:T(8,128)(2,1)S(1)}, bf16[100,400]{0,1:T(8,128)(2,1)S(1)}, u32[]{:S(2)}, u32[]{:S(2)}) collective-permute-start(bf16[100,400]{0,1:T(8,128)(2,1)S(1)} %convolution_convert_fusion.11), channel_id=1, source_target_pairs={{0,1},{1,2},{2,3},{4,5},{5,6},{6,7},{8,9},{9,10},{10,11},{12,13},{... | collective-permute-start | bytes 240008 | tf_op jit(solution)/shard_map/ppermute | solution.py:67
  483.5 22.0 %all-to-all-start.26 = ((bf16[64,2,625]{2,1,0:T(2,128)(2,1)}), bf16[64,2,625]{2,1,0:T(2,128)(2,1)S(1)}, u32[]{:S(2)}, u32[]{:S(2)}) async-start(bf16[64,2,625]{2,1,0:T(2,128)(2,1)} %reshape.144), calls=%async_computation.26 | async-start | bytes 327680 | tf_op jit(solution)/shard_map/all_to_all | solution.py:21
where the time goes:
time: 545 us; the launch traced here: 535 us
  blocking collectives  234 us (43%)
  waiting for transfers between devices  101 us (19%)
  other arithmetic  84.2 us (15%)
  starting transfers between devices  59.1 us (11%)
  local copies, waits for them, and re-layouts  40.1 us (7%)
  matrix products  14.7 us (3%)
    all_to_all x10, blocking collectives, sent_to_all(): return lax.all_to_all(copies, axis, split_axis=0, concat_axis=0, tiled=True)  110 us
    all_to_all x3, blocking collectives, sum_in_two_steps(): lax.all_to_all(own.astype(jnp.bfloat16), far, 0, 0, tiled=True)  64.6 us
    all_to_all x4, waiting for transfers between devices, sent_to_all(): return lax.all_to_all(copies, axis, split_axis=0, concat_axis=0, tiled=True)  48.1 us
    another operation x12, other arithmetic, body(): chol_lower = jnp.linalg.cholesky(gram_matrix)  39.3 us
    all_to_all x1, blocking collectives, summed_rows(): lax.all_to_all(nearer, far, split_axis=0, concat_axis=0, tiled=True)  32 us
    all_to_all x4, starting transfers between devices, sent_to_all(): return lax.all_to_all(copies, axis, split_axis=0, concat_axis=0, tiled=True)  25.6 us
    another operation x6, other arithmetic, body(): lax.linalg.triangular_solve(chol_lower, projected, left_side=True, lower=...  25 us
    all_to_all x2, waiting for transfers between devices, summed_rows(): lax.all_to_all(nearer, far, split_axis=0, concat_axis=0, tiled=True)  21.8 us
  transfers between devices with their start and end apart: 14, of which 12 were waited for; matrix products, arithmetic and copies ran while one was open for 4% of the time, Pallas kernels for 0%

commit v1 on v0

v1 whole, which is shorter than its diff:
```python
import math

import jax
import jax.numpy as jnp
from jax import lax
from jax.experimental import pallas as pl
from jax.experimental.pallas import tpu as pltpu
from jax.sharding import Mesh
from jax.sharding import PartitionSpec as P

AXES = ("y", "zh", "zl", "c", "x")
MODE = ("y", "zh", "zl", "c")
NEAR = ("y", "zl", "c")
RANK = 400
SKETCH = 100
ROWS = 128
LANES = 512
F32 = jnp.float32
BF16 = jnp.bfloat16
PARAMS = pltpu.CompilerParams(vmem_limit_bytes=24 * 1024 * 1024)


def dot(a, b, ca, cb, precision=None):
    return lax.dot_general(
        a, b, (((ca,), (cb,)), ((), ())), precision=precision, preferred_element_type=F32
    )


def inverse_factor(gram):
    size = gram.shape[0]
    count = -(-size // 8)
    padded = jnp.pad(gram, ((0, count * 8 - size), (0, 128 - size)))
    tiles = [padded[8 * t : 8 * t + 8] for t in range(count)]
    lane = lax.broadcasted_iota(jnp.int32, (8, 128), 1)
    sub = lax.broadcasted_iota(jnp.int32, (8, 128), 0)
    for j in range(size):
        own, line = divmod(j, 8)
        pivot = tiles[own][line : line + 1]
        scale = 1.0 / pivot[:, j : j + 1]
        unit = jnp.where(lane[:1] == j, 1.0, pivot)
        for t in range(own, count):
            tile = tiles[t]
            factor = tile[:, j : j + 1] * scale
            new = jnp.where(lane == j, 0.0, tile) - factor * unit
            tiles[t] = jnp.where(sub > line, new, tile) if t == own else new
    done = []
    for t in range(count):
        row = sub + 8 * t
        diagonal = jnp.sum(jnp.where(lane == row, tiles[t], 0.0), axis=1, keepdims=True)
        lower = jnp.where(lane < row, tiles[t], jnp.where(lane == row, 1.0, 0.0))
        done.append(lower * lax.rsqrt(diagonal))
    return jnp.concatenate(done, axis=0)[:size, :size]


def symmetric_gram(m_value, sketch_t):
    return 0.5 * (dot(m_value, sketch_t, 1, 1) + dot(sketch_t, m_value, 1, 1))


def sketch_term(core_ref, sketch_core_ref, sketch_t):
    total = None
    for i in range(core_ref.shape[0]):
        partial = dot(core_ref[i], sketch_t, 1, 1).astype(BF16)
        term = dot(sketch_core_ref[i], partial, 1, 1)
        total = term if total is None else total + term
    return total


def first_kernel(x_ref, core_ref, sketch_core_ref, right_ref, left_ref, out_ref, rest_ref):
    out_ref[...] = jnp.zeros((ROWS, LANES), BF16)
    rest_ref[...] = jnp.zeros((ROWS, LANES), BF16)

    @pl.when(x_ref[0] != 0)
    def _():
        out_ref[:SKETCH, :RANK] = sketch_term(
            core_ref, sketch_core_ref, right_ref[...]
        ).astype(BF16)

    @pl.when(x_ref[0] == 0)
    def _():
        square = None
        for i in range(core_ref.shape[0]):
            built = dot(left_ref[...], core_ref[i], 1, 0).astype(BF16)
            term = dot(built, built, 0, 0)
            square = term if square is None else square + term
        square = square.astype(BF16)
        out_ref[:, :RANK] = square[:128]
        rest_ref[:, :256] = square[128:256, 128:384]
        rest_ref[:, 256:384] = square[256:384, 256:384]
        rest_ref[:, 384:400] = square[128:256, 384:400]
        rest_ref[:, 400:416] = square[256:384, 384:400]
        rest_ref[:16, 416:432] = square[384:400, 384:400]


def sketch_kernel(core_ref, sketch_core_ref, sketch_ref, out_ref):
    out_ref[...] = jnp.zeros((ROWS, LANES), BF16)
    out_ref[:SKETCH, :RANK] = sketch_term(
        core_ref, sketch_core_ref, sketch_ref[:SKETCH, :RANK]
    ).astype(BF16)


def last_sketch_kernel(x_ref, core_ref, sketch_core_ref, sketch_ref, rest_ref, out_ref):
    @pl.when(x_ref[0] == 0)
    def _():
        out_ref[...] = rest_ref[...]

    @pl.when(x_ref[0] != 0)
    def _():
        sketch_kernel(core_ref, sketch_core_ref, sketch_ref, out_ref)


def gram_term(core_ref, carry_low, sketch_t):
    total = None
    for i in range(core_ref.shape[0]):
        built = dot(carry_low, core_ref[i], 1, 0).astype(BF16)
        images = dot(built, sketch_t, 1, 1).astype(BF16)
        term = dot(images, built, 0, 0)
        total = term if total is None else total + term
    return total


def project_kernel(m_ref, before_ref, core_ref, sketch_ref, out_ref, carry_ref):
    m_value = m_ref[:SKETCH, :RANK]
    inverse = inverse_factor(symmetric_gram(m_value, before_ref[:SKETCH, :RANK]))
    carry = dot(inverse, m_value.astype(F32), 1, 0, lax.Precision.HIGHEST).astype(BF16)
    carry_ref[...] = carry
    out_ref[...] = jnp.zeros((ROWS, LANES), BF16)
    out_ref[:SKETCH, :RANK] = gram_term(core_ref, carry, sketch_ref[:SKETCH, :RANK]).astype(BF16)


def first_project_kernel(upper_ref, rest_ref, before_ref, core_ref, sketch_ref, out_ref, carry_ref, m0_ref):
    s = before_ref[:SKETCH, :RANK]
    sa, sb, sc, sd = s[:, :128], s[:, 128:256], s[:, 256:384], s[:, 384:400]
    a = upper_ref[:, :RANK]
    b = rest_ref[:, :256]
    c = rest_ref[:, 256:384]
    b_end = rest_ref[:, 384:400]
    c_end = rest_ref[:, 400:416]
    d_end = rest_ref[:16, 416:432]
    over_a = dot(sa, a, 1, 0)
    m0_ref[:, :128] = over_a[:, :128] + dot(s[:, 128:], a[:, 128:], 1, 1)
    m0_ref[:, 128:256] = (
        over_a[:, 128:256] + dot(sb, b[:, :128], 1, 0) + dot(sc, b[:, 128:], 1, 1) + dot(sd, b_end, 1, 1)
    )
    m0_ref[:, 256:384] = over_a[:, 256:384] + dot(sb, b[:, 128:], 1, 0) + dot(sc, c, 1, 0) + dot(sd, c_end, 1, 1)
    m0_ref[:, 384:400] = over_a[:, 384:400] + dot(sb, b_end, 1, 0) + dot(sc, c_end, 1, 0) + dot(sd, d_end, 1, 0)
    m_value = m0_ref[...]
    high = m_value.astype(BF16)
    low = (m_value - high.astype(F32)).astype(BF16)
    inverse = inverse_factor(symmetric_gram(high, s) + symmetric_gram(low, s))
    carry = dot(inverse, m_value, 1, 0, lax.Precision.HIGHEST).astype(BF16)
    carry_ref[...] = carry
    out_ref[...] = jnp.zeros((ROWS, LANES), BF16)
    out_ref[:SKETCH, :RANK] = gram_term(core_ref, carry, sketch_ref[:SKETCH, :RANK]).astype(BF16)


def images_kernel(carry_ref, core_ref, sketch_ref, out_ref):
    for i in range(core_ref.shape[0]):
        built = dot(carry_ref[...], core_ref[i], 1, 0).astype(BF16)
        out_ref[i] = dot(built, sketch_ref[...], 1, 1)


def final_kernel(scale, m_ref, sketch_ref, images_ref, frames_ref, interface_ref):
    m_value = m_ref[...]
    high = m_value.astype(BF16)
    low = (m_value - high.astype(F32)).astype(BF16)
    sketch_t = sketch_ref[...]
    inverse = inverse_factor(symmetric_gram(high, sketch_t) + symmetric_gram(low, sketch_t))
    interface_ref[...] = dot(inverse, m_value, 1, 0, lax.Precision.HIGHEST)
    for i in range(images_ref.shape[0]):
        orth = dot(images_ref[i], inverse, 1, 1, lax.Precision.HIGHEST)
        frames_ref[i] = (orth * scale).astype(BF16)


def call(kernel, *operands, out, scalar=False):
    specs = [pl.BlockSpec(memory_space=pltpu.VMEM) for _ in operands]
    if scalar:
        specs[0] = pl.BlockSpec(memory_space=pltpu.SMEM)
    outs = [jax.ShapeDtypeStruct(shape, kind) for shape, kind in out]
    return pl.pallas_call(
        kernel,
        out_shape=outs,
        in_specs=specs,
        out_specs=[pl.BlockSpec(memory_space=pltpu.VMEM) for _ in outs],
        compiler_params=PARAMS,
    )(*operands)


PAYLOAD = ((ROWS, LANES), BF16)


def everywhere(shard, axes, groups, count):
    copies = jnp.broadcast_to(shard, (count, *shard.shape))
    return lax.all_to_all(copies, axes, 0, 0, axis_index_groups=groups, tiled=True)


def shard_sum(value):
    near = 16
    tiles = value.reshape(near, ROWS // near, LANES)
    arrived = lax.all_to_all(tiles, NEAR, 0, 0, tiled=True)
    return arrived.astype(F32).sum(axis=0).astype(BF16)


def added(pieces):
    return pieces.astype(F32).sum(axis=0).astype(BF16)


def paired(value, pairs, far):
    groups = [[x * far + z for x in pair for z in range(far)] for pair in pairs]
    pieces = everywhere(shard_sum(value), ("x", "zh"), groups, 2 * far)
    return pieces[:far], pieces[far:]


def whole(shard):
    return everywhere(shard, NEAR, None, 16)


def body(train_cores, sketch_cores, left_interface, right_sketch):
    far = lax.axis_size("zh")
    plane = lax.axis_index("x")
    plane_ref = plane.astype(jnp.int32).reshape(1)
    core = jnp.swapaxes(train_cores[0], 0, 1)
    sketch_core = jnp.swapaxes(sketch_cores[0], 0, 1)
    modes = core.shape[0]
    frame_scale = math.sqrt(SKETCH * modes * lax.axis_size(MODE))
    right_t = right_sketch.T
    left_low = left_interface.astype(BF16)

    def full(shard):
        return whole(shard).reshape(ROWS, LANES)

    term, rest = call(
        first_kernel, plane_ref, core, sketch_core, right_t, left_low, out=[PAYLOAD, PAYLOAD], scalar=True
    )
    first = full(added(paired(term, ((3, 2), (0, 1)), far)[0]))
    (term,) = call(sketch_kernel, core, sketch_core, first, out=[PAYLOAD])
    second = full(added(paired(term, ((2, 1), (3, 0)), far)[0]))
    (term,) = call(last_sketch_kernel, plane_ref, core, sketch_core, second, rest, out=[PAYLOAD], scalar=True)
    both = paired(term, ((1, 0), (3, 2)), far)
    arrived = whole(jnp.concatenate([added(both[0]), added(both[1])], axis=0))
    third = arrived[:, :8].reshape(ROWS, LANES)
    rest = arrived[:, 8:].reshape(ROWS, LANES)

    carry_kind = ((SKETCH, RANK), BF16)
    term, carry_1, m_0 = call(
        first_project_kernel, first, rest, third, core, second, out=[PAYLOAD, carry_kind, ((SKETCH, RANK), F32)]
    )
    m_1 = full(added(paired(term, ((1, 2), (0, 3)), far)[0]))
    term, carry_2 = call(project_kernel, m_1, second, core, first, out=[PAYLOAD, carry_kind])
    m_2 = full(added(paired(term, ((2, 3), (0, 1)), far)[0]))
    right_wide = jnp.pad(right_t, ((0, ROWS - SKETCH), (0, LANES - RANK)))
    term, carry_3 = call(project_kernel, m_2, first, core, right_wide, out=[PAYLOAD, carry_kind])
    m_3 = full(added(everywhere(shard_sum(term), "zh", None, far)))

    def cut(value):
        return value[:SKETCH, :RANK]

    def own(zero, one, two, three):
        low = jnp.where(plane == 0, zero, one)
        high = jnp.where(plane == 2, two, three)
        return jnp.where(plane < 2, low, high)

    sketch_t = own(cut(third), cut(second), cut(first), right_t)
    carry = own(left_low, carry_1, carry_2, carry_3)
    (images,) = call(images_kernel, carry, core, sketch_t, out=[((modes, SKETCH, SKETCH), F32)])
    m_own = own(m_0, cut(m_1).astype(F32), cut(m_2).astype(F32), cut(m_3).astype(F32))

    def finish(*refs):
        final_kernel(frame_scale, *refs)

    frames, interface = call(
        finish, m_own, sketch_t, images, out=[((modes, SKETCH, SKETCH), BF16), ((SKETCH, RANK), F32)]
    )
    return (jnp.swapaxes(frames, 0, 1)[None], interface[None])


def solution(mesh):
    split = Mesh(mesh.devices.reshape(4, 8, 2, 2, 4), AXES)
    placed = (P("x", None, MODE, None), P("x", None, MODE, None), P(), P())
    return jax.shard_map(
        body,
        mesh=split,
        in_specs=placed,
        out_specs=(P("x", None, MODE, None), P("x", None, None)),
        check_vma=False,
    )
```

time: 545 us -> 299 us (0.55); the launches traced: 535 us -> 296 us
  waiting for transfers between devices: 101 us -> 11.4 us
  other arithmetic: 84.2 us -> 0.35 us
  starting transfers between devices: 59.1 us -> 11.7 us
  Pallas kernels: 0 us -> 45.6 us
  local copies, waits for them, and re-layouts: 40.1 us -> 7.81 us
  blocking collectives: 234 us -> 218 us
  matrix products: 14.7 us -> 0 us
    all_to_all x8 -> x2, waiting for transfers between devices: 85.4 us -> 11.4 us  [everywhere(): lax.all_to_all(copies, axes, 0, 0, axis_index_groups=groups, tiled=True)]
    another operation x20 -> x0, other arithmetic: 72.6 us -> none  [the longest x12 39.3 us: body(): chol_lower = jnp.linalg.cholesky(gram_matrix)]
    pallas_call x0 -> x8, Pallas kernels: none -> 45.6 us  [call(): pl.pallas_call(kernel, out_shape=outs, in_specs=specs, out_specs=[pl.Bloc...]
    all_to_all x8 -> x2, starting transfers between devices: 45.5 us -> 11.7 us  [everywhere(): lax.all_to_all(copies, axes, 0, 0, axis_index_groups=groups, tiled=True)]
    another operation x21 -> x0, local copies, waits for them, and re-layouts: 18 us -> none  [the longest x11 7.97 us: cut_along(): shard.reshape(*shape[:dim], size, shape[dim] // size, *shape[dim + 1:])]
    ppermute x6 -> x0, waiting for transfers between devices: 15.8 us -> none  [from_behind(): return lax.ppermute(shard, axis, pairs)]
    all_to_all x20 -> x16, blocking collectives: 234 us -> 218 us  [the longest x10 159 us: everywhere(): lax.all_to_all(copies, axes, 0, 0, axis_index_groups=groups, tiled=True)]
    ppermute x6 -> x0, starting transfers between devices: 13.5 us -> none  [from_behind(): return lax.ppermute(shard, axis, pairs)]
  transfers between devices with their start and end apart: 14 -> 2, of which waited for: 12 -> 2; matrix products, arithmetic and copies ran while one was open for 4% -> 0% of each run, Pallas kernels for 0% -> 0%
where the time goes in v1:
time: 299 us; the launch traced here: 296 us
  blocking collectives  218 us (73%)
  Pallas kernels  45.6 us (15%)
  starting transfers between devices  11.7 us (4%)
  waiting for transfers between devices  11.4 us (4%)
  local copies, waits for them, and re-layouts  7.81 us (3%)
    all_to_all x10, blocking collectives, everywhere(): lax.all_to_all(copies, axes, 0, 0, axis_index_groups=groups, tiled=True)  159 us
    all_to_all x6, blocking collectives, shard_sum(): arrived = lax.all_to_all(tiles, NEAR, 0, 0, tiled=True)  59 us
    pallas_call x8, Pallas kernels, call(): pl.pallas_call(kernel, out_shape=outs, in_specs=specs, out_specs=[pl.Bloc...  45.6 us
    all_to_all x2, starting transfers between devices, everywhere(): lax.all_to_all(copies, axes, 0, 0, axis_index_groups=groups, tiled=True)  11.7 us
    all_to_all x2, waiting for transfers between devices, everywhere(): lax.all_to_all(copies, axes, 0, 0, axis_index_groups=groups, tiled=True)  11.4 us
    unnamed x6, local copies, waits for them, and re-layouts  6.33 us
  transfers between devices with their start and end apart: 2, of which 2 were waited for; matrix products, arithmetic and copies ran while one was open for 0% of the time, Pallas kernels for 0%

profile of v1, /device:TPU:7, one launch (start us, length us, event | category | flops | bytes accessed | tf_op | source)
XLA Modules:
  0.0 295.8 jit_solution(18312000539795899011)
XLA Ops:
  6.7 12.4 %all_to_all.90 = bf16[16,8,512]{2,1,0:T(8,128)(2,1)S(1)} all-to-all(bf16[16,8,512]{2,1,0:T(8,128)(2,1)S(1)} %bitcast.62), channel_id=1, replica_groups=mesh['y'=4,'zh'=8,'zl'=2,'c'=2,'x'=4] {'y','zl','c'}, dimensions={0} | all-to-all | bytes 262144 | tf_op jit(solution)/shard_map/all_to_all | solution.py:199
  19.1 26.4 %all_to_all.91 = bf16[16,8,512]{2,1,0:T(8,128)(2,1)S(1)} all-to-all(bf16[16,8,512]{2,1,0:T(8,128)(2,1)S(1)} %broadcast_in_dim.42), channel_id=1, replica_groups={{3,19,35,51,67,83,99,115,2,18,34,50,66,82,98,114},{0,16,32,48,64,80,96,..., dimensions={0} | all-to-all | bytes 262144 | tf_op jit(solution)/shard_map/all_to_all | solution.py:193
  45.6 12.2 %all_to_all.92 = bf16[16,8,512]{2,1,0:T(8,128)(2,1)S(1)} all-to-all(bf16[16,8,512]{2,1,0:T(8,128)(2,1)S(1)} %broadcast_in_dim.43), channel_id=1, replica_groups=mesh['y'=4,'zh'=8,'zl'=2,'c'=2,'x'=4] {'y','zl','c'}, dimensions={0} | all-to-all | bytes 262144 | tf_op jit(solution)/shard_map/all_to_all | solution.py:193
  59.1 9.3 %all_to_all.93 = bf16[16,8,512]{2,1,0:T(8,128)(2,1)S(1)} all-to-all(bf16[16,8,512]{2,1,0:T(8,128)(2,1)S(1)} %bitcast.58), channel_id=1, replica_groups=mesh['y'=4,'zh'=8,'zl'=2,'c'=2,'x'=4] {'y','zl','c'}, dimensions={0} | all-to-all | bytes 262144 | tf_op jit(solution)/shard_map/all_to_all | solution.py:199
  68.4 17.3 %all_to_all.94 = bf16[16,8,512]{2,1,0:T(8,128)(2,1)S(1)} all-to-all(bf16[16,8,512]{2,1,0:T(8,128)(2,1)S(1)} %broadcast_in_dim.44), channel_id=1, replica_groups={{2,18,34,50,66,82,98,114,1,17,33,49,65,81,97,113},{3,19,35,51,67,83,99,..., dimensions={0} | all-to-all | bytes 262144 | tf_op jit(solution)/shard_map/all_to_all | solution.py:193
  85.8 11.1 %all_to_all.95 = bf16[16,8,512]{2,1,0:T(8,128)(2,1)S(1)} all-to-all(bf16[16,8,512]{2,1,0:T(8,128)(2,1)S(1)} %broadcast_in_dim.45), channel_id=1, replica_groups=mesh['y'=4,'zh'=8,'zl'=2,'c'=2,'x'=4] {'y','zl','c'}, dimensions={0} | all-to-all | bytes 262144 | tf_op jit(solution)/shard_map/all_to_all | solution.py:193
  98.1 9.3 %all_to_all.96 = bf16[16,8,512]{2,1,0:T(8,128)(2,1)S(1)} all-to-all(bf16[16,8,512]{2,1,0:T(8,128)(2,1)S(1)} %bitcast.57), channel_id=1, replica_groups=mesh['y'=4,'zh'=8,'zl'=2,'c'=2,'x'=4] {'y','zl','c'}, dimensions={0} | all-to-all | bytes 262144 | tf_op jit(solution)/shard_map/all_to_all | solution.py:199
  107.4 16.9 %all_to_all.97 = bf16[16,8,512]{2,1,0:T(8,128)(2,1)S(1)} all-to-all(bf16[16,8,512]{2,1,0:T(8,128)(2,1)S(1)} %broadcast_in_dim.46), channel_id=1, replica_groups={{1,17,33,49,65,81,97,113,0,16,32,48,64,80,96,112},{3,19,35,51,67,83,99,..., dimensions={0} | all-to-all | bytes 262144 | tf_op jit(solution)/shard_map/all_to_all | solution.py:193
  124.3 13.3 %all_to_all.98 = bf16[16,16,512]{2,1,0:T(8,128)(2,1)S(1)} all-to-all(bf16[16,16,512]{2,1,0:T(8,128)(2,1)S(1)} %broadcast_in_dim.47), channel_id=1, replica_groups=mesh['y'=4,'zh'=8,'zl'=2,'c'=2,'x'=4] {'y','zl','c'}, dimensions={0} | all-to-all | bytes 524288 | tf_op jit(solution)/shard_map/all_to_all | solution.py:193
  137.6 10.7 %shard_map.62 = (bf16[128,512]{1,0:T(8,128)(2,1)S(1)}, bf16[100,400]{1,0:T(8,128)(2,1)S(1)}, f32[100,400]{1,0:T(8,128)S(1)}) custom-call(bf16[128,512]{1,0:T(8,128)(2,1)S(1)} %bitcast.40, bf16[128,512]{1,0:T(8,128)(2,1)S(1)} %get-tuple-element.31.rest_ref, bf16[128,512]{1,0:T(8,128)(2,1)S(1)} %get-tuple-element.30.before_ref, ...), custom_call_target="tpu_custom_call" | custom-call | tf_op jit(solution)/shard_map/pallas_call | solution.py:179
  148.3 9.5 %all_to_all.99 = bf16[16,8,512]{2,1,0:T(8,128)(2,1)S(1)} all-to-all(bf16[16,8,512]{2,1,0:T(8,128)(2,1)S(1)} %bitcast.60), channel_id=1, replica_groups=mesh['y'=4,'zh'=8,'zl'=2,'c'=2,'x'=4] {'y','zl','c'}, dimensions={0} | all-to-all | bytes 262144 | tf_op jit(solution)/shard_map/all_to_all | solution.py:199
  157.9 17.4 %all_to_all.100 = bf16[16,8,512]{2,1,0:T(8,128)(2,1)S(1)} all-to-all(bf16[16,8,512]{2,1,0:T(8,128)(2,1)S(1)} %broadcast_in_dim.48), channel_id=1, replica_groups={{1,17,33,49,65,81,97,113,2,18,34,50,66,82,98,114},{0,16,32,48,64,80,96,..., dimensions={0} | all-to-all | bytes 262144 | tf_op jit(solution)/shard_map/all_to_all | solution.py:193
  175.3 11.8 %all_to_all.101 = bf16[16,8,512]{2,1,0:T(8,128)(2,1)S(1)} all-to-all(bf16[16,8,512]{2,1,0:T(8,128)(2,1)S(1)} %broadcast_in_dim.49), channel_id=1, replica_groups=mesh['y'=4,'zh'=8,'zl'=2,'c'=2,'x'=4] {'y','zl','c'}, dimensions={0} | all-to-all | bytes 262144 | tf_op jit(solution)/shard_map/all_to_all | solution.py:193
  187.0 10.5 %shard_map.63 = (bf16[128,512]{1,0:T(8,128)(2,1)S(1)}, bf16[100,400]{1,0:T(8,128)(2,1)S(1)}) custom-call(bf16[128,512]{1,0:T(8,128)(2,1)S(1)} %bitcast.53, bf16[128,512]{1,0:T(8,128)(2,1)S(1)} %bitcast.46, bf16[4,400,400]{2,1,0:T(8,128)(2,1)S(1)} %bitcast.36, bf16[128,512]{1,0:T(8,128)(2,1)S(1)} %bitcast.41), custom_call_target="tpu_custom_call" | custom-call | tf_op jit(solution)/shard_map/pallas_call | solution.py:179
  197.6 9.3 %all_to_all.102 = bf16[16,8,512]{2,1,0:T(8,128)(2,1)S(1)} all-to-all(bf16[16,8,512]{2,1,0:T(8,128)(2,1)S(1)} %bitcast.63), channel_id=1, replica_groups=mesh['y'=4,'zh'=8,'zl'=2,'c'=2,'x'=4] {'y','zl','c'}, dimensions={0} | all-to-all | bytes 262144 | tf_op jit(solution)/shard_map/all_to_all | solution.py:199
  206.9 16.6 %all_to_all.103 = bf16[16,8,512]{2,1,0:T(8,128)(2,1)S(1)} all-to-all(bf16[16,8,512]{2,1,0:T(8,128)(2,1)S(1)} %broadcast_in_dim.50), channel_id=1, replica_groups={{2,18,34,50,66,82,98,114,3,19,35,51,67,83,99,115},{0,16,32,48,64,80,96,..., dimensions={0} | all-to-all | bytes 262144 | tf_op jit(solution)/shard_map/all_to_all | solution.py:193
  224.1 6.2 %all-to-all-start.14 = ((bf16[16,8,512]{2,1,0:T(8,128)(2,1)}), bf16[16,8,512]{2,1,0:T(8,128)(2,1)S(1)}, u32[]{:S(2)}, u32[]{:S(2)}) async-start(bf16[16,8,512]{2,1,0:T(8,128)(2,1)} %broadcast_in_dim.51), calls=%async_computation.14 | async-start | bytes 262144 | tf_op jit(solution)/shard_map/all_to_all | solution.py:193
  230.3 6.2 %all-to-all-done.14 = bf16[16,8,512]{2,1,0:T(8,128)(2,1)S(1)} async-done(((bf16[16,8,512]{2,1,0:T(8,128)(2,1)}), bf16[16,8,512]{2,1,0:T(8,128)(2,1)S(1)}, u32[]{:S(2)}, u32[]{:S(2)}) %all-to-all-start.14) | async-done | bytes 131104 | tf_op jit(solution)/shard_map/all_to_all | solution.py:193
  236.5 10.5 %shard_map.64 = (bf16[128,512]{1,0:T(8,128)(2,1)S(1)}, bf16[100,400]{1,0:T(8,128)(2,1)S(1)}) custom-call(bf16[128,512]{1,0:T(8,128)(2,1)S(1)} %bitcast.55, bf16[128,512]{1,0:T(8,128)(2,1)S(1)} %bitcast.42, bf16[4,400,400]{2,1,0:T(8,128)(2,1)S(1)} %bitcast.37, bf16[128,512]{1,0:T(8,128)(2,1)S(1)} %pad.4.sketch_ref), custom_call_target="tpu_custom_call" | custom-call | tf_op jit(solution)/shard_map/pallas_call | solution.py:179
  247.0 9.3 %all_to_all.104 = bf16[16,8,512]{2,1,0:T(8,128)(2,1)S(1)} all-to-all(bf16[16,8,512]{2,1,0:T(8,128)(2,1)S(1)} %bitcast.61), channel_id=1, replica_groups=mesh['y'=4,'zh'=8,'zl'=2,'c'=2,'x'=4] {'y','zl','c'}, dimensions={0} | all-to-all | bytes 262144 | tf_op jit(solution)/shard_map/all_to_all | solution.py:199
  256.4 16.1 %all_to_all.105 = bf16[8,8,512]{2,1,0:T(8,128)(2,1)S(1)} all-to-all(bf16[8,8,512]{2,1,0:T(8,128)(2,1)S(1)} %broadcast_in_dim.52), channel_id=1, replica_groups=mesh['y'=4,'zh'=8,'zl'=2,'c'=2,'x'=4] {'zh'}, dimensions={0} | all-to-all | bytes 131072 | tf_op jit(solution)/shard_map/all_to_all | solution.py:193
  273.1 5.5 %all-to-all-start.17 = ((bf16[16,8,512]{2,1,0:T(8,128)(2,1)}), bf16[16,8,512]{2,1,0:T(8,128)(2,1)S(1)}, u32[]{:S(2)}, u32[]{:S(2)}) async-start(bf16[16,8,512]{2,1,0:T(8,128)(2,1)} %broadcast_in_dim.53), calls=%async_computation.17 | async-start | bytes 262144 | tf_op jit(solution)/shard_map/all_to_all | solution.py:193
  279.6 5.2 %all-to-all-done.17 = bf16[16,8,512]{2,1,0:T(8,128)(2,1)S(1)} async-done(((bf16[16,8,512]{2,1,0:T(8,128)(2,1)}), bf16[16,8,512]{2,1,0:T(8,128)(2,1)S(1)}, u32[]{:S(2)}, u32[]{:S(2)}) %all-to-all-start.17) | async-done | bytes 131104 | tf_op jit(solution)/shard_map/all_to_all | solution.py:193
  284.9 9.3 %shard_map.66 = (bf16[4,100,100]{2,1,0:T(8,128)(2,1)S(1)}, f32[100,400]{1,0:T(8,128)S(1)}) custom-call(f32[100,400]{1,0:T(8,128)S(1)} %select_select_fusion.refs_0_, bf16[100,400]{1,0:T(8,128)(2,1)S(1)} %fusion.sketch_ref.refs_1_, f32[4,100,100]{2,1,0:T(8,128)S(1)} %shard_map.65.refs_2_), custom_call_target="tpu_custom_call" | custom-call | tf_op jit(solution)/shard_map/pallas_call | solution.py:179
  (40 shorter events, 12.8 us)
Async XLA Ops:
  224.1 12.4 %all-to-all-start.14 = ((bf16[16,8,512]{2,1,0:T(8,128)(2,1)}), bf16[16,8,512]{2,1,0:T(8,128)(2,1)S(1)}, u32[]{:S(2)}, u32[]{:S(2)}) async-start(bf16[16,8,512]{2,1,0:T(8,128)(2,1)} %broadcast_in_dim.51), calls=%async_computation.14 | async-start | bytes 262144 | tf_op jit(solution)/shard_map/all_to_all | solution.py:193
  273.1 11.7 %all-to-all-start.17 = ((bf16[16,8,512]{2,1,0:T(8,128)(2,1)}), bf16[16,8,512]{2,1,0:T(8,128)(2,1)S(1)}, u32[]{:S(2)}, u32[]{:S(2)}) async-start(bf16[16,8,512]{2,1,0:T(8,128)(2,1)} %broadcast_in_dim.53), calls=%async_computation.17 | async-start | bytes 262144 | tf_op jit(solution)/shard_map/all_to_all | solution.py:193

commit v2 on v1

--- a/solution.py
+++ b/solution.py
@@ -33,16 +33,41 @@
     tiles = [padded[8 * t : 8 * t + 8] for t in range(count)]
     lane = lax.broadcasted_iota(jnp.int32, (8, 128), 1)
     sub = lax.broadcasted_iota(jnp.int32, (8, 128), 0)
-    for j in range(size):
-        own, line = divmod(j, 8)
-        pivot = tiles[own][line : line + 1]
-        scale = 1.0 / pivot[:, j : j + 1]
-        unit = jnp.where(lane[:1] == j, 1.0, pivot)
-        for t in range(own, count):
-            tile = tiles[t]
-            factor = tile[:, j : j + 1] * scale
-            new = jnp.where(lane == j, 0.0, tile) - factor * unit
-            tiles[t] = jnp.where(sub > line, new, tile) if t == own else new
+
+    def column(tile, j):
+        return jnp.broadcast_to(tile[:, j : j + 1], (8, 128))
+
+    def line(tile, s):
+        return jnp.broadcast_to(tile[s : s + 1], (8, 128))
+
+    for own in range(count):
+        base = 8 * own
+        width = min(8, size - base)
+        step = lane - base
+        columns = {t: [column(tiles[t], base + c) for c in range(width)] for t in range(own, count)}
+        head = columns[own]
+        scales, leads = [], []
+        tile = tiles[own]
+        for s in range(width):
+            scales.append(1.0 / line(head[s], s))
+            leads.append([line(head[c], s) if c > s else None for c in range(width)])
+            factor = jnp.where(sub > s, head[s] * scales[s], 0.0)
+            pivot = jnp.where(step == s, 1.0, line(tile, s))
+            tile = jnp.where((step == s) & (sub > s), 0.0, tile) - factor * pivot
+            for c in range(s + 1, width):
+                head[c] = head[c] - factor * leads[s][c]
+        tiles[own] = tile
+        reduced = jnp.where((step > sub) & (step < 8), 0.0, jnp.where(step == sub, 1.0, tile))
+        pivots = [line(reduced, s) for s in range(width)]
+        for t in range(own + 1, count):
+            col = columns[t]
+            new = jnp.where((step >= 0) & (step < 8), 0.0, tiles[t])
+            for s in range(width):
+                factor = col[s] * scales[s]
+                new = new - factor * pivots[s]
+                for c in range(s + 1, width):
+                    col[c] = col[c] - factor * leads[s][c]
+            tiles[t] = new
     done = []
     for t in range(count):
         row = sub + 8 * t
@@ -56,10 +81,10 @@
     return 0.5 * (dot(m_value, sketch_t, 1, 1) + dot(sketch_t, m_value, 1, 1))
 
 
-def sketch_term(core_ref, sketch_core_ref, sketch_t):
+def sketch_term(core_ref, sketch_core_ref, sketch, dim):
     total = None
     for i in range(core_ref.shape[0]):
-        partial = dot(core_ref[i], sketch_t, 1, 1).astype(BF16)
+        partial = dot(core_ref[i], sketch, 1, dim).astype(BF16)
         term = dot(sketch_core_ref[i], partial, 1, 1)
         total = term if total is None else total + term
     return total
@@ -72,14 +97,15 @@
     @pl.when(x_ref[0] != 0)
     def _():
         out_ref[:SKETCH, :RANK] = sketch_term(
-            core_ref, sketch_core_ref, right_ref[...]
+            core_ref, sketch_core_ref, right_ref[...], 0
         ).astype(BF16)
 
     @pl.when(x_ref[0] == 0)
     def _():
         square = None
+        left_t = left_ref[...].astype(BF16)
         for i in range(core_ref.shape[0]):
-            built = dot(left_ref[...], core_ref[i], 1, 0).astype(BF16)
+            built = dot(left_t, core_ref[i], 0, 0).astype(BF16)
             term = dot(built, built, 0, 0)
             square = term if square is None else square + term
         square = square.astype(BF16)
@@ -94,7 +120,7 @@
 def sketch_kernel(core_ref, sketch_core_ref, sketch_ref, out_ref):
     out_ref[...] = jnp.zeros((ROWS, LANES), BF16)
     out_ref[:SKETCH, :RANK] = sketch_term(
-        core_ref, sketch_core_ref, sketch_ref[:SKETCH, :RANK]
+        core_ref, sketch_core_ref, sketch_ref[:SKETCH, :RANK], 1
     ).astype(BF16)
 
 
@@ -153,25 +179,82 @@
     out_ref[:SKETCH, :RANK] = gram_term(core_ref, carry, sketch_ref[:SKETCH, :RANK]).astype(BF16)
 
 
-def images_kernel(carry_ref, core_ref, sketch_ref, out_ref):
-    for i in range(core_ref.shape[0]):
-        built = dot(carry_ref[...], core_ref[i], 1, 0).astype(BF16)
-        out_ref[i] = dot(built, sketch_ref[...], 1, 1)
-
-
-def final_kernel(scale, m_ref, sketch_ref, images_ref, frames_ref, interface_ref):
-    m_value = m_ref[...]
-    high = m_value.astype(BF16)
-    low = (m_value - high.astype(F32)).astype(BF16)
-    sketch_t = sketch_ref[...]
-    inverse = inverse_factor(symmetric_gram(high, sketch_t) + symmetric_gram(low, sketch_t))
-    interface_ref[...] = dot(inverse, m_value, 1, 0, lax.Precision.HIGHEST)
+def last_project_kernel(
+    x_ref, m_ref, before_ref, core_ref, right_ref, left_ref, carry_1_ref, carry_2_ref,
+    third_ref, second_ref, first_ref, out_ref, images_ref,
+):
+    out_ref[...] = jnp.zeros((ROWS, LANES), BF16)
+
+    @pl.when(x_ref[0] == 3)
+    def _():
+        m_value = m_ref[:SKETCH, :RANK]
+        inverse = inverse_factor(symmetric_gram(m_value, before_ref[:SKETCH, :RANK]))
+        carry = dot(inverse, m_value.astype(F32), 1, 0, lax.Precision.HIGHEST).astype(BF16)
+        total = None
+        for i in range(core_ref.shape[0]):
+            built = dot(carry, core_ref[i], 1, 0).astype(BF16)
+            images = dot(built, right_ref[...], 1, 0)
+            images_ref[i] = images
+            term = dot(images.astype(BF16), built, 0, 0)
+            total = term if total is None else total + term
+        out_ref[:SKETCH, :RANK] = total.astype(BF16)
+
+    def images_of(carry, dim, sketch_t):
+        for i in range(core_ref.shape[0]):
+            built = dot(carry, core_ref[i], dim, 0).astype(BF16)
+            images_ref[i] = dot(built, sketch_t, 1, 1)
+
+    @pl.when(x_ref[0] == 2)
+    def _():
+        images_of(carry_2_ref[...], 1, first_ref[:SKETCH, :RANK])
+
+    @pl.when(x_ref[0] == 1)
+    def _():
+        images_of(carry_1_ref[...], 1, second_ref[:SKETCH, :RANK])
+
+    @pl.when(x_ref[0] == 0)
+    def _():
+        images_of(left_ref[...].astype(BF16), 0, third_ref[:SKETCH, :RANK])
+
+
+def final_kernel(
+    scale, x_ref, m_0_ref, m_1_ref, m_2_ref, m_3_ref, third_ref, second_ref, first_ref, right_ref,
+    images_ref, frames_ref, interface_ref, m_ref, gram_ref,
+):
+    def split_gram(m_value, sketch_t):
+        high = m_value.astype(BF16)
+        low = (m_value - high.astype(F32)).astype(BF16)
+        return symmetric_gram(high, sketch_t) + symmetric_gram(low, sketch_t)
+
+    @pl.when(x_ref[0] == 0)
+    def _():
+        m_ref[...] = m_0_ref[...]
+        gram_ref[...] = split_gram(m_0_ref[...], third_ref[:SKETCH, :RANK])
+
+    @pl.when(x_ref[0] == 1)
+    def _():
+        m_ref[...] = m_1_ref[:SKETCH, :RANK].astype(F32)
+        gram_ref[...] = symmetric_gram(m_1_ref[:SKETCH, :RANK], second_ref[:SKETCH, :RANK])
+
+    @pl.when(x_ref[0] == 2)
+    def _():
+        m_ref[...] = m_2_ref[:SKETCH, :RANK].astype(F32)
+        gram_ref[...] = symmetric_gram(m_2_ref[:SKETCH, :RANK], first_ref[:SKETCH, :RANK])
+
+    @pl.when(x_ref[0] == 3)
+    def _():
+        m_value = m_3_ref[:SKETCH, :RANK]
+        m_ref[...] = m_value.astype(F32)
+        gram_ref[...] = 0.5 * (dot(m_value, right_ref[...], 1, 0) + dot(right_ref[...], m_value, 0, 1))
+
+    inverse = inverse_factor(gram_ref[...])
+    interface_ref[...] = dot(inverse, m_ref[...], 1, 0, lax.Precision.HIGHEST)
     for i in range(images_ref.shape[0]):
         orth = dot(images_ref[i], inverse, 1, 1, lax.Precision.HIGHEST)
         frames_ref[i] = (orth * scale).astype(BF16)
 
 
-def call(kernel, *operands, out, scalar=False):
+def call(kernel, *operands, out, scalar=False, scratch=()):
     specs = [pl.BlockSpec(memory_space=pltpu.VMEM) for _ in operands]
     if scalar:
         specs[0] = pl.BlockSpec(memory_space=pltpu.SMEM)
@@ -181,6 +264,7 @@
         out_shape=outs,
         in_specs=specs,
         out_specs=[pl.BlockSpec(memory_space=pltpu.VMEM) for _ in outs],
+        scratch_shapes=[pltpu.VMEM(shape, F32) for shape in scratch],
         compiler_params=PARAMS,
     )(*operands)
 
@@ -222,14 +306,13 @@
     sketch_core = jnp.swapaxes(sketch_cores[0], 0, 1)
     modes = core.shape[0]
     frame_scale = math.sqrt(SKETCH * modes * lax.axis_size(MODE))
-    right_t = right_sketch.T
-    left_low = left_interface.astype(BF16)
+    left_t = left_interface.T
 
     def full(shard):
         return whole(shard).reshape(ROWS, LANES)
 
     term, rest = call(
-        first_kernel, plane_ref, core, sketch_core, right_t, left_low, out=[PAYLOAD, PAYLOAD], scalar=True
+        first_kernel, plane_ref, core, sketch_core, right_sketch, left_t, out=[PAYLOAD, PAYLOAD], scalar=True
     )
     first = full(added(paired(term, ((3, 2), (0, 1)), far)[0]))
     (term,) = call(sketch_kernel, core, sketch_core, first, out=[PAYLOAD])
@@ -247,28 +330,19 @@
     m_1 = full(added(paired(term, ((1, 2), (0, 3)), far)[0]))
     term, carry_2 = call(project_kernel, m_1, second, core, first, out=[PAYLOAD, carry_kind])
     m_2 = full(added(paired(term, ((2, 3), (0, 1)), far)[0]))
-    right_wide = jnp.pad(right_t, ((0, ROWS - SKETCH), (0, LANES - RANK)))
-    term, carry_3 = call(project_kernel, m_2, first, core, right_wide, out=[PAYLOAD, carry_kind])
+    term, images = call(
+        last_project_kernel, plane_ref, m_2, first, core, right_sketch, left_t, carry_1, carry_2,
+        third, second, first, out=[PAYLOAD, ((modes, SKETCH, SKETCH), F32)], scalar=True,
+    )
     m_3 = full(added(everywhere(shard_sum(term), "zh", None, far)))
-
-    def cut(value):
-        return value[:SKETCH, :RANK]
-
-    def own(zero, one, two, three):
-        low = jnp.where(plane == 0, zero, one)
-        high = jnp.where(plane == 2, two, three)
-        return jnp.where(plane < 2, low, high)
-
-    sketch_t = own(cut(third), cut(second), cut(first), right_t)
-    carry = own(left_low, carry_1, carry_2, carry_3)
-    (images,) = call(images_kernel, carry, core, sketch_t, out=[((modes, SKETCH, SKETCH), F32)])
-    m_own = own(m_0, cut(m_1).astype(F32), cut(m_2).astype(F32), cut(m_3).astype(F32))
 
     def finish(*refs):
         final_kernel(frame_scale, *refs)
 
     frames, interface = call(
-        finish, m_own, sketch_t, images, out=[((modes, SKETCH, SKETCH), BF16), ((SKETCH, RANK), F32)]
+        finish, plane_ref, m_0, m_1, m_2, m_3, third, second, first, right_sketch, images,
+        out=[((modes, SKETCH, SKETCH), BF16), ((SKETCH, RANK), F32)], scalar=True,
+        scratch=((SKETCH, RANK), (SKETCH, SKETCH)),
     )
     return (jnp.swapaxes(frames, 0, 1)[None], interface[None])
 

time: 299 us -> 272 us (0.910)
  blocking collectives: 218 us -> 241 us
  Pallas kernels: 45.6 us -> 24.6 us
  starting transfers between devices: 11.7 us -> 0 us
  waiting for transfers between devices: 11.4 us -> 0 us
  local copies, waits for them, and re-layouts: 7.81 us -> 4.45 us
    all_to_all x10 -> x12, blocking collectives: 159 us -> 182 us  [everywhere(): lax.all_to_all(copies, axes, 0, 0, axis_index_groups=groups, tiled=True)]
    pallas_call x8 -> x7, Pallas kernels: 45.6 us -> 24.6 us  [call(): pl.pallas_call(kernel, out_shape=outs, in_specs=specs, out_specs=[pl.Bloc...]
    all_to_all x2 -> x0, starting transfers between devices: 11.7 us -> none  [everywhere(): lax.all_to_all(copies, axes, 0, 0, axis_index_groups=groups, tiled=True)]
    all_to_all x2 -> x0, waiting for transfers between devices: 11.4 us -> none  [everywhere(): lax.all_to_all(copies, axes, 0, 0, axis_index_groups=groups, tiled=True)]
    unnamed x6 -> x8, local copies, waits for them, and re-layouts: 6.33 us -> 4.29 us
  transfers between devices with their start and end apart: 2 -> 0, of which waited for: 2 -> 0; matrix products, arithmetic and copies ran while one was open for 0% -> 0% of each run, Pallas kernels for 0% -> 0%
where the time goes in v2:
time: 272 us; the launch traced here: 271 us
  blocking collectives  241 us (89%)
  Pallas kernels  24.6 us (9%)
  local copies, waits for them, and re-layouts  4.45 us (2%)
    all_to_all x12, blocking collectives, everywhere(): lax.all_to_all(copies, axes, 0, 0, axis_index_groups=groups, tiled=True)  182 us
    all_to_all x6, blocking collectives, shard_sum(): arrived = lax.all_to_all(tiles, NEAR, 0, 0, tiled=True)  59 us
    pallas_call x7, Pallas kernels, call(): pl.pallas_call(kernel, out_shape=outs, in_specs=specs, out_specs=[pl.Bloc...  24.6 us

profile of v2, /device:TPU:7, one launch (start us, length us, event | category | flops | bytes accessed | tf_op | source)
XLA Modules:
  0.0 270.8 jit_solution(7787316066443197110)
XLA Ops:
  1.6 1.8 copy.16
  3.4 1.3 shard_map.59
  4.7 12.4 %all_to_all.90 = bf16[16,8,512]{2,1,0:T(8,128)(2,1)S(1)} all-to-all(bf16[16,8,512]{2,1,0:T(8,128)(2,1)S(1)} %bitcast.63), channel_id=1, replica_groups=mesh['y'=4,'zh'=8,'zl'=2,'c'=2,'x'=4] {'y','zl','c'}, dimensions={0} | all-to-all | bytes 262144 | tf_op jit(solution)/shard_map/all_to_all | solution.py:283
  17.1 26.4 %all_to_all.91 = bf16[16,8,512]{2,1,0:T(8,128)(2,1)S(1)} all-to-all(bf16[16,8,512]{2,1,0:T(8,128)(2,1)S(1)} %broadcast_in_dim.42), channel_id=1, replica_groups={{3,19,35,51,67,83,99,115,2,18,34,50,66,82,98,114},{0,16,32,48,64,80,96,..., dimensions={0} | all-to-all | bytes 262144 | tf_op jit(solution)/shard_map/all_to_all | solution.py:277
  43.6 12.2 %all_to_all.92 = bf16[16,8,512]{2,1,0:T(8,128)(2,1)S(1)} all-to-all(bf16[16,8,512]{2,1,0:T(8,128)(2,1)S(1)} %broadcast_in_dim.43), channel_id=1, replica_groups=mesh['y'=4,'zh'=8,'zl'=2,'c'=2,'x'=4] {'y','zl','c'}, dimensions={0} | all-to-all | bytes 262144 | tf_op jit(solution)/shard_map/all_to_all | solution.py:277
  57.1 9.3 %all_to_all.93 = bf16[16,8,512]{2,1,0:T(8,128)(2,1)S(1)} all-to-all(bf16[16,8,512]{2,1,0:T(8,128)(2,1)S(1)} %bitcast.59), channel_id=1, replica_groups=mesh['y'=4,'zh'=8,'zl'=2,'c'=2,'x'=4] {'y','zl','c'}, dimensions={0} | all-to-all | bytes 262144 | tf_op jit(solution)/shard_map/all_to_all | solution.py:283
  66.4 17.4 %all_to_all.94 = bf16[16,8,512]{2,1,0:T(8,128)(2,1)S(1)} all-to-all(bf16[16,8,512]{2,1,0:T(8,128)(2,1)S(1)} %broadcast_in_dim.44), channel_id=1, replica_groups={{2,18,34,50,66,82,98,114,1,17,33,49,65,81,97,113},{3,19,35,51,67,83,99,..., dimensions={0} | all-to-all | bytes 262144 | tf_op jit(solution)/shard_map/all_to_all | solution.py:277
  83.8 11.1 %all_to_all.95 = bf16[16,8,512]{2,1,0:T(8,128)(2,1)S(1)} all-to-all(bf16[16,8,512]{2,1,0:T(8,128)(2,1)S(1)} %broadcast_in_dim.45), channel_id=1, replica_groups=mesh['y'=4,'zh'=8,'zl'=2,'c'=2,'x'=4] {'y','zl','c'}, dimensions={0} | all-to-all | bytes 262144 | tf_op jit(solution)/shard_map/all_to_all | solution.py:277
  96.1 9.3 %all_to_all.96 = bf16[16,8,512]{2,1,0:T(8,128)(2,1)S(1)} all-to-all(bf16[16,8,512]{2,1,0:T(8,128)(2,1)S(1)} %bitcast.58), channel_id=1, replica_groups=mesh['y'=4,'zh'=8,'zl'=2,'c'=2,'x'=4] {'y','zl','c'}, dimensions={0} | all-to-all | bytes 262144 | tf_op jit(solution)/shard_map/all_to_all | solution.py:283
  105.4 16.9 %all_to_all.97 = bf16[16,8,512]{2,1,0:T(8,128)(2,1)S(1)} all-to-all(bf16[16,8,512]{2,1,0:T(8,128)(2,1)S(1)} %broadcast_in_dim.46), channel_id=1, replica_groups={{1,17,33,49,65,81,97,113,0,16,32,48,64,80,96,112},{3,19,35,51,67,83,99,..., dimensions={0} | all-to-all | bytes 262144 | tf_op jit(solution)/shard_map/all_to_all | solution.py:277
  122.3 13.3 %all_to_all.98 = bf16[16,16,512]{2,1,0:T(8,128)(2,1)S(1)} all-to-all(bf16[16,16,512]{2,1,0:T(8,128)(2,1)S(1)} %broadcast_in_dim.47), channel_id=1, replica_groups=mesh['y'=4,'zh'=8,'zl'=2,'c'=2,'x'=4] {'y','zl','c'}, dimensions={0} | all-to-all | bytes 524288 | tf_op jit(solution)/shard_map/all_to_all | solution.py:277
  135.6 5.6 %shard_map.62 = (bf16[128,512]{1,0:T(8,128)(2,1)S(1)}, bf16[100,400]{1,0:T(8,128)(2,1)S(1)}, f32[100,400]{1,0:T(8,128)S(1)}) custom-call(bf16[128,512]{1,0:T(8,128)(2,1)S(1)} %bitcast.38, bf16[128,512]{1,0:T(8,128)(2,1)S(1)} %get-tuple-element.31.rest_ref, bf16[128,512]{1,0:T(8,128)(2,1)S(1)} %get-tuple-element.30.before_ref.third_ref.refs_5_, ...), custom_call_target="tpu_custom_call" | custom-call | tf_op jit(solution)/shard_map/pallas_call | solution.py:262
  141.2 9.5 %all_to_all.99 = bf16[16,8,512]{2,1,0:T(8,128)(2,1)S(1)} all-to-all(bf16[16,8,512]{2,1,0:T(8,128)(2,1)S(1)} %bitcast.62), channel_id=1, replica_groups=mesh['y'=4,'zh'=8,'zl'=2,'c'=2,'x'=4] {'y','zl','c'}, dimensions={0} | all-to-all | bytes 262144 | tf_op jit(solution)/shard_map/all_to_all | solution.py:283
  150.8 17.4 %all_to_all.100 = bf16[16,8,512]{2,1,0:T(8,128)(2,1)S(1)} all-to-all(bf16[16,8,512]{2,1,0:T(8,128)(2,1)S(1)} %broadcast_in_dim.48), channel_id=1, replica_groups={{1,17,33,49,65,81,97,113,2,18,34,50,66,82,98,114},{0,16,32,48,64,80,96,..., dimensions={0} | all-to-all | bytes 262144 | tf_op jit(solution)/shard_map/all_to_all | solution.py:277
  168.2 11.8 %all_to_all.101 = bf16[16,8,512]{2,1,0:T(8,128)(2,1)S(1)} all-to-all(bf16[16,8,512]{2,1,0:T(8,128)(2,1)S(1)} %broadcast_in_dim.49), channel_id=1, replica_groups=mesh['y'=4,'zh'=8,'zl'=2,'c'=2,'x'=4] {'y','zl','c'}, dimensions={0} | all-to-all | bytes 262144 | tf_op jit(solution)/shard_map/all_to_all | solution.py:277
  180.0 5.5 %shard_map.63 = (bf16[128,512]{1,0:T(8,128)(2,1)S(1)}, bf16[100,400]{1,0:T(8,128)(2,1)S(1)}) custom-call(bf16[128,512]{1,0:T(8,128)(2,1)S(1)} %bitcast.51, bf16[128,512]{1,0:T(8,128)(2,1)S(1)} %bitcast.45, bf16[4,400,400]{2,1,0:T(8,128)(2,1)S(1)} %bitcast.35, bf16[128,512]{1,0:T(8,128)(2,1)S(1)} %bitcast.39), custom_call_target="tpu_custom_call" | custom-call | tf_op jit(solution)/shard_map/pallas_call | solution.py:262
  185.4 9.3 %all_to_all.102 = bf16[16,8,512]{2,1,0:T(8,128)(2,1)S(1)} all-to-all(bf16[16,8,512]{2,1,0:T(8,128)(2,1)S(1)} %bitcast.64), channel_id=1, replica_groups=mesh['y'=4,'zh'=8,'zl'=2,'c'=2,'x'=4] {'y','zl','c'}, dimensions={0} | all-to-all | bytes 262144 | tf_op jit(solution)/shard_map/all_to_all | solution.py:283
  194.7 16.6 %all_to_all.103 = bf16[16,8,512]{2,1,0:T(8,128)(2,1)S(1)} all-to-all(bf16[16,8,512]{2,1,0:T(8,128)(2,1)S(1)} %broadcast_in_dim.50), channel_id=1, replica_groups={{2,18,34,50,66,82,98,114,3,19,35,51,67,83,99,115},{0,16,32,48,64,80,96,..., dimensions={0} | all-to-all | bytes 262144 | tf_op jit(solution)/shard_map/all_to_all | solution.py:277
  211.3 11.8 %all_to_all.104 = bf16[16,8,512]{2,1,0:T(8,128)(2,1)S(1)} all-to-all(bf16[16,8,512]{2,1,0:T(8,128)(2,1)S(1)} %broadcast_in_dim.51), channel_id=1, replica_groups=mesh['y'=4,'zh'=8,'zl'=2,'c'=2,'x'=4] {'y','zl','c'}, dimensions={0} | all-to-all | bytes 262144 | tf_op jit(solution)/shard_map/all_to_all | solution.py:277
  223.1 5.4 %shard_map.64 = (bf16[128,512]{1,0:T(8,128)(2,1)S(1)}, f32[4,100,100]{2,1,0:T(8,128)S(1)}) custom-call(s32[1]{0:T(128)} %bitcast.x_ref.refs_0_, bf16[128,512]{1,0:T(8,128)(2,1)S(1)} %bitcast.53, bf16[128,512]{1,0:T(8,128)(2,1)S(1)} %bitcast.40, bf16[4,400,400]{2,1,0:T(8,128)(2,1)S(1)} %bitcast.36, bf16[400,100]{1,0:T(8,128)(2,1)S(1)} %copy-done, ...), custom_call_target="tpu_custom_call" | custom-call | tf_op jit(solution)/shard_map/pallas_call | solution.py:262
  228.5 9.3 %all_to_all.105 = bf16[16,8,512]{2,1,0:T(8,128)(2,1)S(1)} all-to-all(bf16[16,8,512]{2,1,0:T(8,128)(2,1)S(1)} %bitcast.61), channel_id=1, replica_groups=mesh['y'=4,'zh'=8,'zl'=2,'c'=2,'x'=4] {'y','zl','c'}, dimensions={0} | all-to-all | bytes 262144 | tf_op jit(solution)/shard_map/all_to_all | solution.py:283
  237.8 15.8 %all_to_all.106 = bf16[8,8,512]{2,1,0:T(8,128)(2,1)S(1)} all-to-all(bf16[8,8,512]{2,1,0:T(8,128)(2,1)S(1)} %broadcast_in_dim.52), channel_id=1, replica_groups=mesh['y'=4,'zh'=8,'zl'=2,'c'=2,'x'=4] {'zh'}, dimensions={0} | all-to-all | bytes 131072 | tf_op jit(solution)/shard_map/all_to_all | solution.py:277
  253.7 11.1 %all_to_all.107 = bf16[16,8,512]{2,1,0:T(8,128)(2,1)S(1)} all-to-all(bf16[16,8,512]{2,1,0:T(8,128)(2,1)S(1)} %broadcast_in_dim.53), channel_id=1, replica_groups=mesh['y'=4,'zh'=8,'zl'=2,'c'=2,'x'=4] {'y','zl','c'}, dimensions={0} | all-to-all | bytes 262144 | tf_op jit(solution)/shard_map/all_to_all | solution.py:277
  264.8 4.4 %shard_map.65 = (bf16[4,100,100]{2,1,0:T(8,128)(2,1)S(1)}, f32[100,400]{1,0:T(8,128)S(1)}) custom-call(s32[1]{0:T(128)} %bitcast.x_ref.refs_0_, f32[100,400]{1,0:T(8,128)S(1)} %get-tuple-element.15.refs_1_, bf16[128,512]{1,0:T(8,128)(2,1)S(1)} %bitcast.52, bf16[128,512]{1,0:T(8,128)(2,1)S(1)} %bitcast.54, bf16[128,512]{1,0:T(8,128)(2,1)S(1)} %bitcast.57, ...), custom_call_target="tpu_custom_call" | custom-call | tf_op jit(solution)/shard_map/pallas_call | solution.py:262
  (35 shorter events, 5.4 us)
Async XLA Ops:
  1.5 1.8 copy-start
  1.6 1.8 copy-start.1

commit v3 on v2

--- a/solution.py
+++ b/solution.py
@@ -8,9 +8,8 @@
 from jax.sharding import Mesh
 from jax.sharding import PartitionSpec as P
 
-AXES = ("y", "zh", "zl", "c", "x")
-MODE = ("y", "zh", "zl", "c")
-NEAR = ("y", "zl", "c")
+AXES = ("y", "z", "c", "x")
+MODE = ("y", "z", "c")
 RANK = 400
 SKETCH = 100
 ROWS = 128
@@ -272,34 +271,30 @@
 PAYLOAD = ((ROWS, LANES), BF16)
 
 
-def everywhere(shard, axes, groups, count):
+def everywhere(shard, axes, count, groups=None):
     copies = jnp.broadcast_to(shard, (count, *shard.shape))
     return lax.all_to_all(copies, axes, 0, 0, axis_index_groups=groups, tiled=True)
 
 
-def shard_sum(value):
-    near = 16
-    tiles = value.reshape(near, ROWS // near, LANES)
-    arrived = lax.all_to_all(tiles, NEAR, 0, 0, tiled=True)
-    return arrived.astype(F32).sum(axis=0).astype(BF16)
-
-
 def added(pieces):
     return pieces.astype(F32).sum(axis=0).astype(BF16)
 
 
-def paired(value, pairs, far):
-    groups = [[x * far + z for x in pair for z in range(far)] for pair in pairs]
-    pieces = everywhere(shard_sum(value), ("x", "zh"), groups, 2 * far)
-    return pieces[:far], pieces[far:]
-
-
-def whole(shard):
-    return everywhere(shard, NEAR, None, 16)
+def plane_sum(value, near, far):
+    tiles = value.reshape(near, ROWS // near, LANES)
+    shard = added(lax.all_to_all(tiles, ("y", "c"), 0, 0, tiled=True))
+    return added(everywhere(shard, "z", far))
+
+
+def whole_pair(shard, pairs, near):
+    groups = [[x * near + d for x in pair for d in range(near)] for pair in pairs]
+    rows = everywhere(shard, ("x", "y", "c"), 2 * near, groups)
+    return rows[:near].reshape(ROWS, LANES), rows[near:].reshape(ROWS, LANES)
 
 
 def body(train_cores, sketch_cores, left_interface, right_sketch):
-    far = lax.axis_size("zh")
+    near = lax.axis_size("y") * lax.axis_size("c")
+    far = lax.axis_size("z")
     plane = lax.axis_index("x")
     plane_ref = plane.astype(jnp.int32).reshape(1)
     core = jnp.swapaxes(train_cores[0], 0, 1)
@@ -308,33 +303,30 @@
     frame_scale = math.sqrt(SKETCH * modes * lax.axis_size(MODE))
     left_t = left_interface.T
 
-    def full(shard):
-        return whole(shard).reshape(ROWS, LANES)
+    def first_of(value, pairs):
+        return whole_pair(plane_sum(value, near, far), pairs, near)[0]
 
     term, rest = call(
         first_kernel, plane_ref, core, sketch_core, right_sketch, left_t, out=[PAYLOAD, PAYLOAD], scalar=True
     )
-    first = full(added(paired(term, ((3, 2), (0, 1)), far)[0]))
+    first = first_of(term, ((3, 2), (0, 1)))
     (term,) = call(sketch_kernel, core, sketch_core, first, out=[PAYLOAD])
-    second = full(added(paired(term, ((2, 1), (3, 0)), far)[0]))
+    second = first_of(term, ((2, 1), (3, 0)))
     (term,) = call(last_sketch_kernel, plane_ref, core, sketch_core, second, rest, out=[PAYLOAD], scalar=True)
-    both = paired(term, ((1, 0), (3, 2)), far)
-    arrived = whole(jnp.concatenate([added(both[0]), added(both[1])], axis=0))
-    third = arrived[:, :8].reshape(ROWS, LANES)
-    rest = arrived[:, 8:].reshape(ROWS, LANES)
+    third, rest = whole_pair(plane_sum(term, near, far), ((1, 0), (3, 2)), near)
 
     carry_kind = ((SKETCH, RANK), BF16)
     term, carry_1, m_0 = call(
         first_project_kernel, first, rest, third, core, second, out=[PAYLOAD, carry_kind, ((SKETCH, RANK), F32)]
     )
-    m_1 = full(added(paired(term, ((1, 2), (0, 3)), far)[0]))
+    m_1 = first_of(term, ((1, 2), (0, 3)))
     term, carry_2 = call(project_kernel, m_1, second, core, first, out=[PAYLOAD, carry_kind])
-    m_2 = full(added(paired(term, ((2, 3), (0, 1)), far)[0]))
+    m_2 = first_of(term, ((2, 3), (0, 1)))
     term, images = call(
         last_project_kernel, plane_ref, m_2, first, core, right_sketch, left_t, carry_1, carry_2,
         third, second, first, out=[PAYLOAD, ((modes, SKETCH, SKETCH), F32)], scalar=True,
     )
-    m_3 = full(added(everywhere(shard_sum(term), "zh", None, far)))
+    m_3 = everywhere(plane_sum(term, near, far), ("y", "c"), near).reshape(ROWS, LANES)
 
     def finish(*refs):
         final_kernel(frame_scale, *refs)
@@ -348,7 +340,7 @@
 
 
 def solution(mesh):
-    split = Mesh(mesh.devices.reshape(4, 8, 2, 2, 4), AXES)
+    split = Mesh(mesh.devices.reshape(4, 16, 2, 4), AXES)
     placed = (P("x", None, MODE, None), P("x", None, MODE, None), P(), P())
     return jax.shard_map(
         body,

time: 272 us -> 300 us (1.10)
  blocking collectives: 241 us -> 269 us
    all_to_all x12, blocking collectives: 182 us -> 217 us  [everywhere(): lax.all_to_all(copies, axes, 0, 0, axis_index_groups=groups, tiled=True)]
    all_to_all x6, blocking collectives: 59 us -> 52.2 us  [plane_sum(): shard = added(lax.all_to_all(tiles, ('y', 'c'), 0, 0, tiled=True))]
where the time goes in v3:
time: 300 us; the launch traced here: 299 us
  blocking collectives  269 us (90%)
  Pallas kernels  24.7 us (8%)
  local copies, waits for them, and re-layouts  4.57 us (2%)
    all_to_all x12, blocking collectives, everywhere(): lax.all_to_all(copies, axes, 0, 0, axis_index_groups=groups, tiled=True)  217 us
    all_to_all x6, blocking collectives, plane_sum(): shard = added(lax.all_to_all(tiles, ('y', 'c'), 0, 0, tiled=True))  52.2 us
    pallas_call x7, Pallas kernels, call(): pl.pallas_call(kernel, out_shape=outs, in_specs=specs, out_specs=[pl.Bloc...  24.7 us

profile of v3, /device:TPU:7, one launch (start us, length us, event | category | flops | bytes accessed | tf_op | source)
XLA Modules:
  0.0 299.4 jit_solution(7879527193490002139)
XLA Ops:
  1.6 1.8 copy.16
  3.4 1.3 shard_map.59
  4.7 10.2 %all_to_all.90 = bf16[8,16,512]{2,1,0:T(8,128)(2,1)S(1)} all-to-all(bf16[8,16,512]{2,1,0:T(8,128)(2,1)S(1)} %bitcast.65), channel_id=1, replica_groups=mesh['y'=4,'z'=16,'c'=2,'x'=4] {'y','c'}, dimensions={0} | all-to-all | bytes 262144 | tf_op jit(solution)/shard_map/all_to_all | solution.py:285
  14.9 27.8 %all_to_all.91 = bf16[16,16,512]{2,1,0:T(8,128)(2,1)S(1)} all-to-all(bf16[16,16,512]{2,1,0:T(8,128)(2,1)S(1)} %broadcast_in_dim.42), channel_id=1, replica_groups=mesh['y'=4,'z'=16,'c'=2,'x'=4] {'z'}, dimensions={0} | all-to-all | bytes 524288 | tf_op jit(solution)/shard_map/all_to_all | solution.py:276
  42.8 16.2 %all_to_all.92 = bf16[16,16,512]{2,1,0:T(8,128)(2,1)S(1)} all-to-all(bf16[16,16,512]{2,1,0:T(8,128)(2,1)S(1)} %broadcast_in_dim.43), channel_id=1, replica_groups={{3,7,131,135,259,263,387,391,2,6,130,134,258,262,386,390},{0,4,128,132,..., dimensions={0} | all-to-all | bytes 524288 | tf_op jit(solution)/shard_map/all_to_all | solution.py:276
  60.2 8.5 %all_to_all.93 = bf16[8,16,512]{2,1,0:T(8,128)(2,1)S(1)} all-to-all(bf16[8,16,512]{2,1,0:T(8,128)(2,1)S(1)} %bitcast.61), channel_id=1, replica_groups=mesh['y'=4,'z'=16,'c'=2,'x'=4] {'y','c'}, dimensions={0} | all-to-all | bytes 262144 | tf_op jit(solution)/shard_map/all_to_all | solution.py:285
  68.8 18.2 %all_to_all.94 = bf16[16,16,512]{2,1,0:T(8,128)(2,1)S(1)} all-to-all(bf16[16,16,512]{2,1,0:T(8,128)(2,1)S(1)} %broadcast_in_dim.44), channel_id=1, replica_groups=mesh['y'=4,'z'=16,'c'=2,'x'=4] {'z'}, dimensions={0} | all-to-all | bytes 524288 | tf_op jit(solution)/shard_map/all_to_all | solution.py:276
  87.0 17.7 %all_to_all.95 = bf16[16,16,512]{2,1,0:T(8,128)(2,1)S(1)} all-to-all(bf16[16,16,512]{2,1,0:T(8,128)(2,1)S(1)} %broadcast_in_dim.45), channel_id=1, replica_groups={{2,6,130,134,258,262,386,390,1,5,129,133,257,261,385,389},{3,7,131,135,..., dimensions={0} | all-to-all | bytes 524288 | tf_op jit(solution)/shard_map/all_to_all | solution.py:276
  106.0 8.5 %all_to_all.96 = bf16[8,16,512]{2,1,0:T(8,128)(2,1)S(1)} all-to-all(bf16[8,16,512]{2,1,0:T(8,128)(2,1)S(1)} %bitcast.59), channel_id=1, replica_groups=mesh['y'=4,'z'=16,'c'=2,'x'=4] {'y','c'}, dimensions={0} | all-to-all | bytes 262144 | tf_op jit(solution)/shard_map/all_to_all | solution.py:285
  114.6 18.2 %all_to_all.97 = bf16[16,16,512]{2,1,0:T(8,128)(2,1)S(1)} all-to-all(bf16[16,16,512]{2,1,0:T(8,128)(2,1)S(1)} %broadcast_in_dim.46), channel_id=1, replica_groups=mesh['y'=4,'z'=16,'c'=2,'x'=4] {'z'}, dimensions={0} | all-to-all | bytes 524288 | tf_op jit(solution)/shard_map/all_to_all | solution.py:276
  132.8 16.2 %all_to_all.98 = bf16[16,16,512]{2,1,0:T(8,128)(2,1)S(1)} all-to-all(bf16[16,16,512]{2,1,0:T(8,128)(2,1)S(1)} %broadcast_in_dim.47), channel_id=1, replica_groups={{1,5,129,133,257,261,385,389,0,4,128,132,256,260,384,388},{3,7,131,135,..., dimensions={0} | all-to-all | bytes 524288 | tf_op jit(solution)/shard_map/all_to_all | solution.py:276
  149.0 5.6 %shard_map.62 = (bf16[128,512]{1,0:T(8,128)(2,1)S(1)}, bf16[100,400]{1,0:T(8,128)(2,1)S(1)}, f32[100,400]{1,0:T(8,128)S(1)}) custom-call(bf16[128,512]{1,0:T(8,128)(2,1)S(1)} %bitcast.36, bf16[128,512]{1,0:T(8,128)(2,1)S(1)} %bitcast.60, bf16[128,512]{1,0:T(8,128)(2,1)S(1)} %bitcast.46, bf16[4,400,400]{2,1,0:T(8,128)(2,1)S(1)} %bitcast.32, ...), custom_call_target="tpu_custom_call" | custom-call | tf_op jit(solution)/shard_map/pallas_call | solution.py:261
  154.6 8.6 %all_to_all.99 = bf16[8,16,512]{2,1,0:T(8,128)(2,1)S(1)} all-to-all(bf16[8,16,512]{2,1,0:T(8,128)(2,1)S(1)} %bitcast.64), channel_id=1, replica_groups=mesh['y'=4,'z'=16,'c'=2,'x'=4] {'y','c'}, dimensions={0} | all-to-all | bytes 262144 | tf_op jit(solution)/shard_map/all_to_all | solution.py:285
  163.2 18.2 %all_to_all.100 = bf16[16,16,512]{2,1,0:T(8,128)(2,1)S(1)} all-to-all(bf16[16,16,512]{2,1,0:T(8,128)(2,1)S(1)} %broadcast_in_dim.48), channel_id=1, replica_groups=mesh['y'=4,'z'=16,'c'=2,'x'=4] {'z'}, dimensions={0} | all-to-all | bytes 524288 | tf_op jit(solution)/shard_map/all_to_all | solution.py:276
  181.4 17.6 %all_to_all.101 = bf16[16,16,512]{2,1,0:T(8,128)(2,1)S(1)} all-to-all(bf16[16,16,512]{2,1,0:T(8,128)(2,1)S(1)} %broadcast_in_dim.49), channel_id=1, replica_groups={{1,5,129,133,257,261,385,389,2,6,130,134,258,262,386,390},{0,4,128,132,..., dimensions={0} | all-to-all | bytes 524288 | tf_op jit(solution)/shard_map/all_to_all | solution.py:276
  199.0 5.5 %shard_map.63 = (bf16[128,512]{1,0:T(8,128)(2,1)S(1)}, bf16[100,400]{1,0:T(8,128)(2,1)S(1)}) custom-call(bf16[128,512]{1,0:T(8,128)(2,1)S(1)} %bitcast.52, bf16[128,512]{1,0:T(8,128)(2,1)S(1)} %bitcast.43, bf16[4,400,400]{2,1,0:T(8,128)(2,1)S(1)} %bitcast.33, bf16[128,512]{1,0:T(8,128)(2,1)S(1)} %bitcast.37), custom_call_target="tpu_custom_call" | custom-call | tf_op jit(solution)/shard_map/pallas_call | solution.py:261
  204.5 8.2 %all_to_all.102 = bf16[8,16,512]{2,1,0:T(8,128)(2,1)S(1)} all-to-all(bf16[8,16,512]{2,1,0:T(8,128)(2,1)S(1)} %bitcast.66), channel_id=1, replica_groups=mesh['y'=4,'z'=16,'c'=2,'x'=4] {'y','c'}, dimensions={0} | all-to-all | bytes 262144 | tf_op jit(solution)/shard_map/all_to_all | solution.py:285
  212.8 18.2 %all_to_all.103 = bf16[16,16,512]{2,1,0:T(8,128)(2,1)S(1)} all-to-all(bf16[16,16,512]{2,1,0:T(8,128)(2,1)S(1)} %broadcast_in_dim.50), channel_id=1, replica_groups=mesh['y'=4,'z'=16,'c'=2,'x'=4] {'z'}, dimensions={0} | all-to-all | bytes 524288 | tf_op jit(solution)/shard_map/all_to_all | solution.py:276
  231.0 16.4 %all_to_all.104 = bf16[16,16,512]{2,1,0:T(8,128)(2,1)S(1)} all-to-all(bf16[16,16,512]{2,1,0:T(8,128)(2,1)S(1)} %broadcast_in_dim.51), channel_id=1, replica_groups={{2,6,130,134,258,262,386,390,3,7,131,135,259,263,387,391},{0,4,128,132,..., dimensions={0} | all-to-all | bytes 524288 | tf_op jit(solution)/shard_map/all_to_all | solution.py:276
  247.4 5.5 %shard_map.64 = (bf16[128,512]{1,0:T(8,128)(2,1)S(1)}, f32[4,100,100]{2,1,0:T(8,128)S(1)}) custom-call(s32[1]{0:T(128)} %bitcast.x_ref.refs_0_, bf16[128,512]{1,0:T(8,128)(2,1)S(1)} %bitcast.54, bf16[128,512]{1,0:T(8,128)(2,1)S(1)} %bitcast.38, bf16[4,400,400]{2,1,0:T(8,128)(2,1)S(1)} %bitcast.34, bf16[400,100]{1,0:T(8,128)(2,1)S(1)} %copy-done, ...), custom_call_target="tpu_custom_call" | custom-call | tf_op jit(solution)/shard_map/pallas_call | solution.py:261
  252.8 8.2 %all_to_all.105 = bf16[8,16,512]{2,1,0:T(8,128)(2,1)S(1)} all-to-all(bf16[8,16,512]{2,1,0:T(8,128)(2,1)S(1)} %bitcast.63), channel_id=1, replica_groups=mesh['y'=4,'z'=16,'c'=2,'x'=4] {'y','c'}, dimensions={0} | all-to-all | bytes 262144 | tf_op jit(solution)/shard_map/all_to_all | solution.py:285
  261.1 18.2 %all_to_all.106 = bf16[16,16,512]{2,1,0:T(8,128)(2,1)S(1)} all-to-all(bf16[16,16,512]{2,1,0:T(8,128)(2,1)S(1)} %broadcast_in_dim.52), channel_id=1, replica_groups=mesh['y'=4,'z'=16,'c'=2,'x'=4] {'z'}, dimensions={0} | all-to-all | bytes 524288 | tf_op jit(solution)/shard_map/all_to_all | solution.py:276
  279.3 14.1 %all_to_all.107 = bf16[8,16,512]{2,1,0:T(8,128)(2,1)S(1)} all-to-all(bf16[8,16,512]{2,1,0:T(8,128)(2,1)S(1)} %broadcast_in_dim.53), channel_id=1, replica_groups=mesh['y'=4,'z'=16,'c'=2,'x'=4] {'y','c'}, dimensions={0} | all-to-all | bytes 262144 | tf_op jit(solution)/shard_map/all_to_all | solution.py:276
  293.4 4.4 %shard_map.65 = (bf16[4,100,100]{2,1,0:T(8,128)(2,1)S(1)}, f32[100,400]{1,0:T(8,128)S(1)}) custom-call(s32[1]{0:T(128)} %bitcast.x_ref.refs_0_, f32[100,400]{1,0:T(8,128)S(1)} %get-tuple-element.15.refs_1_, bf16[128,512]{1,0:T(8,128)(2,1)S(1)} %bitcast.53, bf16[128,512]{1,0:T(8,128)(2,1)S(1)} %bitcast.55, bf16[128,512]{1,0:T(8,128)(2,1)S(1)} %bitcast.58, ...), custom_call_target="tpu_custom_call" | custom-call | tf_op jit(solution)/shard_map/pallas_call | solution.py:261
  (38 shorter events, 5.7 us)
Async XLA Ops:
  1.5 1.8 copy-start
  1.6 1.8 copy-start.1

commit v4 on v2

--- a/solution.py
+++ b/solution.py
@@ -10,7 +10,9 @@
 
 AXES = ("y", "zh", "zl", "c", "x")
 MODE = ("y", "zh", "zl", "c")
-NEAR = ("y", "zl", "c")
+SIZES = (4, 8, 2, 2, 4)
+NEAR = tuple((y, zl, c) for y in range(4) for zl in range(2) for c in range(2))
+FAR = 8
 RANK = 400
 SKETCH = 100
 ROWS = 128
@@ -272,34 +274,50 @@
 PAYLOAD = ((ROWS, LANES), BF16)
 
 
-def everywhere(shard, axes, groups, count):
-    copies = jnp.broadcast_to(shard, (count, *shard.shape))
-    return lax.all_to_all(copies, axes, 0, 0, axis_index_groups=groups, tiled=True)
+def device(place, zh, x):
+    y, zl, c = place
+    if zh >= FAR // 2:
+        zl, c = 1 - zl, 1 - c
+    index = 0
+    for at, size in zip((y, zh, zl, c, x), SIZES):
+        index = index * size + at
+    return index
+
+
+def near_groups(planes):
+    return [[device(place, zh, x) for place in NEAR] for x in planes for zh in range(FAR)]
+
+
+def far_groups(planes):
+    return [[device(place, zh, x) for x in planes for zh in range(FAR)] for place in NEAR]
+
+
+def everywhere(shard, groups):
+    copies = jnp.broadcast_to(shard, (len(groups[0]), *shard.shape))
+    return lax.all_to_all(copies, AXES, 0, 0, axis_index_groups=groups, tiled=True)
 
 
 def shard_sum(value):
-    near = 16
-    tiles = value.reshape(near, ROWS // near, LANES)
-    arrived = lax.all_to_all(tiles, NEAR, 0, 0, tiled=True)
-    return arrived.astype(F32).sum(axis=0).astype(BF16)
+    tiles = value.reshape(len(NEAR), ROWS // len(NEAR), LANES)
+    return added(lax.all_to_all(tiles, AXES, 0, 0, axis_index_groups=near_groups(range(4)), tiled=True))
 
 
 def added(pieces):
     return pieces.astype(F32).sum(axis=0).astype(BF16)
 
 
-def paired(value, pairs, far):
-    groups = [[x * far + z for x in pair for z in range(far)] for pair in pairs]
-    pieces = everywhere(shard_sum(value), ("x", "zh"), groups, 2 * far)
-    return pieces[:far], pieces[far:]
+def paired(value, pairs):
+    spare = [x for x in range(4) if not any(x in pair for pair in pairs)]
+    groups = [group for pair in pairs for group in far_groups(pair)] + near_groups(spare)
+    pieces = everywhere(shard_sum(value), groups)
+    return pieces[:FAR], pieces[FAR:]
 
 
 def whole(shard):
-    return everywhere(shard, NEAR, None, 16)
+    return everywhere(shard, near_groups(range(4)))
 
 
 def body(train_cores, sketch_cores, left_interface, right_sketch):
-    far = lax.axis_size("zh")
     plane = lax.axis_index("x")
     plane_ref = plane.astype(jnp.int32).reshape(1)
     core = jnp.swapaxes(train_cores[0], 0, 1)
@@ -314,11 +332,11 @@
     term, rest = call(
         first_kernel, plane_ref, core, sketch_core, right_sketch, left_t, out=[PAYLOAD, PAYLOAD], scalar=True
     )
-    first = full(added(paired(term, ((3, 2), (0, 1)), far)[0]))
+    first = full(added(paired(term, ((3, 2), (0, 1)))[0]))
     (term,) = call(sketch_kernel, core, sketch_core, first, out=[PAYLOAD])
-    second = full(added(paired(term, ((2, 1), (3, 0)), far)[0]))
+    second = full(added(paired(term, ((2, 1),))[0]))
     (term,) = call(last_sketch_kernel, plane_ref, core, sketch_core, second, rest, out=[PAYLOAD], scalar=True)
-    both = paired(term, ((1, 0), (3, 2)), far)
+    both = paired(term, ((1, 0),))
     arrived = whole(jnp.concatenate([added(both[0]), added(both[1])], axis=0))
     third = arrived[:, :8].reshape(ROWS, LANES)
     rest = arrived[:, 8:].reshape(ROWS, LANES)
@@ -327,14 +345,15 @@
     term, carry_1, m_0 = call(
         first_project_kernel, first, rest, third, core, second, out=[PAYLOAD, carry_kind, ((SKETCH, RANK), F32)]
     )
-    m_1 = full(added(paired(term, ((1, 2), (0, 3)), far)[0]))
+    m_1 = full(added(paired(term, ((1, 2),))[0]))
     term, carry_2 = call(project_kernel, m_1, second, core, first, out=[PAYLOAD, carry_kind])
-    m_2 = full(added(paired(term, ((2, 3), (0, 1)), far)[0]))
+    m_2 = full(added(paired(term, ((2, 3),))[0]))
     term, images = call(
         last_project_kernel, plane_ref, m_2, first, core, right_sketch, left_t, carry_1, carry_2,
         third, second, first, out=[PAYLOAD, ((modes, SKETCH, SKETCH), F32)], scalar=True,
     )
-    m_3 = full(added(everywhere(shard_sum(term), "zh", None, far)))
+    alone = [group for x in range(4) for group in far_groups((x,))]
+    m_3 = full(added(everywhere(shard_sum(term), alone)))
 
     def finish(*refs):
         final_kernel(frame_scale, *refs)
@@ -348,7 +367,7 @@
 
 
 def solution(mesh):
-    split = Mesh(mesh.devices.reshape(4, 8, 2, 2, 4), AXES)
+    split = Mesh(mesh.devices.reshape(*SIZES), AXES)
     placed = (P("x", None, MODE, None), P("x", None, MODE, None), P(), P())
     return jax.shard_map(
         body,

time: 272 us -> 267 us (0.982)
  blocking collectives: 241 us -> 236 us
    all_to_all x18, blocking collectives: 241 us -> 236 us  [the longest x12 177 us: everywhere(): lax.all_to_all(copies, AXES, 0, 0, axis_index_groups=groups, tiled=True)]
where the time goes in v4:
time: 267 us; the launch traced here: 266 us
  blocking collectives  236 us (88%)
  Pallas kernels  24.6 us (9%)
  local copies, waits for them, and re-layouts  4.45 us (2%)
    all_to_all x12, blocking collectives, everywhere(): lax.all_to_all(copies, AXES, 0, 0, axis_index_groups=groups, tiled=True)  177 us
    all_to_all x6, blocking collectives, shard_sum(): lax.all_to_all(tiles, AXES, 0, 0, axis_index_groups=near_groups(range(4))...  59.1 us
    pallas_call x7, Pallas kernels, call(): pl.pallas_call(kernel, out_shape=outs, in_specs=specs, out_specs=[pl.Bloc...  24.6 us

profile of v4, /device:TPU:7, one launch (start us, length us, event | category | flops | bytes accessed | tf_op | source)
XLA Modules:
  0.0 266.2 jit_solution(13100652172529412585)
XLA Ops:
  1.6 1.8 copy.16
  3.4 1.3 shard_map.59
  4.7 12.4 %all_to_all.90 = bf16[16,8,512]{2,1,0:T(8,128)(2,1)S(1)} all-to-all(bf16[16,8,512]{2,1,0:T(8,128)(2,1)S(1)} %bitcast.63), channel_id=1, replica_groups={{0,4,8,12,128,132,136,140,256,260,264,268,384,388,392,396},{16,20,24,28..., dimensions={0} | all-to-all | bytes 262144 | tf_op jit(solution)/shard_map/all_to_all | solution.py:302
  17.1 26.6 %all_to_all.91 = bf16[16,8,512]{2,1,0:T(8,128)(2,1)S(1)} all-to-all(bf16[16,8,512]{2,1,0:T(8,128)(2,1)S(1)} %broadcast_in_dim.42), channel_id=1, replica_groups={{3,19,35,51,79,95,111,127,2,18,34,50,78,94,110,126},{7,23,39,55,75,91,1..., dimensions={0} | all-to-all | bytes 262144 | tf_op jit(solution)/shard_map/all_to_all | solution.py:297
  43.8 9.5 %all_to_all.92 = bf16[16,8,512]{2,1,0:T(8,128)(2,1)S(1)} all-to-all(bf16[16,8,512]{2,1,0:T(8,128)(2,1)S(1)} %broadcast_in_dim.43), channel_id=1, replica_groups={{0,4,8,12,128,132,136,140,256,260,264,268,384,388,392,396},{16,20,24,28..., dimensions={0} | all-to-all | bytes 262144 | tf_op jit(solution)/shard_map/all_to_all | solution.py:297
  54.6 9.3 %all_to_all.93 = bf16[16,8,512]{2,1,0:T(8,128)(2,1)S(1)} all-to-all(bf16[16,8,512]{2,1,0:T(8,128)(2,1)S(1)} %bitcast.59), channel_id=1, replica_groups={{0,4,8,12,128,132,136,140,256,260,264,268,384,388,392,396},{16,20,24,28..., dimensions={0} | all-to-all | bytes 262144 | tf_op jit(solution)/shard_map/all_to_all | solution.py:302
  63.9 9.3 %all_to_all.94 = bf16[16,8,512]{2,1,0:T(8,128)(2,1)S(1)} all-to-all(bf16[16,8,512]{2,1,0:T(8,128)(2,1)S(1)} %broadcast_in_dim.44), channel_id=1, replica_groups={{2,18,34,50,78,94,110,126,1,17,33,49,77,93,109,125},{6,22,38,54,74,90,1..., dimensions={0} | all-to-all | bytes 262144 | tf_op jit(solution)/shard_map/all_to_all | solution.py:297
  73.2 9.3 %all_to_all.95 = bf16[16,8,512]{2,1,0:T(8,128)(2,1)S(1)} all-to-all(bf16[16,8,512]{2,1,0:T(8,128)(2,1)S(1)} %broadcast_in_dim.45), channel_id=1, replica_groups={{0,4,8,12,128,132,136,140,256,260,264,268,384,388,392,396},{16,20,24,28..., dimensions={0} | all-to-all | bytes 262144 | tf_op jit(solution)/shard_map/all_to_all | solution.py:297
  83.7 9.3 %all_to_all.96 = bf16[16,8,512]{2,1,0:T(8,128)(2,1)S(1)} all-to-all(bf16[16,8,512]{2,1,0:T(8,128)(2,1)S(1)} %bitcast.58), channel_id=1, replica_groups={{0,4,8,12,128,132,136,140,256,260,264,268,384,388,392,396},{16,20,24,28..., dimensions={0} | all-to-all | bytes 262144 | tf_op jit(solution)/shard_map/all_to_all | solution.py:302
  93.1 9.3 %all_to_all.97 = bf16[16,8,512]{2,1,0:T(8,128)(2,1)S(1)} all-to-all(bf16[16,8,512]{2,1,0:T(8,128)(2,1)S(1)} %broadcast_in_dim.46), channel_id=1, replica_groups={{1,17,33,49,77,93,109,125,0,16,32,48,76,92,108,124},{5,21,37,53,73,89,1..., dimensions={0} | all-to-all | bytes 262144 | tf_op jit(solution)/shard_map/all_to_all | solution.py:297
  102.4 10.4 %all_to_all.98 = bf16[16,16,512]{2,1,0:T(8,128)(2,1)S(1)} all-to-all(bf16[16,16,512]{2,1,0:T(8,128)(2,1)S(1)} %broadcast_in_dim.47), channel_id=1, replica_groups={{0,4,8,12,128,132,136,140,256,260,264,268,384,388,392,396},{16,20,24,28..., dimensions={0} | all-to-all | bytes 524288 | tf_op jit(solution)/shard_map/all_to_all | solution.py:297
  112.8 5.6 %shard_map.62 = (bf16[128,512]{1,0:T(8,128)(2,1)S(1)}, bf16[100,400]{1,0:T(8,128)(2,1)S(1)}, f32[100,400]{1,0:T(8,128)S(1)}) custom-call(bf16[128,512]{1,0:T(8,128)(2,1)S(1)} %bitcast.38, bf16[128,512]{1,0:T(8,128)(2,1)S(1)} %get-tuple-element.31.rest_ref, bf16[128,512]{1,0:T(8,128)(2,1)S(1)} %get-tuple-element.30.before_ref.third_ref.refs_5_, ...), custom_call_target="tpu_custom_call" | custom-call | tf_op jit(solution)/shard_map/pallas_call | solution.py:264
  118.4 9.5 %all_to_all.99 = bf16[16,8,512]{2,1,0:T(8,128)(2,1)S(1)} all-to-all(bf16[16,8,512]{2,1,0:T(8,128)(2,1)S(1)} %bitcast.62), channel_id=1, replica_groups={{0,4,8,12,128,132,136,140,256,260,264,268,384,388,392,396},{16,20,24,28..., dimensions={0} | all-to-all | bytes 262144 | tf_op jit(solution)/shard_map/all_to_all | solution.py:302
  128.0 9.3 %all_to_all.100 = bf16[16,8,512]{2,1,0:T(8,128)(2,1)S(1)} all-to-all(bf16[16,8,512]{2,1,0:T(8,128)(2,1)S(1)} %broadcast_in_dim.48), channel_id=1, replica_groups={{1,17,33,49,77,93,109,125,2,18,34,50,78,94,110,126},{5,21,37,53,73,89,1..., dimensions={0} | all-to-all | bytes 262144 | tf_op jit(solution)/shard_map/all_to_all | solution.py:297
  137.3 9.3 %all_to_all.101 = bf16[16,8,512]{2,1,0:T(8,128)(2,1)S(1)} all-to-all(bf16[16,8,512]{2,1,0:T(8,128)(2,1)S(1)} %broadcast_in_dim.49), channel_id=1, replica_groups={{0,4,8,12,128,132,136,140,256,260,264,268,384,388,392,396},{16,20,24,28..., dimensions={0} | all-to-all | bytes 262144 | tf_op jit(solution)/shard_map/all_to_all | solution.py:297
  146.6 5.5 %shard_map.63 = (bf16[128,512]{1,0:T(8,128)(2,1)S(1)}, bf16[100,400]{1,0:T(8,128)(2,1)S(1)}) custom-call(bf16[128,512]{1,0:T(8,128)(2,1)S(1)} %bitcast.51, bf16[128,512]{1,0:T(8,128)(2,1)S(1)} %bitcast.45, bf16[4,400,400]{2,1,0:T(8,128)(2,1)S(1)} %bitcast.35, bf16[128,512]{1,0:T(8,128)(2,1)S(1)} %bitcast.39), custom_call_target="tpu_custom_call" | custom-call | tf_op jit(solution)/shard_map/pallas_call | solution.py:264
  152.1 9.3 %all_to_all.102 = bf16[16,8,512]{2,1,0:T(8,128)(2,1)S(1)} all-to-all(bf16[16,8,512]{2,1,0:T(8,128)(2,1)S(1)} %bitcast.64), channel_id=1, replica_groups={{0,4,8,12,128,132,136,140,256,260,264,268,384,388,392,396},{16,20,24,28..., dimensions={0} | all-to-all | bytes 262144 | tf_op jit(solution)/shard_map/all_to_all | solution.py:302
  161.4 46.9 %all_to_all.103 = bf16[16,8,512]{2,1,0:T(8,128)(2,1)S(1)} all-to-all(bf16[16,8,512]{2,1,0:T(8,128)(2,1)S(1)} %broadcast_in_dim.50), channel_id=1, replica_groups={{2,18,34,50,78,94,110,126,3,19,35,51,79,95,111,127},{6,22,38,54,74,90,1..., dimensions={0} | all-to-all | bytes 262144 | tf_op jit(solution)/shard_map/all_to_all | solution.py:297
  208.3 9.0 %all_to_all.104 = bf16[16,8,512]{2,1,0:T(8,128)(2,1)S(1)} all-to-all(bf16[16,8,512]{2,1,0:T(8,128)(2,1)S(1)} %broadcast_in_dim.51), channel_id=1, replica_groups={{0,4,8,12,128,132,136,140,256,260,264,268,384,388,392,396},{16,20,24,28..., dimensions={0} | all-to-all | bytes 262144 | tf_op jit(solution)/shard_map/all_to_all | solution.py:297
  217.4 5.4 %shard_map.64 = (bf16[128,512]{1,0:T(8,128)(2,1)S(1)}, f32[4,100,100]{2,1,0:T(8,128)S(1)}) custom-call(s32[1]{0:T(128)} %bitcast.x_ref.refs_0_, bf16[128,512]{1,0:T(8,128)(2,1)S(1)} %bitcast.53, bf16[128,512]{1,0:T(8,128)(2,1)S(1)} %bitcast.40, bf16[4,400,400]{2,1,0:T(8,128)(2,1)S(1)} %bitcast.36, bf16[400,100]{1,0:T(8,128)(2,1)S(1)} %copy-done, ...), custom_call_target="tpu_custom_call" | custom-call | tf_op jit(solution)/shard_map/pallas_call | solution.py:264
  222.8 9.3 %all_to_all.105 = bf16[16,8,512]{2,1,0:T(8,128)(2,1)S(1)} all-to-all(bf16[16,8,512]{2,1,0:T(8,128)(2,1)S(1)} %bitcast.61), channel_id=1, replica_groups={{0,4,8,12,128,132,136,140,256,260,264,268,384,388,392,396},{16,20,24,28..., dimensions={0} | all-to-all | bytes 262144 | tf_op jit(solution)/shard_map/all_to_all | solution.py:302
  232.2 18.9 %all_to_all.106 = bf16[8,8,512]{2,1,0:T(8,128)(2,1)S(1)} all-to-all(bf16[8,8,512]{2,1,0:T(8,128)(2,1)S(1)} %broadcast_in_dim.52), channel_id=1, replica_groups={{0,16,32,48,76,92,108,124},{4,20,36,52,72,88,104,120},{8,24,40,56,68,84..., dimensions={0} | all-to-all | bytes 131072 | tf_op jit(solution)/shard_map/all_to_all | solution.py:297
  251.1 9.1 %all_to_all.107 = bf16[16,8,512]{2,1,0:T(8,128)(2,1)S(1)} all-to-all(bf16[16,8,512]{2,1,0:T(8,128)(2,1)S(1)} %broadcast_in_dim.53), channel_id=1, replica_groups={{0,4,8,12,128,132,136,140,256,260,264,268,384,388,392,396},{16,20,24,28..., dimensions={0} | all-to-all | bytes 262144 | tf_op jit(solution)/shard_map/all_to_all | solution.py:297
  260.1 4.4 %shard_map.65 = (bf16[4,100,100]{2,1,0:T(8,128)(2,1)S(1)}, f32[100,400]{1,0:T(8,128)S(1)}) custom-call(s32[1]{0:T(128)} %bitcast.x_ref.refs_0_, f32[100,400]{1,0:T(8,128)S(1)} %get-tuple-element.15.refs_1_, bf16[128,512]{1,0:T(8,128)(2,1)S(1)} %bitcast.52, bf16[128,512]{1,0:T(8,128)(2,1)S(1)} %bitcast.54, bf16[128,512]{1,0:T(8,128)(2,1)S(1)} %bitcast.57, ...), custom_call_target="tpu_custom_call" | custom-call | tf_op jit(solution)/shard_map/pallas_call | solution.py:264
  (35 shorter events, 5.4 us)
Async XLA Ops:
  1.5 1.8 copy-start
  1.6 1.8 copy-start.1

commit v5 on v4

--- a/solution.py
+++ b/solution.py
@@ -22,10 +22,8 @@
 PARAMS = pltpu.CompilerParams(vmem_limit_bytes=24 * 1024 * 1024)
 
 
-def dot(a, b, ca, cb, precision=None):
-    return lax.dot_general(
-        a, b, (((ca,), (cb,)), ((), ())), precision=precision, preferred_element_type=F32
-    )
+def dot(a, b, ca, cb):
+    return lax.dot_general(a, b, (((ca,), (cb,)), ((), ())), preferred_element_type=F32)
 
 
 def inverse_factor(gram):
@@ -36,6 +34,8 @@
     lane = lax.broadcasted_iota(jnp.int32, (8, 128), 1)
     sub = lax.broadcasted_iota(jnp.int32, (8, 128), 0)
 
+    none = jnp.where(lane >= 128, 1.0, 0.0)
+
     def column(tile, j):
         return jnp.broadcast_to(tile[:, j : j + 1], (8, 128))
 
@@ -47,11 +47,11 @@
         width = min(8, size - base)
         step = lane - base
         columns = {t: [column(tiles[t], base + c) for c in range(width)] for t in range(own, count)}
-        head = columns[own]
+        head = [value + none for value in columns[own]]
         scales, leads = [], []
         tile = tiles[own]
         for s in range(width):
-            scales.append(1.0 / line(head[s], s))
+            scales.append(line(1.0 / head[s], s))
             leads.append([line(head[c], s) if c > s else None for c in range(width)])
             factor = jnp.where(sub > s, head[s] * scales[s], 0.0)
             pivot = jnp.where(step == s, 1.0, line(tile, s))
@@ -79,6 +79,22 @@
     return jnp.concatenate(done, axis=0)[:size, :size]
 
 
+def halves(value):
+    high = value.astype(BF16)
+    return high, (value - high.astype(F32)).astype(BF16)
+
+
+def wide_dot(a, b, ca, cb):
+    a_high, a_low = halves(a)
+    b_high, b_low = halves(b)
+    return dot(a_high, b_high, ca, cb) + (dot(a_high, b_low, ca, cb) + dot(a_low, b_high, ca, cb))
+
+
+def left_wide_dot(a, b, ca, cb):
+    a_high, a_low = halves(a)
+    return dot(a_high, b, ca, cb) + dot(a_low, b, ca, cb)
+
+
 def symmetric_gram(m_value, sketch_t):
     return 0.5 * (dot(m_value, sketch_t, 1, 1) + dot(sketch_t, m_value, 1, 1))
 
@@ -149,7 +165,7 @@
 def project_kernel(m_ref, before_ref, core_ref, sketch_ref, out_ref, carry_ref):
     m_value = m_ref[:SKETCH, :RANK]
     inverse = inverse_factor(symmetric_gram(m_value, before_ref[:SKETCH, :RANK]))
-    carry = dot(inverse, m_value.astype(F32), 1, 0, lax.Precision.HIGHEST).astype(BF16)
+    carry = left_wide_dot(inverse, m_value, 1, 0).astype(BF16)
     carry_ref[...] = carry
     out_ref[...] = jnp.zeros((ROWS, LANES), BF16)
     out_ref[:SKETCH, :RANK] = gram_term(core_ref, carry, sketch_ref[:SKETCH, :RANK]).astype(BF16)
@@ -172,10 +188,9 @@
     m0_ref[:, 256:384] = over_a[:, 256:384] + dot(sb, b[:, 128:], 1, 0) + dot(sc, c, 1, 0) + dot(sd, c_end, 1, 1)
     m0_ref[:, 384:400] = over_a[:, 384:400] + dot(sb, b_end, 1, 0) + dot(sc, c_end, 1, 0) + dot(sd, d_end, 1, 0)
     m_value = m0_ref[...]
-    high = m_value.astype(BF16)
-    low = (m_value - high.astype(F32)).astype(BF16)
+    high, low = halves(m_value)
     inverse = inverse_factor(symmetric_gram(high, s) + symmetric_gram(low, s))
-    carry = dot(inverse, m_value, 1, 0, lax.Precision.HIGHEST).astype(BF16)
+    carry = wide_dot(inverse, m_value, 1, 0).astype(BF16)
     carry_ref[...] = carry
     out_ref[...] = jnp.zeros((ROWS, LANES), BF16)
     out_ref[:SKETCH, :RANK] = gram_term(core_ref, carry, sketch_ref[:SKETCH, :RANK]).astype(BF16)
@@ -191,7 +206,7 @@
     def _():
         m_value = m_ref[:SKETCH, :RANK]
         inverse = inverse_factor(symmetric_gram(m_value, before_ref[:SKETCH, :RANK]))
-        carry = dot(inverse, m_value.astype(F32), 1, 0, lax.Precision.HIGHEST).astype(BF16)
+        carry = left_wide_dot(inverse, m_value, 1, 0).astype(BF16)
         total = None
         for i in range(core_ref.shape[0]):
             built = dot(carry, core_ref[i], 1, 0).astype(BF16)
@@ -224,8 +239,7 @@
     images_ref, frames_ref, interface_ref, m_ref, gram_ref,
 ):
     def split_gram(m_value, sketch_t):
-        high = m_value.astype(BF16)
-        low = (m_value - high.astype(F32)).astype(BF16)
+        high, low = halves(m_value)
         return symmetric_gram(high, sketch_t) + symmetric_gram(low, sketch_t)
 
     @pl.when(x_ref[0] == 0)
@@ -250,10 +264,10 @@
         gram_ref[...] = 0.5 * (dot(m_value, right_ref[...], 1, 0) + dot(right_ref[...], m_value, 0, 1))
 
     inverse = inverse_factor(gram_ref[...])
-    interface_ref[...] = dot(inverse, m_ref[...], 1, 0, lax.Precision.HIGHEST)
+    interface_ref[:, 0, :] = wide_dot(inverse, m_ref[...], 1, 0)
     for i in range(images_ref.shape[0]):
-        orth = dot(images_ref[i], inverse, 1, 1, lax.Precision.HIGHEST)
-        frames_ref[i] = (orth * scale).astype(BF16)
+        orth = wide_dot(images_ref[i], inverse, 1, 1)
+        frames_ref[:, i, :] = (orth * scale).astype(BF16)
 
 
 def call(kernel, *operands, out, scalar=False, scratch=()):
@@ -360,10 +374,10 @@
 
     frames, interface = call(
         finish, plane_ref, m_0, m_1, m_2, m_3, third, second, first, right_sketch, images,
-        out=[((modes, SKETCH, SKETCH), BF16), ((SKETCH, RANK), F32)], scalar=True,
+        out=[((SKETCH, modes, SKETCH), BF16), ((SKETCH, 1, RANK), F32)], scalar=True,
         scratch=((SKETCH, RANK), (SKETCH, SKETCH)),
     )
-    return (jnp.swapaxes(frames, 0, 1)[None], interface[None])
+    return (frames[None], interface.reshape(1, SKETCH, RANK))
 
 
 def solution(mesh):

time: 267 us -> 264 us (0.989)
  no operation moved by 1% of the time
where the time goes in v5:
time: 264 us; the launch traced here: 263 us
  blocking collectives  236 us (89%)
  Pallas kernels  23.5 us (9%)
  local copies, waits for them, and re-layouts  2.87 us (1%)
    all_to_all x12, blocking collectives, everywhere(): lax.all_to_all(copies, AXES, 0, 0, axis_index_groups=groups, tiled=True)  177 us
    all_to_all x6, blocking collectives, shard_sum(): lax.all_to_all(tiles, AXES, 0, 0, axis_index_groups=near_groups(range(4))...  59.1 us
    pallas_call x7, Pallas kernels, call(): pl.pallas_call(kernel, out_shape=outs, in_specs=specs, out_specs=[pl.Bloc...  23.5 us

profile of v5, /device:TPU:7, one launch (start us, length us, event | category | flops | bytes accessed | tf_op | source)
XLA Modules:
  0.0 263.4 jit_solution(4083588616224188479)
XLA Ops:
  1.6 1.8 copy.12
  3.4 1.3 shard_map.59
  4.7 12.4 %all_to_all.90 = bf16[16,8,512]{2,1,0:T(8,128)(2,1)S(1)} all-to-all(bf16[16,8,512]{2,1,0:T(8,128)(2,1)S(1)} %bitcast.60), channel_id=1, replica_groups={{0,4,8,12,128,132,136,140,256,260,264,268,384,388,392,396},{16,20,24,28..., dimensions={0} | all-to-all | bytes 262144 | tf_op jit(solution)/shard_map/all_to_all | solution.py:316
  17.1 26.6 %all_to_all.91 = bf16[16,8,512]{2,1,0:T(8,128)(2,1)S(1)} all-to-all(bf16[16,8,512]{2,1,0:T(8,128)(2,1)S(1)} %broadcast_in_dim.39), channel_id=1, replica_groups={{3,19,35,51,79,95,111,127,2,18,34,50,78,94,110,126},{7,23,39,55,75,91,1..., dimensions={0} | all-to-all | bytes 262144 | tf_op jit(solution)/shard_map/all_to_all | solution.py:311
  43.8 9.5 %all_to_all.92 = bf16[16,8,512]{2,1,0:T(8,128)(2,1)S(1)} all-to-all(bf16[16,8,512]{2,1,0:T(8,128)(2,1)S(1)} %broadcast_in_dim.40), channel_id=1, replica_groups={{0,4,8,12,128,132,136,140,256,260,264,268,384,388,392,396},{16,20,24,28..., dimensions={0} | all-to-all | bytes 262144 | tf_op jit(solution)/shard_map/all_to_all | solution.py:311
  54.6 9.3 %all_to_all.93 = bf16[16,8,512]{2,1,0:T(8,128)(2,1)S(1)} all-to-all(bf16[16,8,512]{2,1,0:T(8,128)(2,1)S(1)} %bitcast.57), channel_id=1, replica_groups={{0,4,8,12,128,132,136,140,256,260,264,268,384,388,392,396},{16,20,24,28..., dimensions={0} | all-to-all | bytes 262144 | tf_op jit(solution)/shard_map/all_to_all | solution.py:316
  63.9 9.3 %all_to_all.94 = bf16[16,8,512]{2,1,0:T(8,128)(2,1)S(1)} all-to-all(bf16[16,8,512]{2,1,0:T(8,128)(2,1)S(1)} %broadcast_in_dim.41), channel_id=1, replica_groups={{2,18,34,50,78,94,110,126,1,17,33,49,77,93,109,125},{6,22,38,54,74,90,1..., dimensions={0} | all-to-all | bytes 262144 | tf_op jit(solution)/shard_map/all_to_all | solution.py:311
  73.2 9.3 %all_to_all.95 = bf16[16,8,512]{2,1,0:T(8,128)(2,1)S(1)} all-to-all(bf16[16,8,512]{2,1,0:T(8,128)(2,1)S(1)} %broadcast_in_dim.42), channel_id=1, replica_groups={{0,4,8,12,128,132,136,140,256,260,264,268,384,388,392,396},{16,20,24,28..., dimensions={0} | all-to-all | bytes 262144 | tf_op jit(solution)/shard_map/all_to_all | solution.py:311
  83.7 9.3 %all_to_all.96 = bf16[16,8,512]{2,1,0:T(8,128)(2,1)S(1)} all-to-all(bf16[16,8,512]{2,1,0:T(8,128)(2,1)S(1)} %bitcast.56), channel_id=1, replica_groups={{0,4,8,12,128,132,136,140,256,260,264,268,384,388,392,396},{16,20,24,28..., dimensions={0} | all-to-all | bytes 262144 | tf_op jit(solution)/shard_map/all_to_all | solution.py:316
  93.1 9.3 %all_to_all.97 = bf16[16,8,512]{2,1,0:T(8,128)(2,1)S(1)} all-to-all(bf16[16,8,512]{2,1,0:T(8,128)(2,1)S(1)} %broadcast_in_dim.43), channel_id=1, replica_groups={{1,17,33,49,77,93,109,125,0,16,32,48,76,92,108,124},{5,21,37,53,73,89,1..., dimensions={0} | all-to-all | bytes 262144 | tf_op jit(solution)/shard_map/all_to_all | solution.py:311
  102.4 10.4 %all_to_all.98 = bf16[16,16,512]{2,1,0:T(8,128)(2,1)S(1)} all-to-all(bf16[16,16,512]{2,1,0:T(8,128)(2,1)S(1)} %broadcast_in_dim.44), channel_id=1, replica_groups={{0,4,8,12,128,132,136,140,256,260,264,268,384,388,392,396},{16,20,24,28..., dimensions={0} | all-to-all | bytes 524288 | tf_op jit(solution)/shard_map/all_to_all | solution.py:311
  112.8 5.4 %shard_map.62 = (bf16[128,512]{1,0:T(8,128)(2,1)S(1)}, bf16[100,400]{1,0:T(8,128)(2,1)S(1)}, f32[100,400]{1,0:T(8,128)S(1)}) custom-call(bf16[128,512]{1,0:T(8,128)(2,1)S(1)} %bitcast.36, bf16[128,512]{1,0:T(8,128)(2,1)S(1)} %get-tuple-element.27.rest_ref, bf16[128,512]{1,0:T(8,128)(2,1)S(1)} %get-tuple-element.26.before_ref.third_ref.refs_5_, ...), custom_call_target="tpu_custom_call" | custom-call | tf_op jit(solution)/shard_map/pallas_call | solution.py:278
  118.3 9.5 %all_to_all.99 = bf16[16,8,512]{2,1,0:T(8,128)(2,1)S(1)} all-to-all(bf16[16,8,512]{2,1,0:T(8,128)(2,1)S(1)} %bitcast.59), channel_id=1, replica_groups={{0,4,8,12,128,132,136,140,256,260,264,268,384,388,392,396},{16,20,24,28..., dimensions={0} | all-to-all | bytes 262144 | tf_op jit(solution)/shard_map/all_to_all | solution.py:316
  127.9 9.3 %all_to_all.100 = bf16[16,8,512]{2,1,0:T(8,128)(2,1)S(1)} all-to-all(bf16[16,8,512]{2,1,0:T(8,128)(2,1)S(1)} %broadcast_in_dim.45), channel_id=1, replica_groups={{1,17,33,49,77,93,109,125,2,18,34,50,78,94,110,126},{5,21,37,53,73,89,1..., dimensions={0} | all-to-all | bytes 262144 | tf_op jit(solution)/shard_map/all_to_all | solution.py:311
  137.2 9.3 %all_to_all.101 = bf16[16,8,512]{2,1,0:T(8,128)(2,1)S(1)} all-to-all(bf16[16,8,512]{2,1,0:T(8,128)(2,1)S(1)} %broadcast_in_dim.46), channel_id=1, replica_groups={{0,4,8,12,128,132,136,140,256,260,264,268,384,388,392,396},{16,20,24,28..., dimensions={0} | all-to-all | bytes 262144 | tf_op jit(solution)/shard_map/all_to_all | solution.py:311
  146.5 5.0 %shard_map.63 = (bf16[128,512]{1,0:T(8,128)(2,1)S(1)}, bf16[100,400]{1,0:T(8,128)(2,1)S(1)}) custom-call(bf16[128,512]{1,0:T(8,128)(2,1)S(1)} %bitcast.49, bf16[128,512]{1,0:T(8,128)(2,1)S(1)} %bitcast.43, bf16[4,400,400]{2,1,0:T(8,128)(2,1)S(1)} %bitcast.33, bf16[128,512]{1,0:T(8,128)(2,1)S(1)} %bitcast.37), custom_call_target="tpu_custom_call" | custom-call | tf_op jit(solution)/shard_map/pallas_call | solution.py:278
  151.4 9.3 %all_to_all.102 = bf16[16,8,512]{2,1,0:T(8,128)(2,1)S(1)} all-to-all(bf16[16,8,512]{2,1,0:T(8,128)(2,1)S(1)} %bitcast.61), channel_id=1, replica_groups={{0,4,8,12,128,132,136,140,256,260,264,268,384,388,392,396},{16,20,24,28..., dimensions={0} | all-to-all | bytes 262144 | tf_op jit(solution)/shard_map/all_to_all | solution.py:316
  160.8 46.9 %all_to_all.103 = bf16[16,8,512]{2,1,0:T(8,128)(2,1)S(1)} all-to-all(bf16[16,8,512]{2,1,0:T(8,128)(2,1)S(1)} %broadcast_in_dim.47), channel_id=1, replica_groups={{2,18,34,50,78,94,110,126,3,19,35,51,79,95,111,127},{6,22,38,54,74,90,1..., dimensions={0} | all-to-all | bytes 262144 | tf_op jit(solution)/shard_map/all_to_all | solution.py:311
  207.7 9.0 %all_to_all.104 = bf16[16,8,512]{2,1,0:T(8,128)(2,1)S(1)} all-to-all(bf16[16,8,512]{2,1,0:T(8,128)(2,1)S(1)} %broadcast_in_dim.48), channel_id=1, replica_groups={{0,4,8,12,128,132,136,140,256,260,264,268,384,388,392,396},{16,20,24,28..., dimensions={0} | all-to-all | bytes 262144 | tf_op jit(solution)/shard_map/all_to_all | solution.py:311
  216.7 4.9 %shard_map.64 = (bf16[128,512]{1,0:T(8,128)(2,1)S(1)}, f32[4,100,100]{2,1,0:T(8,128)S(1)}) custom-call(s32[1]{0:T(128)} %bitcast.x_ref.refs_0_, bf16[128,512]{1,0:T(8,128)(2,1)S(1)} %bitcast.51, bf16[128,512]{1,0:T(8,128)(2,1)S(1)} %bitcast.38, bf16[4,400,400]{2,1,0:T(8,128)(2,1)S(1)} %bitcast.34, bf16[400,100]{1,0:T(8,128)(2,1)S(1)} %copy-done, ...), custom_call_target="tpu_custom_call" | custom-call | tf_op jit(solution)/shard_map/pallas_call | solution.py:278
  221.7 9.3 %all_to_all.105 = bf16[16,8,512]{2,1,0:T(8,128)(2,1)S(1)} all-to-all(bf16[16,8,512]{2,1,0:T(8,128)(2,1)S(1)} %bitcast.58), channel_id=1, replica_groups={{0,4,8,12,128,132,136,140,256,260,264,268,384,388,392,396},{16,20,24,28..., dimensions={0} | all-to-all | bytes 262144 | tf_op jit(solution)/shard_map/all_to_all | solution.py:316
  231.0 18.9 %all_to_all.106 = bf16[8,8,512]{2,1,0:T(8,128)(2,1)S(1)} all-to-all(bf16[8,8,512]{2,1,0:T(8,128)(2,1)S(1)} %broadcast_in_dim.49), channel_id=1, replica_groups={{0,16,32,48,76,92,108,124},{4,20,36,52,72,88,104,120},{8,24,40,56,68,84..., dimensions={0} | all-to-all | bytes 131072 | tf_op jit(solution)/shard_map/all_to_all | solution.py:311
  249.9 9.1 %all_to_all.107 = bf16[16,8,512]{2,1,0:T(8,128)(2,1)S(1)} all-to-all(bf16[16,8,512]{2,1,0:T(8,128)(2,1)S(1)} %broadcast_in_dim.50), channel_id=1, replica_groups={{0,4,8,12,128,132,136,140,256,260,264,268,384,388,392,396},{16,20,24,28..., dimensions={0} | all-to-all | bytes 262144 | tf_op jit(solution)/shard_map/all_to_all | solution.py:311
  259.0 4.4 %shard_map.65 = (bf16[100,4,100]{2,1,0:T(4,128)(2,1)}, f32[100,1,400]{2,1,0:T(1,128)}) custom-call(s32[1]{0:T(128)} %bitcast.x_ref.refs_0_, f32[100,400]{1,0:T(8,128)S(1)} %get-tuple-element.15.refs_1_, bf16[128,512]{1,0:T(8,128)(2,1)S(1)} %bitcast.50, bf16[128,512]{1,0:T(8,128)(2,1)S(1)} %bitcast.52, bf16[128,512]{1,0:T(8,128)(2,1)S(1)} %bitcast.55, ...), custom_call_target="tpu_custom_call" | custom-call | tf_op jit(solution)/shard_map/pallas_call | solution.py:278
  (33 shorter events, 3.8 us)
Async XLA Ops:
  1.5 1.8 copy-start
  1.6 1.8 copy-start.1

commit v6 on v5

--- a/solution.py
+++ b/solution.py
@@ -17,6 +17,7 @@
 SKETCH = 100
 ROWS = 128
 LANES = 512
+MAIN = 384
 F32 = jnp.float32
 BF16 = jnp.bfloat16
 PARAMS = pltpu.CompilerParams(vmem_limit_bytes=24 * 1024 * 1024)
@@ -95,28 +96,43 @@
     return dot(a_high, b, ca, cb) + dot(a_low, b, ca, cb)
 
 
-def symmetric_gram(m_value, sketch_t):
-    return 0.5 * (dot(m_value, sketch_t, 1, 1) + dot(sketch_t, m_value, 1, 1))
-
-
-def sketch_term(core_ref, sketch_core_ref, sketch, dim):
-    total = None
+def read(ref):
+    return ref[:SKETCH, :MAIN], ref[104:120, :SKETCH]
+
+
+def write(ref, main, rest):
+    ref[...] = jnp.zeros(ref.shape, BF16)
+    ref[:SKETCH, :MAIN] = main.astype(BF16)
+    ref[104:120, :SKETCH] = rest.astype(BF16)
+
+
+def symmetric_gram(m_pieces, sketch_pieces):
+    main, rest = m_pieces
+    sketch, sketch_rest = sketch_pieces
+    return 0.5 * (
+        dot(main, sketch, 1, 1)
+        + dot(rest, sketch_rest, 0, 0)
+        + dot(sketch, main, 1, 1)
+        + dot(sketch_rest, rest, 0, 0)
+    )
+
+
+def sketch_term(out_ref, core_ref, sketch_core_ref, partial_of):
+    total = rest = None
     for i in range(core_ref.shape[0]):
-        partial = dot(core_ref[i], sketch, 1, dim).astype(BF16)
-        term = dot(sketch_core_ref[i], partial, 1, 1)
-        total = term if total is None else total + term
-    return total
+        partial = partial_of(core_ref[i]).astype(BF16)
+        term = dot(sketch_core_ref[i], partial[:MAIN], 1, 1)
+        end = dot(partial[MAIN:], sketch_core_ref[i], 1, 1)
+        total, rest = (term, end) if total is None else (total + term, rest + end)
+    write(out_ref, total, rest)
 
 
 def first_kernel(x_ref, core_ref, sketch_core_ref, right_ref, left_ref, out_ref, rest_ref):
-    out_ref[...] = jnp.zeros((ROWS, LANES), BF16)
-    rest_ref[...] = jnp.zeros((ROWS, LANES), BF16)
+    rest_ref[...] = jnp.zeros((ROWS, MAIN), BF16)
 
     @pl.when(x_ref[0] != 0)
     def _():
-        out_ref[:SKETCH, :RANK] = sketch_term(
-            core_ref, sketch_core_ref, right_ref[...], 0
-        ).astype(BF16)
+        sketch_term(out_ref, core_ref, sketch_core_ref, lambda core: dot(core, right_ref[...], 1, 0))
 
     @pl.when(x_ref[0] == 0)
     def _():
@@ -127,19 +143,23 @@
             term = dot(built, built, 0, 0)
             square = term if square is None else square + term
         square = square.astype(BF16)
+        out_ref[:, RANK:] = jnp.zeros((ROWS, LANES - RANK), BF16)
         out_ref[:, :RANK] = square[:128]
+        out_ref[:, 400:416] = square[128:256, 384:400]
+        out_ref[:, 416:432] = square[256:384, 384:400]
+        out_ref[:16, 432:448] = square[384:400, 384:400]
         rest_ref[:, :256] = square[128:256, 128:384]
         rest_ref[:, 256:384] = square[256:384, 256:384]
-        rest_ref[:, 384:400] = square[128:256, 384:400]
-        rest_ref[:, 400:416] = square[256:384, 384:400]
-        rest_ref[:16, 416:432] = square[384:400, 384:400]
 
 
 def sketch_kernel(core_ref, sketch_core_ref, sketch_ref, out_ref):
-    out_ref[...] = jnp.zeros((ROWS, LANES), BF16)
-    out_ref[:SKETCH, :RANK] = sketch_term(
-        core_ref, sketch_core_ref, sketch_ref[:SKETCH, :RANK], 1
-    ).astype(BF16)
+    sketch, rest = read(sketch_ref)
+    sketch_term(
+        out_ref,
+        core_ref,
+        sketch_core_ref,
+        lambda core: dot(core[:, :MAIN], sketch, 1, 1) + dot(core[:, MAIN:], rest, 1, 0),
+    )
 
 
 def last_sketch_kernel(x_ref, core_ref, sketch_core_ref, sketch_ref, rest_ref, out_ref):
@@ -152,119 +172,138 @@
         sketch_kernel(core_ref, sketch_core_ref, sketch_ref, out_ref)
 
 
-def gram_term(core_ref, carry_low, sketch_t):
+def gram_term(out_ref, core_ref, carry, images_of, images_ref=None):
+    total = rest = None
+    for i in range(core_ref.shape[0]):
+        built = dot(carry, core_ref[i], 1, 0).astype(BF16)
+        images = images_of(built)
+        if images_ref is not None:
+            images_ref[i] = images
+        images = images.astype(BF16)
+        term = dot(images, built[:, :MAIN], 0, 0)
+        end = dot(built[:, MAIN:], images, 0, 0)
+        total, rest = (term, end) if total is None else (total + term, rest + end)
+    write(out_ref, total, rest)
+
+
+def images_with(sketch_ref):
+    sketch, rest = read(sketch_ref)
+    return lambda built: dot(built[:, :MAIN], sketch, 1, 1) + dot(built[:, MAIN:], rest, 1, 0)
+
+
+def project(carry_ref, m_ref, before_ref):
+    main, rest = read(m_ref)
+    inverse = inverse_factor(symmetric_gram((main, rest), read(before_ref)))
+    carry_ref[:, :MAIN] = left_wide_dot(inverse, main, 1, 0).astype(BF16)
+    carry_ref[:, MAIN:] = left_wide_dot(inverse, rest, 1, 1).astype(BF16)
+
+
+def project_kernel(m_ref, before_ref, core_ref, sketch_ref, out_ref, carry_ref):
+    project(carry_ref, m_ref, before_ref)
+    gram_term(out_ref, core_ref, carry_ref[...], images_with(sketch_ref))
+
+
+def m_0_gram(m_value, sketch, sketch_rest):
+    high, low = halves(m_value)
     total = None
-    for i in range(core_ref.shape[0]):
-        built = dot(carry_low, core_ref[i], 1, 0).astype(BF16)
-        images = dot(built, sketch_t, 1, 1).astype(BF16)
-        term = dot(images, built, 0, 0)
+    for part in (high, low):
+        term = 0.5 * (
+            dot(part[:, :MAIN], sketch, 1, 1)
+            + dot(part[:, MAIN:], sketch_rest, 1, 0)
+            + dot(sketch, part[:, :MAIN], 1, 1)
+            + dot(sketch_rest, part[:, MAIN:], 0, 1)
+        )
         total = term if total is None else total + term
     return total
 
 
-def project_kernel(m_ref, before_ref, core_ref, sketch_ref, out_ref, carry_ref):
-    m_value = m_ref[:SKETCH, :RANK]
-    inverse = inverse_factor(symmetric_gram(m_value, before_ref[:SKETCH, :RANK]))
-    carry = left_wide_dot(inverse, m_value, 1, 0).astype(BF16)
-    carry_ref[...] = carry
-    out_ref[...] = jnp.zeros((ROWS, LANES), BF16)
-    out_ref[:SKETCH, :RANK] = gram_term(core_ref, carry, sketch_ref[:SKETCH, :RANK]).astype(BF16)
-
-
 def first_project_kernel(upper_ref, rest_ref, before_ref, core_ref, sketch_ref, out_ref, carry_ref, m0_ref):
-    s = before_ref[:SKETCH, :RANK]
-    sa, sb, sc, sd = s[:, :128], s[:, 128:256], s[:, 256:384], s[:, 384:400]
+    s, sd = read(before_ref)
+    sa, sb, sc = s[:, :128], s[:, 128:256], s[:, 256:384]
     a = upper_ref[:, :RANK]
     b = rest_ref[:, :256]
     c = rest_ref[:, 256:384]
-    b_end = rest_ref[:, 384:400]
-    c_end = rest_ref[:, 400:416]
-    d_end = rest_ref[:16, 416:432]
+    b_end = upper_ref[:, 400:416]
+    c_end = upper_ref[:, 416:432]
+    d_end = upper_ref[:16, 432:448]
     over_a = dot(sa, a, 1, 0)
-    m0_ref[:, :128] = over_a[:, :128] + dot(s[:, 128:], a[:, 128:], 1, 1)
+    m0_ref[:, :128] = over_a[:, :128] + dot(s[:, 128:], a[:, 128:MAIN], 1, 1) + dot(sd, a[:, MAIN:], 0, 1)
     m0_ref[:, 128:256] = (
-        over_a[:, 128:256] + dot(sb, b[:, :128], 1, 0) + dot(sc, b[:, 128:], 1, 1) + dot(sd, b_end, 1, 1)
-    )
-    m0_ref[:, 256:384] = over_a[:, 256:384] + dot(sb, b[:, 128:], 1, 0) + dot(sc, c, 1, 0) + dot(sd, c_end, 1, 1)
-    m0_ref[:, 384:400] = over_a[:, 384:400] + dot(sb, b_end, 1, 0) + dot(sc, c_end, 1, 0) + dot(sd, d_end, 1, 0)
+        over_a[:, 128:256] + dot(sb, b[:, :128], 1, 0) + dot(sc, b[:, 128:], 1, 1) + dot(sd, b_end, 0, 1)
+    )
+    m0_ref[:, 256:384] = over_a[:, 256:384] + dot(sb, b[:, 128:], 1, 0) + dot(sc, c, 1, 0) + dot(sd, c_end, 0, 1)
+    m0_ref[:, 384:400] = over_a[:, 384:400] + dot(sb, b_end, 1, 0) + dot(sc, c_end, 1, 0) + dot(sd, d_end, 0, 0)
     m_value = m0_ref[...]
-    high, low = halves(m_value)
-    inverse = inverse_factor(symmetric_gram(high, s) + symmetric_gram(low, s))
+    inverse = inverse_factor(m_0_gram(m_value, s, sd))
     carry = wide_dot(inverse, m_value, 1, 0).astype(BF16)
     carry_ref[...] = carry
-    out_ref[...] = jnp.zeros((ROWS, LANES), BF16)
-    out_ref[:SKETCH, :RANK] = gram_term(core_ref, carry, sketch_ref[:SKETCH, :RANK]).astype(BF16)
+    gram_term(out_ref, core_ref, carry, images_with(sketch_ref))
 
 
 def last_project_kernel(
     x_ref, m_ref, before_ref, core_ref, right_ref, left_ref, carry_1_ref, carry_2_ref,
-    third_ref, second_ref, first_ref, out_ref, images_ref,
+    third_ref, second_ref, first_ref, out_ref, images_ref, carry_ref,
 ):
-    out_ref[...] = jnp.zeros((ROWS, LANES), BF16)
-
     @pl.when(x_ref[0] == 3)
     def _():
-        m_value = m_ref[:SKETCH, :RANK]
-        inverse = inverse_factor(symmetric_gram(m_value, before_ref[:SKETCH, :RANK]))
-        carry = left_wide_dot(inverse, m_value, 1, 0).astype(BF16)
-        total = None
+        project(carry_ref, m_ref, before_ref)
+        gram_term(out_ref, core_ref, carry_ref[...], lambda built: dot(built, right_ref[...], 1, 0), images_ref)
+
+    def only_images(carry, dim, sketch_ref):
+        out_ref[...] = jnp.zeros(out_ref.shape, BF16)
+        images_of = images_with(sketch_ref)
         for i in range(core_ref.shape[0]):
-            built = dot(carry, core_ref[i], 1, 0).astype(BF16)
-            images = dot(built, right_ref[...], 1, 0)
-            images_ref[i] = images
-            term = dot(images.astype(BF16), built, 0, 0)
-            total = term if total is None else total + term
-        out_ref[:SKETCH, :RANK] = total.astype(BF16)
-
-    def images_of(carry, dim, sketch_t):
-        for i in range(core_ref.shape[0]):
-            built = dot(carry, core_ref[i], dim, 0).astype(BF16)
-            images_ref[i] = dot(built, sketch_t, 1, 1)
+            images_ref[i] = images_of(dot(carry, core_ref[i], dim, 0).astype(BF16))
 
     @pl.when(x_ref[0] == 2)
     def _():
-        images_of(carry_2_ref[...], 1, first_ref[:SKETCH, :RANK])
+        only_images(carry_2_ref[...], 1, first_ref)
 
     @pl.when(x_ref[0] == 1)
     def _():
-        images_of(carry_1_ref[...], 1, second_ref[:SKETCH, :RANK])
+        only_images(carry_1_ref[...], 1, second_ref)
 
     @pl.when(x_ref[0] == 0)
     def _():
-        images_of(left_ref[...].astype(BF16), 0, third_ref[:SKETCH, :RANK])
+        only_images(left_ref[...].astype(BF16), 0, third_ref)
 
 
 def final_kernel(
     scale, x_ref, m_0_ref, m_1_ref, m_2_ref, m_3_ref, third_ref, second_ref, first_ref, right_ref,
-    images_ref, frames_ref, interface_ref, m_ref, gram_ref,
+    images_ref, frames_ref, interface_ref, main_ref, rest_ref, gram_ref,
 ):
-    def split_gram(m_value, sketch_t):
-        high, low = halves(m_value)
-        return symmetric_gram(high, sketch_t) + symmetric_gram(low, sketch_t)
+    def take(m_ref):
+        main, rest = read(m_ref)
+        main_ref[...] = main.astype(F32)
+        rest_ref[...] = rest.astype(F32)
+        return main, rest
 
     @pl.when(x_ref[0] == 0)
     def _():
-        m_ref[...] = m_0_ref[...]
-        gram_ref[...] = split_gram(m_0_ref[...], third_ref[:SKETCH, :RANK])
+        m_value = m_0_ref[...]
+        main_ref[...] = m_value[:, :MAIN]
+        rest_ref[...] = m_value[:, MAIN:].T
+        gram_ref[...] = m_0_gram(m_value, *read(third_ref))
 
     @pl.when(x_ref[0] == 1)
     def _():
-        m_ref[...] = m_1_ref[:SKETCH, :RANK].astype(F32)
-        gram_ref[...] = symmetric_gram(m_1_ref[:SKETCH, :RANK], second_ref[:SKETCH, :RANK])
+        gram_ref[...] = symmetric_gram(take(m_1_ref), read(second_ref))
 
     @pl.when(x_ref[0] == 2)
     def _():
-        m_ref[...] = m_2_ref[:SKETCH, :RANK].astype(F32)
-        gram_ref[...] = symmetric_gram(m_2_ref[:SKETCH, :RANK], first_ref[:SKETCH, :RANK])
+        gram_ref[...] = symmetric_gram(take(m_2_ref), read(first_ref))
 
     @pl.when(x_ref[0] == 3)
     def _():
-        m_value = m_3_ref[:SKETCH, :RANK]
-        m_ref[...] = m_value.astype(F32)
-        gram_ref[...] = 0.5 * (dot(m_value, right_ref[...], 1, 0) + dot(right_ref[...], m_value, 0, 1))
+        main, rest = take(m_3_ref)
+        right, right_rest = right_ref[:MAIN], right_ref[MAIN:]
+        gram_ref[...] = 0.5 * (
+            dot(main, right, 1, 0) + dot(rest, right_rest, 0, 0) + dot(right, main, 0, 1) + dot(right_rest, rest, 0, 0)
+        )
 
     inverse = inverse_factor(gram_ref[...])
-    interface_ref[:, 0, :] = wide_dot(inverse, m_ref[...], 1, 0)
+    interface_ref[:, 0, :MAIN] = wide_dot(inverse, main_ref[...], 1, 0)
+    interface_ref[:, 0, MAIN:] = wide_dot(inverse, rest_ref[...], 1, 1)
     for i in range(images_ref.shape[0]):
         orth = wide_dot(images_ref[i], inverse, 1, 1)
         frames_ref[:, i, :] = (orth * scale).astype(BF16)
@@ -280,12 +319,13 @@
         out_shape=outs,
         in_specs=specs,
         out_specs=[pl.BlockSpec(memory_space=pltpu.VMEM) for _ in outs],
-        scratch_shapes=[pltpu.VMEM(shape, F32) for shape in scratch],
+        scratch_shapes=[pltpu.VMEM(*piece) for piece in scratch],
         compiler_params=PARAMS,
     )(*operands)
 
 
-PAYLOAD = ((ROWS, LANES), BF16)
+WIDE = ((ROWS, LANES), BF16)
+PAYLOAD = ((ROWS, MAIN), BF16)
 
 
 def device(place, zh, x):
@@ -312,7 +352,7 @@
 
 
 def shard_sum(value):
-    tiles = value.reshape(len(NEAR), ROWS // len(NEAR), LANES)
+    tiles = value.reshape(len(NEAR), ROWS // len(NEAR), -1)
     return added(lax.all_to_all(tiles, AXES, 0, 0, axis_index_groups=near_groups(range(4)), tiled=True))
 
 
@@ -341,10 +381,10 @@
     left_t = left_interface.T
 
     def full(shard):
-        return whole(shard).reshape(ROWS, LANES)
+        return whole(shard).reshape(ROWS, -1)
 
     term, rest = call(
-        first_kernel, plane_ref, core, sketch_core, right_sketch, left_t, out=[PAYLOAD, PAYLOAD], scalar=True
+        first_kernel, plane_ref, core, sketch_core, right_sketch, left_t, out=[WIDE, PAYLOAD], scalar=True
     )
     first = full(added(paired(term, ((3, 2), (0, 1)))[0]))
     (term,) = call(sketch_kernel, core, sketch_core, first, out=[PAYLOAD])
@@ -352,8 +392,8 @@
     (term,) = call(last_sketch_kernel, plane_ref, core, sketch_core, second, rest, out=[PAYLOAD], scalar=True)
     both = paired(term, ((1, 0),))
     arrived = whole(jnp.concatenate([added(both[0]), added(both[1])], axis=0))
-    third = arrived[:, :8].reshape(ROWS, LANES)
-    rest = arrived[:, 8:].reshape(ROWS, LANES)
+    third = arrived[:, :8].reshape(ROWS, MAIN)
+    rest = arrived[:, 8:].reshape(ROWS, MAIN)
 
     carry_kind = ((SKETCH, RANK), BF16)
     term, carry_1, m_0 = call(
@@ -365,6 +405,7 @@
     term, images = call(
         last_project_kernel, plane_ref, m_2, first, core, right_sketch, left_t, carry_1, carry_2,
         third, second, first, out=[PAYLOAD, ((modes, SKETCH, SKETCH), F32)], scalar=True,
+        scratch=[((SKETCH, RANK), BF16)],
     )
     alone = [group for x in range(4) for group in far_groups((x,))]
     m_3 = full(added(everywhere(shard_sum(term), alone)))
@@ -375,7 +416,7 @@
     frames, interface = call(
         finish, plane_ref, m_0, m_1, m_2, m_3, third, second, first, right_sketch, images,
         out=[((SKETCH, modes, SKETCH), BF16), ((SKETCH, 1, RANK), F32)], scalar=True,
-        scratch=((SKETCH, RANK), (SKETCH, SKETCH)),
+        scratch=[((SKETCH, MAIN), F32), ((RANK - MAIN, SKETCH), F32), ((SKETCH, SKETCH), F32)],
     )
     return (frames[None], interface.reshape(1, SKETCH, RANK))
 

time: 264 us -> 257 us (0.973)
  blocking collectives: 236 us -> 227 us
    all_to_all x12, blocking collectives: 177 us -> 170 us  [everywhere(): lax.all_to_all(copies, AXES, 0, 0, axis_index_groups=groups, tiled=True)]
where the time goes in v6:
time: 257 us; the launch traced here: 256 us
  blocking collectives  227 us (88%)
  Pallas kernels  25.2 us (10%)
  local copies, waits for them, and re-layouts  2.87 us (1%)
    all_to_all x12, blocking collectives, everywhere(): lax.all_to_all(copies, AXES, 0, 0, axis_index_groups=groups, tiled=True)  170 us
    all_to_all x6, blocking collectives, shard_sum(): lax.all_to_all(tiles, AXES, 0, 0, axis_index_groups=near_groups(range(4))...  57.2 us
    pallas_call x7, Pallas kernels, call(): pl.pallas_call(kernel, out_shape=outs, in_specs=specs, out_specs=[pl.Bloc...  25.2 us

profile of v6, /device:TPU:7, one launch (start us, length us, event | category | flops | bytes accessed | tf_op | source)
XLA Modules:
  0.0 255.8 jit_solution(6771744793840210571)
XLA Ops:
  1.6 1.8 copy.12
  4.7 12.4 %all_to_all.90 = bf16[16,8,512]{2,1,0:T(8,128)(2,1)S(1)} all-to-all(bf16[16,8,512]{2,1,0:T(8,128)(2,1)S(1)} %bitcast.58), channel_id=1, replica_groups={{0,4,8,12,128,132,136,140,256,260,264,268,384,388,392,396},{16,20,24,28..., dimensions={0} | all-to-all | bytes 262144 | tf_op jit(solution)/shard_map/all_to_all | solution.py:356
  17.2 26.6 %all_to_all.91 = bf16[16,8,512]{2,1,0:T(8,128)(2,1)S(1)} all-to-all(bf16[16,8,512]{2,1,0:T(8,128)(2,1)S(1)} %broadcast_in_dim.39), channel_id=1, replica_groups={{3,19,35,51,79,95,111,127,2,18,34,50,78,94,110,126},{7,23,39,55,75,91,1..., dimensions={0} | all-to-all | bytes 262144 | tf_op jit(solution)/shard_map/all_to_all | solution.py:351
  43.9 9.5 %all_to_all.92 = bf16[16,8,512]{2,1,0:T(8,128)(2,1)S(1)} all-to-all(bf16[16,8,512]{2,1,0:T(8,128)(2,1)S(1)} %broadcast_in_dim.40), channel_id=1, replica_groups={{0,4,8,12,128,132,136,140,256,260,264,268,384,388,392,396},{16,20,24,28..., dimensions={0} | all-to-all | bytes 262144 | tf_op jit(solution)/shard_map/all_to_all | solution.py:351
  53.4 1.6 shard_map.60
  55.0 9.0 %all_to_all.93 = bf16[16,8,384]{2,1,0:T(8,128)(2,1)S(1)} all-to-all(bf16[16,8,384]{2,1,0:T(8,128)(2,1)S(1)} %bitcast.57), channel_id=1, replica_groups={{0,4,8,12,128,132,136,140,256,260,264,268,384,388,392,396},{16,20,24,28..., dimensions={0} | all-to-all | bytes 196608 | tf_op jit(solution)/shard_map/all_to_all | solution.py:356
  64.0 8.9 %all_to_all.94 = bf16[16,8,384]{2,1,0:T(8,128)(2,1)S(1)} all-to-all(bf16[16,8,384]{2,1,0:T(8,128)(2,1)S(1)} %broadcast_in_dim.41), channel_id=1, replica_groups={{2,18,34,50,78,94,110,126,1,17,33,49,77,93,109,125},{6,22,38,54,74,90,1..., dimensions={0} | all-to-all | bytes 196608 | tf_op jit(solution)/shard_map/all_to_all | solution.py:351
  72.9 8.9 %all_to_all.95 = bf16[16,8,384]{2,1,0:T(8,128)(2,1)S(1)} all-to-all(bf16[16,8,384]{2,1,0:T(8,128)(2,1)S(1)} %broadcast_in_dim.42), channel_id=1, replica_groups={{0,4,8,12,128,132,136,140,256,260,264,268,384,388,392,396},{16,20,24,28..., dimensions={0} | all-to-all | bytes 196608 | tf_op jit(solution)/shard_map/all_to_all | solution.py:351
  83.4 8.9 %all_to_all.96 = bf16[16,8,384]{2,1,0:T(8,128)(2,1)S(1)} all-to-all(bf16[16,8,384]{2,1,0:T(8,128)(2,1)S(1)} %bitcast.55), channel_id=1, replica_groups={{0,4,8,12,128,132,136,140,256,260,264,268,384,388,392,396},{16,20,24,28..., dimensions={0} | all-to-all | bytes 196608 | tf_op jit(solution)/shard_map/all_to_all | solution.py:356
  92.3 8.9 %all_to_all.97 = bf16[16,8,384]{2,1,0:T(8,128)(2,1)S(1)} all-to-all(bf16[16,8,384]{2,1,0:T(8,128)(2,1)S(1)} %broadcast_in_dim.43), channel_id=1, replica_groups={{1,17,33,49,77,93,109,125,0,16,32,48,76,92,108,124},{5,21,37,53,73,89,1..., dimensions={0} | all-to-all | bytes 196608 | tf_op jit(solution)/shard_map/all_to_all | solution.py:351
  101.3 9.7 %all_to_all.98 = bf16[16,16,384]{2,1,0:T(8,128)(2,1)S(1)} all-to-all(bf16[16,16,384]{2,1,0:T(8,128)(2,1)S(1)} %broadcast_in_dim.44), channel_id=1, replica_groups={{0,4,8,12,128,132,136,140,256,260,264,268,384,388,392,396},{16,20,24,28..., dimensions={0} | all-to-all | bytes 393216 | tf_op jit(solution)/shard_map/all_to_all | solution.py:351
  111.0 5.6 %shard_map.62 = (bf16[128,384]{1,0:T(8,128)(2,1)S(1)}, bf16[100,400]{1,0:T(8,128)(2,1)S(1)}, f32[100,400]{1,0:T(8,128)S(1)}) custom-call(bf16[128,512]{1,0:T(8,128)(2,1)S(1)} %bitcast.36, bf16[128,384]{1,0:T(8,128)(2,1)S(1)} %get-tuple-element.27.rest_ref, bf16[128,384]{1,0:T(8,128)(2,1)S(1)} %get-tuple-element.26.before_ref.third_ref.refs_5_, ...), custom_call_target="tpu_custom_call" | custom-call | tf_op jit(solution)/shard_map/pallas_call | solution.py:317
  116.6 9.1 %all_to_all.99 = bf16[16,8,384]{2,1,0:T(8,128)(2,1)S(1)} all-to-all(bf16[16,8,384]{2,1,0:T(8,128)(2,1)S(1)} %bitcast.60), channel_id=1, replica_groups={{0,4,8,12,128,132,136,140,256,260,264,268,384,388,392,396},{16,20,24,28..., dimensions={0} | all-to-all | bytes 196608 | tf_op jit(solution)/shard_map/all_to_all | solution.py:356
  125.8 8.9 %all_to_all.100 = bf16[16,8,384]{2,1,0:T(8,128)(2,1)S(1)} all-to-all(bf16[16,8,384]{2,1,0:T(8,128)(2,1)S(1)} %broadcast_in_dim.45), channel_id=1, replica_groups={{1,17,33,49,77,93,109,125,2,18,34,50,78,94,110,126},{5,21,37,53,73,89,1..., dimensions={0} | all-to-all | bytes 196608 | tf_op jit(solution)/shard_map/all_to_all | solution.py:351
  134.7 8.9 %all_to_all.101 = bf16[16,8,384]{2,1,0:T(8,128)(2,1)S(1)} all-to-all(bf16[16,8,384]{2,1,0:T(8,128)(2,1)S(1)} %broadcast_in_dim.46), channel_id=1, replica_groups={{0,4,8,12,128,132,136,140,256,260,264,268,384,388,392,396},{16,20,24,28..., dimensions={0} | all-to-all | bytes 196608 | tf_op jit(solution)/shard_map/all_to_all | solution.py:351
  143.6 5.2 %shard_map.63 = (bf16[128,384]{1,0:T(8,128)(2,1)S(1)}, bf16[100,400]{1,0:T(8,128)(2,1)S(1)}) custom-call(bf16[128,384]{1,0:T(8,128)(2,1)S(1)} %bitcast.51, bf16[128,384]{1,0:T(8,128)(2,1)S(1)} %bitcast.43, bf16[4,400,400]{2,1,0:T(8,128)(2,1)S(1)} %bitcast.33, bf16[128,512]{1,0:T(8,128)(2,1)S(1)} %bitcast.37), custom_call_target="tpu_custom_call" | custom-call | tf_op jit(solution)/shard_map/pallas_call | solution.py:317
  148.8 8.9 %all_to_all.102 = bf16[16,8,384]{2,1,0:T(8,128)(2,1)S(1)} all-to-all(bf16[16,8,384]{2,1,0:T(8,128)(2,1)S(1)} %bitcast.61), channel_id=1, replica_groups={{0,4,8,12,128,132,136,140,256,260,264,268,384,388,392,396},{16,20,24,28..., dimensions={0} | all-to-all | bytes 196608 | tf_op jit(solution)/shard_map/all_to_all | solution.py:356
  157.8 44.2 %all_to_all.103 = bf16[16,8,384]{2,1,0:T(8,128)(2,1)S(1)} all-to-all(bf16[16,8,384]{2,1,0:T(8,128)(2,1)S(1)} %broadcast_in_dim.47), channel_id=1, replica_groups={{2,18,34,50,78,94,110,126,3,19,35,51,79,95,111,127},{6,22,38,54,74,90,1..., dimensions={0} | all-to-all | bytes 196608 | tf_op jit(solution)/shard_map/all_to_all | solution.py:351
  202.0 9.1 %all_to_all.104 = bf16[16,8,384]{2,1,0:T(8,128)(2,1)S(1)} all-to-all(bf16[16,8,384]{2,1,0:T(8,128)(2,1)S(1)} %broadcast_in_dim.48), channel_id=1, replica_groups={{0,4,8,12,128,132,136,140,256,260,264,268,384,388,392,396},{16,20,24,28..., dimensions={0} | all-to-all | bytes 196608 | tf_op jit(solution)/shard_map/all_to_all | solution.py:351
  211.1 5.2 %shard_map.64 = (bf16[128,384]{1,0:T(8,128)(2,1)S(1)}, f32[4,100,100]{2,1,0:T(8,128)S(1)}) custom-call(s32[1]{0:T(128)} %bitcast.x_ref.refs_0_, bf16[128,384]{1,0:T(8,128)(2,1)S(1)} %bitcast.49, bf16[128,512]{1,0:T(8,128)(2,1)S(1)} %bitcast.38, bf16[4,400,400]{2,1,0:T(8,128)(2,1)S(1)} %bitcast.34, bf16[400,100]{1,0:T(8,128)(2,1)S(1)} %copy-done, ...), custom_call_target="tpu_custom_call" | custom-call | tf_op jit(solution)/shard_map/pallas_call | solution.py:317
  216.2 8.9 %all_to_all.105 = bf16[16,8,384]{2,1,0:T(8,128)(2,1)S(1)} all-to-all(bf16[16,8,384]{2,1,0:T(8,128)(2,1)S(1)} %bitcast.59), channel_id=1, replica_groups={{0,4,8,12,128,132,136,140,256,260,264,268,384,388,392,396},{16,20,24,28..., dimensions={0} | all-to-all | bytes 196608 | tf_op jit(solution)/shard_map/all_to_all | solution.py:356
  225.1 16.8 %all_to_all.106 = bf16[8,8,384]{2,1,0:T(8,128)(2,1)S(1)} all-to-all(bf16[8,8,384]{2,1,0:T(8,128)(2,1)S(1)} %broadcast_in_dim.49), channel_id=1, replica_groups={{0,16,32,48,76,92,108,124},{4,20,36,52,72,88,104,120},{8,24,40,56,68,84..., dimensions={0} | all-to-all | bytes 98304 | tf_op jit(solution)/shard_map/all_to_all | solution.py:351
  242.0 9.1 %all_to_all.107 = bf16[16,8,384]{2,1,0:T(8,128)(2,1)S(1)} all-to-all(bf16[16,8,384]{2,1,0:T(8,128)(2,1)S(1)} %broadcast_in_dim.50), channel_id=1, replica_groups={{0,4,8,12,128,132,136,140,256,260,264,268,384,388,392,396},{16,20,24,28..., dimensions={0} | all-to-all | bytes 196608 | tf_op jit(solution)/shard_map/all_to_all | solution.py:351
  251.1 4.7 %shard_map.65 = (bf16[100,4,100]{2,1,0:T(4,128)(2,1)}, f32[100,1,400]{2,1,0:T(1,128)}) custom-call(s32[1]{0:T(128)} %bitcast.x_ref.refs_0_, f32[100,400]{1,0:T(8,128)S(1)} %get-tuple-element.15.refs_1_, bf16[128,384]{1,0:T(8,128)(2,1)S(1)} %bitcast.52, bf16[128,384]{1,0:T(8,128)(2,1)S(1)} %bitcast.50, bf16[128,384]{1,0:T(8,128)(2,1)S(1)} %bitcast.56, ...), custom_call_target="tpu_custom_call" | custom-call | tf_op jit(solution)/shard_map/pallas_call | solution.py:317
  (33 shorter events, 4.2 us)
Async XLA Ops:
  1.5 1.8 copy-start
  1.6 1.8 copy-start.1

commit v7 on v6

--- a/solution.py
+++ b/solution.py
@@ -338,37 +338,51 @@
     return index
 
 
-def near_groups(planes):
-    return [[device(place, zh, x) for place in NEAR] for x in planes for zh in range(FAR)]
+def near_group(zh, x):
+    return [device(place, zh, x) for place in NEAR]
 
 
 def far_groups(planes):
-    return [[device(place, zh, x) for x in planes for zh in range(FAR)] for place in NEAR]
+    groups = [[device(place, zh, x) for zh in range(FAR)] for x in planes for place in NEAR]
+    for x in range(4):
+        if x not in planes:
+            for zh in range(FAR):
+                for chip in range(2):
+                    groups.append([device(place, zh, x) for place in NEAR if place[1] == chip])
+    return groups
+
+
+def pair_groups(pairs):
+    groups = [near_group(zh, x) + near_group(zh, other) for x, other in pairs for zh in range(FAR)]
+    for x in range(4):
+        if not any(x in pair for pair in pairs):
+            groups += [near_group(zh, x) + near_group(zh + 1, x) for zh in range(0, FAR, 2)]
+    return groups
+
+
+NEAR_GROUPS = [near_group(zh, x) for x in range(4) for zh in range(FAR)]
+
+
+def exchanged(tiles, groups):
+    return lax.all_to_all(tiles, AXES, 0, 0, axis_index_groups=groups, tiled=True)
 
 
 def everywhere(shard, groups):
-    copies = jnp.broadcast_to(shard, (len(groups[0]), *shard.shape))
-    return lax.all_to_all(copies, AXES, 0, 0, axis_index_groups=groups, tiled=True)
-
-
-def shard_sum(value):
-    tiles = value.reshape(len(NEAR), ROWS // len(NEAR), -1)
-    return added(lax.all_to_all(tiles, AXES, 0, 0, axis_index_groups=near_groups(range(4)), tiled=True))
+    return exchanged(jnp.broadcast_to(shard, (len(groups[0]), *shard.shape)), groups)
 
 
 def added(pieces):
     return pieces.astype(F32).sum(axis=0).astype(BF16)
 
 
-def paired(value, pairs):
-    spare = [x for x in range(4) if not any(x in pair for pair in pairs)]
-    groups = [group for pair in pairs for group in far_groups(pair)] + near_groups(spare)
-    pieces = everywhere(shard_sum(value), groups)
-    return pieces[:FAR], pieces[FAR:]
-
-
-def whole(shard):
-    return everywhere(shard, near_groups(range(4)))
+def plane_sum(value, planes):
+    tiles = value.reshape(len(NEAR), ROWS // len(NEAR), -1)
+    return added(everywhere(added(exchanged(tiles, NEAR_GROUPS)), far_groups(planes)))
+
+
+def whole_pair(shard, pairs):
+    rows = everywhere(shard, pair_groups(pairs))
+    return rows[: len(NEAR)].reshape(ROWS, -1), rows[len(NEAR) :].reshape(ROWS, -1)
 
 
 def body(train_cores, sketch_cores, left_interface, right_sketch):
@@ -380,35 +394,28 @@
     frame_scale = math.sqrt(SKETCH * modes * lax.axis_size(MODE))
     left_t = left_interface.T
 
-    def full(shard):
-        return whole(shard).reshape(ROWS, -1)
-
     term, rest = call(
         first_kernel, plane_ref, core, sketch_core, right_sketch, left_t, out=[WIDE, PAYLOAD], scalar=True
     )
-    first = full(added(paired(term, ((3, 2), (0, 1)))[0]))
+    first = whole_pair(plane_sum(term, (3, 0)), ((3, 2), (0, 1)))[0]
     (term,) = call(sketch_kernel, core, sketch_core, first, out=[PAYLOAD])
-    second = full(added(paired(term, ((2, 1),))[0]))
+    second = whole_pair(plane_sum(term, (2,)), ((2, 1),))[0]
     (term,) = call(last_sketch_kernel, plane_ref, core, sketch_core, second, rest, out=[PAYLOAD], scalar=True)
-    both = paired(term, ((1, 0),))
-    arrived = whole(jnp.concatenate([added(both[0]), added(both[1])], axis=0))
-    third = arrived[:, :8].reshape(ROWS, MAIN)
-    rest = arrived[:, 8:].reshape(ROWS, MAIN)
+    third, rest = whole_pair(plane_sum(term, (1, 0)), ((1, 0),))
 
     carry_kind = ((SKETCH, RANK), BF16)
     term, carry_1, m_0 = call(
         first_project_kernel, first, rest, third, core, second, out=[PAYLOAD, carry_kind, ((SKETCH, RANK), F32)]
     )
-    m_1 = full(added(paired(term, ((1, 2),))[0]))
+    m_1 = whole_pair(plane_sum(term, (1,)), ((1, 2),))[0]
     term, carry_2 = call(project_kernel, m_1, second, core, first, out=[PAYLOAD, carry_kind])
-    m_2 = full(added(paired(term, ((2, 3),))[0]))
+    m_2 = whole_pair(plane_sum(term, (2,)), ((2, 3),))[0]
     term, images = call(
         last_project_kernel, plane_ref, m_2, first, core, right_sketch, left_t, carry_1, carry_2,
         third, second, first, out=[PAYLOAD, ((modes, SKETCH, SKETCH), F32)], scalar=True,
         scratch=[((SKETCH, RANK), BF16)],
     )
-    alone = [group for x in range(4) for group in far_groups((x,))]
-    m_3 = full(added(everywhere(shard_sum(term), alone)))
+    m_3 = everywhere(plane_sum(term, (3,)), NEAR_GROUPS).reshape(ROWS, -1)
 
     def finish(*refs):
         final_kernel(frame_scale, *refs)

time: 257 us -> 252 us (0.981)
  blocking collectives: 227 us -> 222 us
    all_to_all x18, blocking collectives: 227 us -> 222 us  [exchanged(): lax.all_to_all(tiles, AXES, 0, 0, axis_index_groups=groups, tiled=True)]
where the time goes in v7:
time: 252 us; the launch traced here: 251 us
  blocking collectives  222 us (88%)
  Pallas kernels  25.2 us (10%)
  local copies, waits for them, and re-layouts  2.92 us (1%)
    all_to_all x18, blocking collectives, exchanged(): lax.all_to_all(tiles, AXES, 0, 0, axis_index_groups=groups, tiled=True)  222 us
    pallas_call x7, Pallas kernels, call(): pl.pallas_call(kernel, out_shape=outs, in_specs=specs, out_specs=[pl.Bloc...  25.2 us

profile of v7, /device:TPU:7, one launch (start us, length us, event | category | flops | bytes accessed | tf_op | source)
XLA Modules:
  0.0 251.2 jit_solution(5911592961002719487)
XLA Ops:
  1.6 1.8 copy.12
  4.7 12.4 %all_to_all.90 = bf16[16,8,512]{2,1,0:T(8,128)(2,1)S(1)} all-to-all(bf16[16,8,512]{2,1,0:T(8,128)(2,1)S(1)} %bitcast.47), channel_id=1, replica_groups={{0,4,8,12,128,132,136,140,256,260,264,268,384,388,392,396},{16,20,24,28..., dimensions={0} | all-to-all | bytes 262144 | tf_op jit(solution)/shard_map/all_to_all | solution.py:367
  17.2 26.3 %all_to_all.91 = bf16[8,8,512]{2,1,0:T(8,128)(2,1)S(1)} all-to-all(bf16[8,8,512]{2,1,0:T(8,128)(2,1)S(1)} %broadcast_in_dim.39), channel_id=1, replica_groups={{3,19,35,51,79,95,111,127},{7,23,39,55,75,91,107,123},{11,27,43,59,71,8..., dimensions={0} | all-to-all | bytes 131072 | tf_op jit(solution)/shard_map/all_to_all | solution.py:367
  43.5 11.0 %all_to_all.92 = bf16[32,8,512]{2,1,0:T(8,128)(2,1)S(1)} all-to-all(bf16[32,8,512]{2,1,0:T(8,128)(2,1)S(1)} %broadcast_in_dim.40), channel_id=1, replica_groups={{3,7,11,15,131,135,139,143,259,263,267,271,387,391,395,399,2,6,10,14,13..., dimensions={0} | all-to-all | bytes 524288 | tf_op jit(solution)/shard_map/all_to_all | solution.py:367
  56.1 8.9 %all_to_all.93 = bf16[16,8,384]{2,1,0:T(8,128)(2,1)S(1)} all-to-all(bf16[16,8,384]{2,1,0:T(8,128)(2,1)S(1)} %bitcast.46), channel_id=1, replica_groups={{0,4,8,12,128,132,136,140,256,260,264,268,384,388,392,396},{16,20,24,28..., dimensions={0} | all-to-all | bytes 196608 | tf_op jit(solution)/shard_map/all_to_all | solution.py:367
  65.0 7.7 %all_to_all.94 = bf16[8,8,384]{2,1,0:T(8,128)(2,1)S(1)} all-to-all(bf16[8,8,384]{2,1,0:T(8,128)(2,1)S(1)} %broadcast_in_dim.41), channel_id=1, replica_groups={{2,18,34,50,78,94,110,126},{6,22,38,54,74,90,106,122},{10,26,42,58,70,8..., dimensions={0} | all-to-all | bytes 98304 | tf_op jit(solution)/shard_map/all_to_all | solution.py:367
  72.8 13.6 %all_to_all.95 = bf16[32,8,384]{2,1,0:T(8,128)(2,1)S(1)} all-to-all(bf16[32,8,384]{2,1,0:T(8,128)(2,1)S(1)} %broadcast_in_dim.42), channel_id=1, replica_groups={{2,6,10,14,130,134,138,142,258,262,266,270,386,390,394,398,1,5,9,13,129..., dimensions={0} | all-to-all | bytes 393216 | tf_op jit(solution)/shard_map/all_to_all | solution.py:367
  86.4 1.6 shard_map.61
  88.0 9.3 %all_to_all.96 = bf16[16,8,384]{2,1,0:T(8,128)(2,1)S(1)} all-to-all(bf16[16,8,384]{2,1,0:T(8,128)(2,1)S(1)} %bitcast.44), channel_id=1, replica_groups={{0,4,8,12,128,132,136,140,256,260,264,268,384,388,392,396},{16,20,24,28..., dimensions={0} | all-to-all | bytes 196608 | tf_op jit(solution)/shard_map/all_to_all | solution.py:367
  97.4 7.7 %all_to_all.97 = bf16[8,8,384]{2,1,0:T(8,128)(2,1)S(1)} all-to-all(bf16[8,8,384]{2,1,0:T(8,128)(2,1)S(1)} %broadcast_in_dim.43), channel_id=1, replica_groups={{1,17,33,49,77,93,109,125},{5,21,37,53,73,89,105,121},{9,25,41,57,69,85..., dimensions={0} | all-to-all | bytes 98304 | tf_op jit(solution)/shard_map/all_to_all | solution.py:367
  105.2 13.0 %all_to_all.98 = bf16[32,8,384]{2,1,0:T(8,128)(2,1)S(1)} all-to-all(bf16[32,8,384]{2,1,0:T(8,128)(2,1)S(1)} %broadcast_in_dim.44), channel_id=1, replica_groups={{1,5,9,13,129,133,137,141,257,261,265,269,385,389,393,397,0,4,8,12,128,..., dimensions={0} | all-to-all | bytes 393216 | tf_op jit(solution)/shard_map/all_to_all | solution.py:367
  118.2 5.6 %shard_map.62 = (bf16[128,384]{1,0:T(8,128)(2,1)S(1)}, bf16[100,400]{1,0:T(8,128)(2,1)S(1)}, f32[100,400]{1,0:T(8,128)S(1)}) custom-call(bf16[128,512]{1,0:T(8,128)(2,1)S(1)} %slice_bitcast_fusion.sketch_ref.upper_ref.before_ref.first_ref.refs_7_, bf16[128,384]{1,0:T(8,128)(2,1)S(1)} %get-tuple-element.25.rest_ref, ...), custom_call_target="tpu_custom_call" | custom-call | tf_op jit(solution)/shard_map/pallas_call | solution.py:317
  123.8 9.3 %all_to_all.99 = bf16[16,8,384]{2,1,0:T(8,128)(2,1)S(1)} all-to-all(bf16[16,8,384]{2,1,0:T(8,128)(2,1)S(1)} %bitcast.49), channel_id=1, replica_groups={{0,4,8,12,128,132,136,140,256,260,264,268,384,388,392,396},{16,20,24,28..., dimensions={0} | all-to-all | bytes 196608 | tf_op jit(solution)/shard_map/all_to_all | solution.py:367
  133.2 7.7 %all_to_all.100 = bf16[8,8,384]{2,1,0:T(8,128)(2,1)S(1)} all-to-all(bf16[8,8,384]{2,1,0:T(8,128)(2,1)S(1)} %broadcast_in_dim.45), channel_id=1, replica_groups={{1,17,33,49,77,93,109,125},{5,21,37,53,73,89,105,121},{9,25,41,57,69,85..., dimensions={0} | all-to-all | bytes 98304 | tf_op jit(solution)/shard_map/all_to_all | solution.py:367
  141.0 13.0 %all_to_all.101 = bf16[32,8,384]{2,1,0:T(8,128)(2,1)S(1)} all-to-all(bf16[32,8,384]{2,1,0:T(8,128)(2,1)S(1)} %broadcast_in_dim.46), channel_id=1, replica_groups={{1,5,9,13,129,133,137,141,257,261,265,269,385,389,393,397,2,6,10,14,130..., dimensions={0} | all-to-all | bytes 393216 | tf_op jit(solution)/shard_map/all_to_all | solution.py:367
  154.0 5.2 %shard_map.63 = (bf16[128,384]{1,0:T(8,128)(2,1)S(1)}, bf16[100,400]{1,0:T(8,128)(2,1)S(1)}) custom-call(bf16[128,384]{1,0:T(8,128)(2,1)S(1)} %slice_bitcast_fusion.2.m_ref.refs_2_, bf16[128,384]{1,0:T(8,128)(2,1)S(1)} %slice_bitcast_fusion.5.sketch_ref.before_ref.second_ref.refs_6_, bf16[4,400,400]{2,1,0:T(8,128)(2,1)S(1)} %bitcast.37, ...), custom_call_target="tpu_custom_call" | custom-call | tf_op jit(solution)/shard_map/pallas_call | solution.py:317
  159.2 9.3 %all_to_all.102 = bf16[16,8,384]{2,1,0:T(8,128)(2,1)S(1)} all-to-all(bf16[16,8,384]{2,1,0:T(8,128)(2,1)S(1)} %bitcast.50), channel_id=1, replica_groups={{0,4,8,12,128,132,136,140,256,260,264,268,384,388,392,396},{16,20,24,28..., dimensions={0} | all-to-all | bytes 196608 | tf_op jit(solution)/shard_map/all_to_all | solution.py:367
  168.6 7.7 %all_to_all.103 = bf16[8,8,384]{2,1,0:T(8,128)(2,1)S(1)} all-to-all(bf16[8,8,384]{2,1,0:T(8,128)(2,1)S(1)} %broadcast_in_dim.47), channel_id=1, replica_groups={{2,18,34,50,78,94,110,126},{6,22,38,54,74,90,106,122},{10,26,42,58,70,8..., dimensions={0} | all-to-all | bytes 98304 | tf_op jit(solution)/shard_map/all_to_all | solution.py:367
  176.4 31.7 %all_to_all.104 = bf16[32,8,384]{2,1,0:T(8,128)(2,1)S(1)} all-to-all(bf16[32,8,384]{2,1,0:T(8,128)(2,1)S(1)} %broadcast_in_dim.48), channel_id=1, replica_groups={{2,6,10,14,130,134,138,142,258,262,266,270,386,390,394,398,3,7,11,15,13..., dimensions={0} | all-to-all | bytes 393216 | tf_op jit(solution)/shard_map/all_to_all | solution.py:367
  208.0 5.2 %shard_map.64 = (bf16[128,384]{1,0:T(8,128)(2,1)S(1)}, f32[4,100,100]{2,1,0:T(8,128)S(1)}) custom-call(s32[1]{0:T(128)} %bitcast.x_ref.refs_0_, bf16[128,384]{1,0:T(8,128)(2,1)S(1)} %slice_bitcast_fusion.1.m_ref.refs_3_, bf16[128,512]{1,0:T(8,128)(2,1)S(1)} %slice_bitcast_fusion.sketch_ref.upper_ref.before_ref.first_ref.refs_7_, ...), custom_call_target="tpu_custom_call" | custom-call | tf_op jit(solution)/shard_map/pallas_call | solution.py:317
  213.2 9.0 %all_to_all.105 = bf16[16,8,384]{2,1,0:T(8,128)(2,1)S(1)} all-to-all(bf16[16,8,384]{2,1,0:T(8,128)(2,1)S(1)} %bitcast.48), channel_id=1, replica_groups={{0,4,8,12,128,132,136,140,256,260,264,268,384,388,392,396},{16,20,24,28..., dimensions={0} | all-to-all | bytes 196608 | tf_op jit(solution)/shard_map/all_to_all | solution.py:367
  222.2 15.5 %all_to_all.106 = bf16[8,8,384]{2,1,0:T(8,128)(2,1)S(1)} all-to-all(bf16[8,8,384]{2,1,0:T(8,128)(2,1)S(1)} %broadcast_in_dim.49), channel_id=1, replica_groups={{3,19,35,51,79,95,111,127},{7,23,39,55,75,91,107,123},{11,27,43,59,71,8..., dimensions={0} | all-to-all | bytes 98304 | tf_op jit(solution)/shard_map/all_to_all | solution.py:367
  237.7 8.7 %all_to_all.107 = bf16[16,8,384]{2,1,0:T(8,128)(2,1)S(1)} all-to-all(bf16[16,8,384]{2,1,0:T(8,128)(2,1)S(1)} %broadcast_in_dim.50), channel_id=1, replica_groups={{0,4,8,12,128,132,136,140,256,260,264,268,384,388,392,396},{16,20,24,28..., dimensions={0} | all-to-all | bytes 196608 | tf_op jit(solution)/shard_map/all_to_all | solution.py:367
  246.4 4.7 %shard_map.65 = (bf16[100,4,100]{2,1,0:T(4,128)(2,1)}, f32[100,1,400]{2,1,0:T(1,128)}) custom-call(s32[1]{0:T(128)} %bitcast.x_ref.refs_0_, f32[100,400]{1,0:T(8,128)S(1)} %get-tuple-element.15.refs_1_, bf16[128,384]{1,0:T(8,128)(2,1)S(1)} %slice_bitcast_fusion.2.m_ref.refs_2_, bf16[128,384]{1,0:T(8,128)(2,1)S(1)} %slice_bitcast_fusion.1.m_ref.refs_3_, ...), custom_call_target="tpu_custom_call" | custom-call | tf_op jit(solution)/shard_map/pallas_call | solution.py:317
  (36 shorter events, 4.2 us)
Async XLA Ops:
  1.5 1.8 copy-start
  1.6 1.8 copy-start.1

commit v8 on v7

--- a/solution.py
+++ b/solution.py
@@ -11,8 +11,9 @@
 AXES = ("y", "zh", "zl", "c", "x")
 MODE = ("y", "zh", "zl", "c")
 SIZES = (4, 8, 2, 2, 4)
-NEAR = tuple((y, zl, c) for y in range(4) for zl in range(2) for c in range(2))
+NEAR = tuple(((0, 2, 1, 3)[k % 4], (k + k // 4) % 2, k // 8) for k in range(16))
 FAR = 8
+FAR_ORDER = (0, 4, 1, 5, 2, 6, 3, 7)
 RANK = 400
 SKETCH = 100
 ROWS = 128
@@ -343,7 +344,7 @@
 
 
 def far_groups(planes):
-    groups = [[device(place, zh, x) for zh in range(FAR)] for x in planes for place in NEAR]
+    groups = [[device(place, zh, x) for zh in FAR_ORDER] for x in planes for place in NEAR]
     for x in range(4):
         if x not in planes:
             for zh in range(FAR):

time: 252 us -> 252 us (level)
  no operation moved by 1% of the time
where the time goes in v8:
time: 252 us; the launch traced here: 251 us
  blocking collectives  222 us (88%)
  Pallas kernels  25.2 us (10%)
  local copies, waits for them, and re-layouts  2.92 us (1%)
    all_to_all x18, blocking collectives, exchanged(): lax.all_to_all(tiles, AXES, 0, 0, axis_index_groups=groups, tiled=True)  222 us
    pallas_call x7, Pallas kernels, call(): pl.pallas_call(kernel, out_shape=outs, in_specs=specs, out_specs=[pl.Bloc...  25.2 us

profile of v8, /device:TPU:7, one launch (start us, length us, event | category | flops | bytes accessed | tf_op | source)
XLA Modules:
  0.0 251.1 jit_solution(5159119787241937625)
XLA Ops:
  1.6 1.8 copy.12
  4.7 12.4 %all_to_all.90 = bf16[16,8,512]{2,1,0:T(8,128)(2,1)S(1)} all-to-all(bf16[16,8,512]{2,1,0:T(8,128)(2,1)S(1)} %bitcast.47), channel_id=1, replica_groups={{0,264,128,392,8,256,136,384,4,268,132,396,12,260,140,388},{16,280,144,..., dimensions={0} | all-to-all | bytes 262144 | tf_op jit(solution)/shard_map/all_to_all | solution.py:368
  17.2 25.3 %all_to_all.91 = bf16[8,8,512]{2,1,0:T(8,128)(2,1)S(1)} all-to-all(bf16[8,8,512]{2,1,0:T(8,128)(2,1)S(1)} %broadcast_in_dim.39), channel_id=1, replica_groups={{3,79,19,95,35,111,51,127},{267,327,283,343,299,359,315,375},{131,207,1..., dimensions={0} | all-to-all | bytes 131072 | tf_op jit(solution)/shard_map/all_to_all | solution.py:368
  42.6 10.9 %all_to_all.92 = bf16[32,8,512]{2,1,0:T(8,128)(2,1)S(1)} all-to-all(bf16[32,8,512]{2,1,0:T(8,128)(2,1)S(1)} %broadcast_in_dim.40), channel_id=1, replica_groups={{3,267,131,395,11,259,139,387,7,271,135,399,15,263,143,391,2,266,130,39..., dimensions={0} | all-to-all | bytes 524288 | tf_op jit(solution)/shard_map/all_to_all | solution.py:368
  55.1 8.7 %all_to_all.93 = bf16[16,8,384]{2,1,0:T(8,128)(2,1)S(1)} all-to-all(bf16[16,8,384]{2,1,0:T(8,128)(2,1)S(1)} %bitcast.46), channel_id=1, replica_groups={{0,264,128,392,8,256,136,384,4,268,132,396,12,260,140,388},{16,280,144,..., dimensions={0} | all-to-all | bytes 196608 | tf_op jit(solution)/shard_map/all_to_all | solution.py:368
  63.9 8.1 %all_to_all.94 = bf16[8,8,384]{2,1,0:T(8,128)(2,1)S(1)} all-to-all(bf16[8,8,384]{2,1,0:T(8,128)(2,1)S(1)} %broadcast_in_dim.41), channel_id=1, replica_groups={{2,78,18,94,34,110,50,126},{266,326,282,342,298,358,314,374},{130,206,1..., dimensions={0} | all-to-all | bytes 98304 | tf_op jit(solution)/shard_map/all_to_all | solution.py:368
  72.1 15.2 %all_to_all.95 = bf16[32,8,384]{2,1,0:T(8,128)(2,1)S(1)} all-to-all(bf16[32,8,384]{2,1,0:T(8,128)(2,1)S(1)} %broadcast_in_dim.42), channel_id=1, replica_groups={{2,266,130,394,10,258,138,386,6,270,134,398,14,262,142,390,1,265,129,39..., dimensions={0} | all-to-all | bytes 393216 | tf_op jit(solution)/shard_map/all_to_all | solution.py:368
  87.3 1.6 shard_map.61
  88.8 9.1 %all_to_all.96 = bf16[16,8,384]{2,1,0:T(8,128)(2,1)S(1)} all-to-all(bf16[16,8,384]{2,1,0:T(8,128)(2,1)S(1)} %bitcast.44), channel_id=1, replica_groups={{0,264,128,392,8,256,136,384,4,268,132,396,12,260,140,388},{16,280,144,..., dimensions={0} | all-to-all | bytes 196608 | tf_op jit(solution)/shard_map/all_to_all | solution.py:368
  98.0 8.1 %all_to_all.97 = bf16[8,8,384]{2,1,0:T(8,128)(2,1)S(1)} all-to-all(bf16[8,8,384]{2,1,0:T(8,128)(2,1)S(1)} %broadcast_in_dim.43), channel_id=1, replica_groups={{1,77,17,93,33,109,49,125},{265,325,281,341,297,357,313,373},{129,205,1..., dimensions={0} | all-to-all | bytes 98304 | tf_op jit(solution)/shard_map/all_to_all | solution.py:368
  106.1 14.3 %all_to_all.98 = bf16[32,8,384]{2,1,0:T(8,128)(2,1)S(1)} all-to-all(bf16[32,8,384]{2,1,0:T(8,128)(2,1)S(1)} %broadcast_in_dim.44), channel_id=1, replica_groups={{1,265,129,393,9,257,137,385,5,269,133,397,13,261,141,389,0,264,128,392..., dimensions={0} | all-to-all | bytes 393216 | tf_op jit(solution)/shard_map/all_to_all | solution.py:368
  120.4 5.6 %shard_map.62 = (bf16[128,384]{1,0:T(8,128)(2,1)S(1)}, bf16[100,400]{1,0:T(8,128)(2,1)S(1)}, f32[100,400]{1,0:T(8,128)S(1)}) custom-call(bf16[128,512]{1,0:T(8,128)(2,1)S(1)} %slice_bitcast_fusion.sketch_ref.upper_ref.before_ref.first_ref.refs_7_, bf16[128,384]{1,0:T(8,128)(2,1)S(1)} %get-tuple-element.25.rest_ref, ...), custom_call_target="tpu_custom_call" | custom-call | tf_op jit(solution)/shard_map/pallas_call | solution.py:318
  126.1 9.1 %all_to_all.99 = bf16[16,8,384]{2,1,0:T(8,128)(2,1)S(1)} all-to-all(bf16[16,8,384]{2,1,0:T(8,128)(2,1)S(1)} %bitcast.49), channel_id=1, replica_groups={{0,264,128,392,8,256,136,384,4,268,132,396,12,260,140,388},{16,280,144,..., dimensions={0} | all-to-all | bytes 196608 | tf_op jit(solution)/shard_map/all_to_all | solution.py:368
  135.2 8.1 %all_to_all.100 = bf16[8,8,384]{2,1,0:T(8,128)(2,1)S(1)} all-to-all(bf16[8,8,384]{2,1,0:T(8,128)(2,1)S(1)} %broadcast_in_dim.45), channel_id=1, replica_groups={{1,77,17,93,33,109,49,125},{265,325,281,341,297,357,313,373},{129,205,1..., dimensions={0} | all-to-all | bytes 98304 | tf_op jit(solution)/shard_map/all_to_all | solution.py:368
  143.4 14.3 %all_to_all.101 = bf16[32,8,384]{2,1,0:T(8,128)(2,1)S(1)} all-to-all(bf16[32,8,384]{2,1,0:T(8,128)(2,1)S(1)} %broadcast_in_dim.46), channel_id=1, replica_groups={{1,265,129,393,9,257,137,385,5,269,133,397,13,261,141,389,2,266,130,394..., dimensions={0} | all-to-all | bytes 393216 | tf_op jit(solution)/shard_map/all_to_all | solution.py:368
  157.7 5.2 %shard_map.63 = (bf16[128,384]{1,0:T(8,128)(2,1)S(1)}, bf16[100,400]{1,0:T(8,128)(2,1)S(1)}) custom-call(bf16[128,384]{1,0:T(8,128)(2,1)S(1)} %slice_bitcast_fusion.2.m_ref.refs_2_, bf16[128,384]{1,0:T(8,128)(2,1)S(1)} %slice_bitcast_fusion.5.sketch_ref.before_ref.second_ref.refs_6_, bf16[4,400,400]{2,1,0:T(8,128)(2,1)S(1)} %bitcast.37, ...), custom_call_target="tpu_custom_call" | custom-call | tf_op jit(solution)/shard_map/pallas_call | solution.py:318
  162.9 9.1 %all_to_all.102 = bf16[16,8,384]{2,1,0:T(8,128)(2,1)S(1)} all-to-all(bf16[16,8,384]{2,1,0:T(8,128)(2,1)S(1)} %bitcast.50), channel_id=1, replica_groups={{0,264,128,392,8,256,136,384,4,268,132,396,12,260,140,388},{16,280,144,..., dimensions={0} | all-to-all | bytes 196608 | tf_op jit(solution)/shard_map/all_to_all | solution.py:368
  172.0 8.1 %all_to_all.103 = bf16[8,8,384]{2,1,0:T(8,128)(2,1)S(1)} all-to-all(bf16[8,8,384]{2,1,0:T(8,128)(2,1)S(1)} %broadcast_in_dim.47), channel_id=1, replica_groups={{2,78,18,94,34,110,50,126},{266,326,282,342,298,358,314,374},{130,206,1..., dimensions={0} | all-to-all | bytes 98304 | tf_op jit(solution)/shard_map/all_to_all | solution.py:368
  180.2 27.9 %all_to_all.104 = bf16[32,8,384]{2,1,0:T(8,128)(2,1)S(1)} all-to-all(bf16[32,8,384]{2,1,0:T(8,128)(2,1)S(1)} %broadcast_in_dim.48), channel_id=1, replica_groups={{2,266,130,394,10,258,138,386,6,270,134,398,14,262,142,390,3,267,131,39..., dimensions={0} | all-to-all | bytes 393216 | tf_op jit(solution)/shard_map/all_to_all | solution.py:368
  208.1 5.2 %shard_map.64 = (bf16[128,384]{1,0:T(8,128)(2,1)S(1)}, f32[4,100,100]{2,1,0:T(8,128)S(1)}) custom-call(s32[1]{0:T(128)} %bitcast.x_ref.refs_0_, bf16[128,384]{1,0:T(8,128)(2,1)S(1)} %slice_bitcast_fusion.1.m_ref.refs_3_, bf16[128,512]{1,0:T(8,128)(2,1)S(1)} %slice_bitcast_fusion.sketch_ref.upper_ref.before_ref.first_ref.refs_7_, ...), custom_call_target="tpu_custom_call" | custom-call | tf_op jit(solution)/shard_map/pallas_call | solution.py:318
  213.3 9.0 %all_to_all.105 = bf16[16,8,384]{2,1,0:T(8,128)(2,1)S(1)} all-to-all(bf16[16,8,384]{2,1,0:T(8,128)(2,1)S(1)} %bitcast.48), channel_id=1, replica_groups={{0,264,128,392,8,256,136,384,4,268,132,396,12,260,140,388},{16,280,144,..., dimensions={0} | all-to-all | bytes 196608 | tf_op jit(solution)/shard_map/all_to_all | solution.py:368
  222.3 14.3 %all_to_all.106 = bf16[8,8,384]{2,1,0:T(8,128)(2,1)S(1)} all-to-all(bf16[8,8,384]{2,1,0:T(8,128)(2,1)S(1)} %broadcast_in_dim.49), channel_id=1, replica_groups={{3,79,19,95,35,111,51,127},{267,327,283,343,299,359,315,375},{131,207,1..., dimensions={0} | all-to-all | bytes 98304 | tf_op jit(solution)/shard_map/all_to_all | solution.py:368
  236.7 9.8 %all_to_all.107 = bf16[16,8,384]{2,1,0:T(8,128)(2,1)S(1)} all-to-all(bf16[16,8,384]{2,1,0:T(8,128)(2,1)S(1)} %broadcast_in_dim.50), channel_id=1, replica_groups={{0,264,128,392,8,256,136,384,4,268,132,396,12,260,140,388},{16,280,144,..., dimensions={0} | all-to-all | bytes 196608 | tf_op jit(solution)/shard_map/all_to_all | solution.py:368
  246.4 4.7 %shard_map.65 = (bf16[100,4,100]{2,1,0:T(4,128)(2,1)}, f32[100,1,400]{2,1,0:T(1,128)}) custom-call(s32[1]{0:T(128)} %bitcast.x_ref.refs_0_, f32[100,400]{1,0:T(8,128)S(1)} %get-tuple-element.15.refs_1_, bf16[128,384]{1,0:T(8,128)(2,1)S(1)} %slice_bitcast_fusion.2.m_ref.refs_2_, bf16[128,384]{1,0:T(8,128)(2,1)S(1)} %slice_bitcast_fusion.1.m_ref.refs_3_, ...), custom_call_target="tpu_custom_call" | custom-call | tf_op jit(solution)/shard_map/pallas_call | solution.py:318
  (36 shorter events, 4.2 us)
Async XLA Ops:
  1.5 1.8 copy-start
  1.6 1.8 copy-start.1

commit v9 on v7

--- a/solution.py
+++ b/solution.py
@@ -16,7 +16,6 @@
 RANK = 400
 SKETCH = 100
 ROWS = 128
-LANES = 512
 MAIN = 384
 F32 = jnp.float32
 BF16 = jnp.bfloat16
@@ -143,13 +142,14 @@
             term = dot(built, built, 0, 0)
             square = term if square is None else square + term
         square = square.astype(BF16)
-        out_ref[:, RANK:] = jnp.zeros((ROWS, LANES - RANK), BF16)
-        out_ref[:, :RANK] = square[:128]
-        out_ref[:, 400:416] = square[128:256, 384:400]
-        out_ref[:, 416:432] = square[256:384, 384:400]
-        out_ref[:16, 432:448] = square[384:400, 384:400]
+        out_ref[...] = square[:128, :MAIN]
+        for k in range(4):
+            out_ref[64:128, 16 * k : 16 * k + 16] = square[64 * k : 64 * k + 64, MAIN:]
         rest_ref[:, :256] = square[128:256, 128:384]
         rest_ref[:, 256:384] = square[256:384, 256:384]
+        rest_ref[64:128, 256:272] = square[256:320, MAIN:]
+        rest_ref[64:128, 272:288] = square[320:384, MAIN:]
+        rest_ref[64:80, 288:304] = square[384:400, MAIN:]
 
 
 def sketch_kernel(core_ref, sketch_core_ref, sketch_ref, out_ref):
@@ -172,13 +172,31 @@
         sketch_kernel(core_ref, sketch_core_ref, sketch_ref, out_ref)
 
 
-def gram_term(out_ref, core_ref, carry, images_of, images_ref=None):
+def images_with(sketch_ref):
+    sketch, rest = read(sketch_ref)
+    return lambda built: dot(built[:, :MAIN], sketch, 1, 1) + dot(built[:, MAIN:], rest, 1, 0)
+
+
+def prepare(core_ref, product, images_of, y_ref, z_ref):
+    for i in range(core_ref.shape[0]):
+        high, low = halves(product(core_ref[i]))
+        y_ref[0, i], y_ref[1, i] = high, low
+        z_ref[0, i], z_ref[1, i] = halves(images_of(high) + images_of(low))
+
+
+def gram_term(out_ref, images_ref, inverse, y_ref, z_ref):
+    inverse_high, inverse_low = halves(inverse)
+
+    def scaled(ref, i):
+        return dot(inverse_high, ref[0, i], 1, 0) + (
+            dot(inverse_high, ref[1, i], 1, 0) + dot(inverse_low, ref[0, i], 1, 0)
+        )
+
     total = rest = None
-    for i in range(core_ref.shape[0]):
-        built = dot(carry, core_ref[i], 1, 0).astype(BF16)
-        images = images_of(built)
-        if images_ref is not None:
-            images_ref[i] = images
+    for i in range(images_ref.shape[0]):
+        built = scaled(y_ref, i).astype(BF16)
+        images = scaled(z_ref, i)
+        images_ref[i] = images
         images = images.astype(BF16)
         term = dot(images, built[:, :MAIN], 0, 0)
         end = dot(built[:, MAIN:], images, 0, 0)
@@ -186,21 +204,17 @@
     write(out_ref, total, rest)
 
 
-def images_with(sketch_ref):
-    sketch, rest = read(sketch_ref)
-    return lambda built: dot(built[:, :MAIN], sketch, 1, 1) + dot(built[:, MAIN:], rest, 1, 0)
-
-
-def project(carry_ref, m_ref, before_ref):
+def project(m_ref, before_ref, core_ref, images_of, out_ref, images_ref, y_ref, z_ref):
     main, rest = read(m_ref)
-    inverse = inverse_factor(symmetric_gram((main, rest), read(before_ref)))
-    carry_ref[:, :MAIN] = left_wide_dot(inverse, main, 1, 0).astype(BF16)
-    carry_ref[:, MAIN:] = left_wide_dot(inverse, rest, 1, 1).astype(BF16)
-
-
-def project_kernel(m_ref, before_ref, core_ref, sketch_ref, out_ref, carry_ref):
-    project(carry_ref, m_ref, before_ref)
-    gram_term(out_ref, core_ref, carry_ref[...], images_with(sketch_ref))
+    gram = symmetric_gram((main, rest), read(before_ref))
+    prepare(
+        core_ref, lambda core: dot(main, core[:MAIN], 1, 0) + dot(rest, core[MAIN:], 0, 0), images_of, y_ref, z_ref
+    )
+    gram_term(out_ref, images_ref, inverse_factor(gram), y_ref, z_ref)
+
+
+def project_kernel(m_ref, before_ref, core_ref, sketch_ref, out_ref, images_ref, y_ref, z_ref):
+    project(m_ref, before_ref, core_ref, images_with(sketch_ref), out_ref, images_ref, y_ref, z_ref)
 
 
 def m_0_gram(m_value, sketch, sketch_rest):
@@ -217,60 +231,66 @@
     return total
 
 
-def first_project_kernel(upper_ref, rest_ref, before_ref, core_ref, sketch_ref, out_ref, carry_ref, m0_ref):
+def first_project_kernel(
+    upper_ref, rest_ref, before_ref, core_ref, sketch_ref, out_ref, images_ref, m0_ref, y_ref, z_ref
+):
     s, sd = read(before_ref)
     sa, sb, sc = s[:, :128], s[:, 128:256], s[:, 256:384]
-    a = upper_ref[:, :RANK]
+
+    def mended(block):
+        wide = block.astype(F32)
+        row = lax.broadcasted_iota(jnp.int32, (128, 128), 0)
+        lane = lax.broadcasted_iota(jnp.int32, (128, 128), 1)
+        return jnp.where((row >= 64) & (lane < 64), wide.T, wide).astype(BF16)
+
+    def ends(ref, lane):
+        return jnp.concatenate([ref[64:128, lane : lane + 16], ref[64:128, lane + 16 : lane + 32]], axis=0)
+
+    a_end, b_end, c_end = ends(upper_ref, 0), ends(upper_ref, 32), ends(rest_ref, 256)
+    d_end = rest_ref[64:80, 288:304]
+    a_own = mended(upper_ref[:, :128])
+    a_far = upper_ref[:, 128:]
     b = rest_ref[:, :256]
-    c = rest_ref[:, 256:384]
-    b_end = upper_ref[:, 400:416]
-    c_end = upper_ref[:, 416:432]
-    d_end = upper_ref[:16, 432:448]
-    over_a = dot(sa, a, 1, 0)
-    m0_ref[:, :128] = over_a[:, :128] + dot(s[:, 128:], a[:, 128:MAIN], 1, 1) + dot(sd, a[:, MAIN:], 0, 1)
+    c = mended(rest_ref[:, 256:384])
+    m0_ref[:, :128] = dot(sa, a_own, 1, 0) + dot(s[:, 128:], a_far, 1, 1) + dot(sd, a_end, 0, 1)
     m0_ref[:, 128:256] = (
-        over_a[:, 128:256] + dot(sb, b[:, :128], 1, 0) + dot(sc, b[:, 128:], 1, 1) + dot(sd, b_end, 0, 1)
-    )
-    m0_ref[:, 256:384] = over_a[:, 256:384] + dot(sb, b[:, 128:], 1, 0) + dot(sc, c, 1, 0) + dot(sd, c_end, 0, 1)
-    m0_ref[:, 384:400] = over_a[:, 384:400] + dot(sb, b_end, 1, 0) + dot(sc, c_end, 1, 0) + dot(sd, d_end, 0, 0)
+        dot(sa, a_far[:, :128], 1, 0) + dot(sb, b[:, :128], 1, 0) + dot(sc, b[:, 128:], 1, 1) + dot(sd, b_end, 0, 1)
+    )
+    m0_ref[:, 256:384] = (
+        dot(sa, a_far[:, 128:], 1, 0) + dot(sb, b[:, 128:], 1, 0) + dot(sc, c, 1, 0) + dot(sd, c_end, 0, 1)
+    )
+    m0_ref[:, 384:] = dot(sa, a_end, 1, 0) + dot(sb, b_end, 1, 0) + dot(sc, c_end, 1, 0) + dot(sd, d_end, 0, 0)
     m_value = m0_ref[...]
-    inverse = inverse_factor(m_0_gram(m_value, s, sd))
-    carry = wide_dot(inverse, m_value, 1, 0).astype(BF16)
-    carry_ref[...] = carry
-    gram_term(out_ref, core_ref, carry, images_with(sketch_ref))
+    gram = m_0_gram(m_value, s, sd)
+    high, low = halves(m_value)
+    prepare(
+        core_ref, lambda core: dot(high, core, 1, 0) + dot(low, core, 1, 0), images_with(sketch_ref), y_ref, z_ref
+    )
+    gram_term(out_ref, images_ref, inverse_factor(gram), y_ref, z_ref)
 
 
 def last_project_kernel(
-    x_ref, m_ref, before_ref, core_ref, right_ref, left_ref, carry_1_ref, carry_2_ref,
-    third_ref, second_ref, first_ref, out_ref, images_ref, carry_ref,
+    x_ref, m_ref, before_ref, core_ref, right_ref, left_ref, third_ref, out_ref, images_ref, y_ref, z_ref
 ):
     @pl.when(x_ref[0] == 3)
     def _():
-        project(carry_ref, m_ref, before_ref)
-        gram_term(out_ref, core_ref, carry_ref[...], lambda built: dot(built, right_ref[...], 1, 0), images_ref)
-
-    def only_images(carry, dim, sketch_ref):
+        project(
+            m_ref, before_ref, core_ref, lambda built: dot(built, right_ref[...], 1, 0), out_ref, images_ref,
+            y_ref, z_ref,
+        )
+
+    @pl.when(x_ref[0] != 3)
+    def _():
         out_ref[...] = jnp.zeros(out_ref.shape, BF16)
-        images_of = images_with(sketch_ref)
+        images_of = images_with(third_ref)
+        left_t = left_ref[...].astype(BF16)
         for i in range(core_ref.shape[0]):
-            images_ref[i] = images_of(dot(carry, core_ref[i], dim, 0).astype(BF16))
-
-    @pl.when(x_ref[0] == 2)
-    def _():
-        only_images(carry_2_ref[...], 1, first_ref)
-
-    @pl.when(x_ref[0] == 1)
-    def _():
-        only_images(carry_1_ref[...], 1, second_ref)
-
-    @pl.when(x_ref[0] == 0)
-    def _():
-        only_images(left_ref[...].astype(BF16), 0, third_ref)
+            images_ref[i] = images_of(dot(left_t, core_ref[i], 0, 0).astype(BF16))
 
 
 def final_kernel(
     scale, x_ref, m_0_ref, m_1_ref, m_2_ref, m_3_ref, third_ref, second_ref, first_ref, right_ref,
-    images_ref, frames_ref, interface_ref, main_ref, rest_ref, gram_ref,
+    images_1_ref, images_2_ref, images_0_ref, frames_ref, interface_ref, main_ref, rest_ref, gram_ref, images_ref,
 ):
     def take(m_ref):
         main, rest = read(m_ref)
@@ -283,18 +303,22 @@
         m_value = m_0_ref[...]
         main_ref[...] = m_value[:, :MAIN]
         rest_ref[...] = m_value[:, MAIN:].T
+        images_ref[...] = images_0_ref[...]
         gram_ref[...] = m_0_gram(m_value, *read(third_ref))
 
     @pl.when(x_ref[0] == 1)
     def _():
+        images_ref[...] = images_1_ref[...]
         gram_ref[...] = symmetric_gram(take(m_1_ref), read(second_ref))
 
     @pl.when(x_ref[0] == 2)
     def _():
+        images_ref[...] = images_2_ref[...]
         gram_ref[...] = symmetric_gram(take(m_2_ref), read(first_ref))
 
     @pl.when(x_ref[0] == 3)
     def _():
+        images_ref[...] = images_0_ref[...]
         main, rest = take(m_3_ref)
         right, right_rest = right_ref[:MAIN], right_ref[MAIN:]
         gram_ref[...] = 0.5 * (
@@ -305,8 +329,7 @@
     interface_ref[:, 0, :MAIN] = wide_dot(inverse, main_ref[...], 1, 0)
     interface_ref[:, 0, MAIN:] = wide_dot(inverse, rest_ref[...], 1, 1)
     for i in range(images_ref.shape[0]):
-        orth = wide_dot(images_ref[i], inverse, 1, 1)
-        frames_ref[:, i, :] = (orth * scale).astype(BF16)
+        frames_ref[:, i, :] = (wide_dot(images_ref[i], inverse, 1, 1) * scale).astype(BF16)
 
 
 def call(kernel, *operands, out, scalar=False, scratch=()):
@@ -324,7 +347,6 @@
     )(*operands)
 
 
-WIDE = ((ROWS, LANES), BF16)
 PAYLOAD = ((ROWS, MAIN), BF16)
 
 
@@ -395,7 +417,7 @@
     left_t = left_interface.T
 
     term, rest = call(
-        first_kernel, plane_ref, core, sketch_core, right_sketch, left_t, out=[WIDE, PAYLOAD], scalar=True
+        first_kernel, plane_ref, core, sketch_core, right_sketch, left_t, out=[PAYLOAD, PAYLOAD], scalar=True
     )
     first = whole_pair(plane_sum(term, (3, 0)), ((3, 2), (0, 1)))[0]
     (term,) = call(sketch_kernel, core, sketch_core, first, out=[PAYLOAD])
@@ -403,17 +425,18 @@
     (term,) = call(last_sketch_kernel, plane_ref, core, sketch_core, second, rest, out=[PAYLOAD], scalar=True)
     third, rest = whole_pair(plane_sum(term, (1, 0)), ((1, 0),))
 
-    carry_kind = ((SKETCH, RANK), BF16)
-    term, carry_1, m_0 = call(
-        first_project_kernel, first, rest, third, core, second, out=[PAYLOAD, carry_kind, ((SKETCH, RANK), F32)]
+    images_kind = ((modes, SKETCH, SKETCH), F32)
+    kept = [((2, modes, SKETCH, RANK), BF16), ((2, modes, SKETCH, SKETCH), BF16)]
+    term, images_1, m_0 = call(
+        first_project_kernel, first, rest, third, core, second,
+        out=[PAYLOAD, images_kind, ((SKETCH, RANK), F32)], scratch=kept,
     )
     m_1 = whole_pair(plane_sum(term, (1,)), ((1, 2),))[0]
-    term, carry_2 = call(project_kernel, m_1, second, core, first, out=[PAYLOAD, carry_kind])
+    term, images_2 = call(project_kernel, m_1, second, core, first, out=[PAYLOAD, images_kind], scratch=kept)
     m_2 = whole_pair(plane_sum(term, (2,)), ((2, 3),))[0]
     term, images = call(
-        last_project_kernel, plane_ref, m_2, first, core, right_sketch, left_t, carry_1, carry_2,
-        third, second, first, out=[PAYLOAD, ((modes, SKETCH, SKETCH), F32)], scalar=True,
-        scratch=[((SKETCH, RANK), BF16)],
+        last_project_kernel, plane_ref, m_2, first, core, right_sketch, left_t, third,
+        out=[PAYLOAD, images_kind], scalar=True, scratch=kept,
     )
     m_3 = everywhere(plane_sum(term, (3,)), NEAR_GROUPS).reshape(ROWS, -1)
 
@@ -421,9 +444,10 @@
         final_kernel(frame_scale, *refs)
 
     frames, interface = call(
-        finish, plane_ref, m_0, m_1, m_2, m_3, third, second, first, right_sketch, images,
+        finish, plane_ref, m_0, m_1, m_2, m_3, third, second, first, right_sketch,
+        images_1, images_2, images,
         out=[((SKETCH, modes, SKETCH), BF16), ((SKETCH, 1, RANK), F32)], scalar=True,
-        scratch=[((SKETCH, MAIN), F32), ((RANK - MAIN, SKETCH), F32), ((SKETCH, SKETCH), F32)],
+        scratch=[((SKETCH, MAIN), F32), ((RANK - MAIN, SKETCH), F32), ((SKETCH, SKETCH), F32), images_kind],
     )
     return (frames[None], interface.reshape(1, SKETCH, RANK))
 

time: 252 us -> 249 us (0.988)
  no operation moved by 1% of the time
where the time goes in v9:
time: 249 us; the launch traced here: 248 us
  blocking collectives  220 us (88%)
  Pallas kernels  24 us (10%)
  local copies, waits for them, and re-layouts  2.92 us (1%)
    all_to_all x18, blocking collectives, exchanged(): lax.all_to_all(tiles, AXES, 0, 0, axis_index_groups=groups, tiled=True)  220 us
    pallas_call x7, Pallas kernels, call(): pl.pallas_call(kernel, out_shape=outs, in_specs=specs, out_specs=[pl.Bloc...  24 us

profile of v9, /device:TPU:7, one launch (start us, length us, event | category | flops | bytes accessed | tf_op | source)
XLA Modules:
  0.0 248.3 jit_solution(5475759522388592074)
XLA Ops:
  1.6 1.8 copy.12
  4.7 12.2 %all_to_all.90 = bf16[16,8,384]{2,1,0:T(8,128)(2,1)S(1)} all-to-all(bf16[16,8,384]{2,1,0:T(8,128)(2,1)S(1)} %bitcast.49), channel_id=1, replica_groups={{0,4,8,12,128,132,136,140,256,260,264,268,384,388,392,396},{16,20,24,28..., dimensions={0} | all-to-all | bytes 196608 | tf_op jit(solution)/shard_map/all_to_all | solution.py:389
  16.9 25.5 %all_to_all.91 = bf16[8,8,384]{2,1,0:T(8,128)(2,1)S(1)} all-to-all(bf16[8,8,384]{2,1,0:T(8,128)(2,1)S(1)} %broadcast_in_dim.39), channel_id=1, replica_groups={{3,19,35,51,79,95,111,127},{7,23,39,55,75,91,107,123},{11,27,43,59,71,8..., dimensions={0} | all-to-all | bytes 98304 | tf_op jit(solution)/shard_map/all_to_all | solution.py:389
  42.5 10.3 %all_to_all.92 = bf16[32,8,384]{2,1,0:T(8,128)(2,1)S(1)} all-to-all(bf16[32,8,384]{2,1,0:T(8,128)(2,1)S(1)} %broadcast_in_dim.40), channel_id=1, replica_groups={{3,7,11,15,131,135,139,143,259,263,267,271,387,391,395,399,2,6,10,14,13..., dimensions={0} | all-to-all | bytes 393216 | tf_op jit(solution)/shard_map/all_to_all | solution.py:389
  54.4 8.9 %all_to_all.93 = bf16[16,8,384]{2,1,0:T(8,128)(2,1)S(1)} all-to-all(bf16[16,8,384]{2,1,0:T(8,128)(2,1)S(1)} %bitcast.46), channel_id=1, replica_groups={{0,4,8,12,128,132,136,140,256,260,264,268,384,388,392,396},{16,20,24,28..., dimensions={0} | all-to-all | bytes 196608 | tf_op jit(solution)/shard_map/all_to_all | solution.py:389
  63.4 7.7 %all_to_all.94 = bf16[8,8,384]{2,1,0:T(8,128)(2,1)S(1)} all-to-all(bf16[8,8,384]{2,1,0:T(8,128)(2,1)S(1)} %broadcast_in_dim.41), channel_id=1, replica_groups={{2,18,34,50,78,94,110,126},{6,22,38,54,74,90,106,122},{10,26,42,58,70,8..., dimensions={0} | all-to-all | bytes 98304 | tf_op jit(solution)/shard_map/all_to_all | solution.py:389
  71.2 13.6 %all_to_all.95 = bf16[32,8,384]{2,1,0:T(8,128)(2,1)S(1)} all-to-all(bf16[32,8,384]{2,1,0:T(8,128)(2,1)S(1)} %broadcast_in_dim.42), channel_id=1, replica_groups={{2,6,10,14,130,134,138,142,258,262,266,270,386,390,394,398,1,5,9,13,129..., dimensions={0} | all-to-all | bytes 393216 | tf_op jit(solution)/shard_map/all_to_all | solution.py:389
  84.8 1.6 shard_map.61
  86.4 9.3 %all_to_all.96 = bf16[16,8,384]{2,1,0:T(8,128)(2,1)S(1)} all-to-all(bf16[16,8,384]{2,1,0:T(8,128)(2,1)S(1)} %bitcast.44), channel_id=1, replica_groups={{0,4,8,12,128,132,136,140,256,260,264,268,384,388,392,396},{16,20,24,28..., dimensions={0} | all-to-all | bytes 196608 | tf_op jit(solution)/shard_map/all_to_all | solution.py:389
  95.8 7.7 %all_to_all.97 = bf16[8,8,384]{2,1,0:T(8,128)(2,1)S(1)} all-to-all(bf16[8,8,384]{2,1,0:T(8,128)(2,1)S(1)} %broadcast_in_dim.43), channel_id=1, replica_groups={{1,17,33,49,77,93,109,125},{5,21,37,53,73,89,105,121},{9,25,41,57,69,85..., dimensions={0} | all-to-all | bytes 98304 | tf_op jit(solution)/shard_map/all_to_all | solution.py:389
  103.6 13.0 %all_to_all.98 = bf16[32,8,384]{2,1,0:T(8,128)(2,1)S(1)} all-to-all(bf16[32,8,384]{2,1,0:T(8,128)(2,1)S(1)} %broadcast_in_dim.44), channel_id=1, replica_groups={{1,5,9,13,129,133,137,141,257,261,265,269,385,389,393,397,0,4,8,12,128,..., dimensions={0} | all-to-all | bytes 393216 | tf_op jit(solution)/shard_map/all_to_all | solution.py:389
  116.6 5.2 %shard_map.62 = (bf16[128,384]{1,0:T(8,128)(2,1)S(1)}, f32[4,100,100]{2,1,0:T(8,128)S(1)}, f32[100,400]{1,0:T(8,128)S(1)}) custom-call(bf16[128,384]{1,0:T(8,128)(2,1)S(1)} %slice_bitcast_fusion.5.sketch_ref.upper_ref.before_ref.refs_7_, bf16[128,384]{1,0:T(8,128)(2,1)S(1)} %get-tuple-element.25.rest_ref, ...), custom_call_target="tpu_custom_call" | custom-call | tf_op jit(solution)/shard_map/pallas_call | solution.py:340
  121.8 9.3 %all_to_all.99 = bf16[16,8,384]{2,1,0:T(8,128)(2,1)S(1)} all-to-all(bf16[16,8,384]{2,1,0:T(8,128)(2,1)S(1)} %bitcast.47), channel_id=1, replica_groups={{0,4,8,12,128,132,136,140,256,260,264,268,384,388,392,396},{16,20,24,28..., dimensions={0} | all-to-all | bytes 196608 | tf_op jit(solution)/shard_map/all_to_all | solution.py:389
  131.2 7.7 %all_to_all.100 = bf16[8,8,384]{2,1,0:T(8,128)(2,1)S(1)} all-to-all(bf16[8,8,384]{2,1,0:T(8,128)(2,1)S(1)} %broadcast_in_dim.45), channel_id=1, replica_groups={{1,17,33,49,77,93,109,125},{5,21,37,53,73,89,105,121},{9,25,41,57,69,85..., dimensions={0} | all-to-all | bytes 98304 | tf_op jit(solution)/shard_map/all_to_all | solution.py:389
  139.0 13.0 %all_to_all.101 = bf16[32,8,384]{2,1,0:T(8,128)(2,1)S(1)} all-to-all(bf16[32,8,384]{2,1,0:T(8,128)(2,1)S(1)} %broadcast_in_dim.46), channel_id=1, replica_groups={{1,5,9,13,129,133,137,141,257,261,265,269,385,389,393,397,2,6,10,14,130..., dimensions={0} | all-to-all | bytes 393216 | tf_op jit(solution)/shard_map/all_to_all | solution.py:389
  152.0 4.8 %shard_map.63 = (bf16[128,384]{1,0:T(8,128)(2,1)S(1)}, f32[4,100,100]{2,1,0:T(8,128)S(1)}) custom-call(bf16[128,384]{1,0:T(8,128)(2,1)S(1)} %slice_bitcast_fusion.1.m_ref.refs_2_, bf16[128,384]{1,0:T(8,128)(2,1)S(1)} %slice_bitcast_fusion.4.sketch_ref.before_ref.refs_6_, bf16[4,400,400]{2,1,0:T(8,128)(2,1)S(1)} %bitcast.37, ...), custom_call_target="tpu_custom_call" | custom-call | tf_op jit(solution)/shard_map/pallas_call | solution.py:340
  156.8 9.3 %all_to_all.102 = bf16[16,8,384]{2,1,0:T(8,128)(2,1)S(1)} all-to-all(bf16[16,8,384]{2,1,0:T(8,128)(2,1)S(1)} %bitcast.50), channel_id=1, replica_groups={{0,4,8,12,128,132,136,140,256,260,264,268,384,388,392,396},{16,20,24,28..., dimensions={0} | all-to-all | bytes 196608 | tf_op jit(solution)/shard_map/all_to_all | solution.py:389
  166.1 7.7 %all_to_all.103 = bf16[8,8,384]{2,1,0:T(8,128)(2,1)S(1)} all-to-all(bf16[8,8,384]{2,1,0:T(8,128)(2,1)S(1)} %broadcast_in_dim.47), channel_id=1, replica_groups={{2,18,34,50,78,94,110,126},{6,22,38,54,74,90,106,122},{10,26,42,58,70,8..., dimensions={0} | all-to-all | bytes 98304 | tf_op jit(solution)/shard_map/all_to_all | solution.py:389
  173.9 31.7 %all_to_all.104 = bf16[32,8,384]{2,1,0:T(8,128)(2,1)S(1)} all-to-all(bf16[32,8,384]{2,1,0:T(8,128)(2,1)S(1)} %broadcast_in_dim.48), channel_id=1, replica_groups={{2,6,10,14,130,134,138,142,258,262,266,270,386,390,394,398,3,7,11,15,13..., dimensions={0} | all-to-all | bytes 393216 | tf_op jit(solution)/shard_map/all_to_all | solution.py:389
  205.6 4.8 %shard_map.64 = (bf16[128,384]{1,0:T(8,128)(2,1)S(1)}, f32[4,100,100]{2,1,0:T(8,128)S(1)}) custom-call(s32[1]{0:T(128)} %bitcast.x_ref.refs_0_, bf16[128,384]{1,0:T(8,128)(2,1)S(1)} %slice_bitcast_fusion.m_ref.refs_3_, bf16[128,384]{1,0:T(8,128)(2,1)S(1)} %slice_bitcast_fusion.5.sketch_ref.upper_ref.before_ref.refs_7_, bf16[4,400,400]{2,1,0:T(8,128)(2,1)S(1)} %bitcast.38, ...), custom_call_target="tpu_custom_call" | custom-call | tf_op jit(solution)/shard_map/pallas_call | solution.py:340
  210.4 9.0 %all_to_all.105 = bf16[16,8,384]{2,1,0:T(8,128)(2,1)S(1)} all-to-all(bf16[16,8,384]{2,1,0:T(8,128)(2,1)S(1)} %bitcast.48), channel_id=1, replica_groups={{0,4,8,12,128,132,136,140,256,260,264,268,384,388,392,396},{16,20,24,28..., dimensions={0} | all-to-all | bytes 196608 | tf_op jit(solution)/shard_map/all_to_all | solution.py:389
  219.4 15.5 %all_to_all.106 = bf16[8,8,384]{2,1,0:T(8,128)(2,1)S(1)} all-to-all(bf16[8,8,384]{2,1,0:T(8,128)(2,1)S(1)} %broadcast_in_dim.49), channel_id=1, replica_groups={{3,19,35,51,79,95,111,127},{7,23,39,55,75,91,107,123},{11,27,43,59,71,8..., dimensions={0} | all-to-all | bytes 98304 | tf_op jit(solution)/shard_map/all_to_all | solution.py:389
  234.9 8.7 %all_to_all.107 = bf16[16,8,384]{2,1,0:T(8,128)(2,1)S(1)} all-to-all(bf16[16,8,384]{2,1,0:T(8,128)(2,1)S(1)} %broadcast_in_dim.50), channel_id=1, replica_groups={{0,4,8,12,128,132,136,140,256,260,264,268,384,388,392,396},{16,20,24,28..., dimensions={0} | all-to-all | bytes 196608 | tf_op jit(solution)/shard_map/all_to_all | solution.py:389
  243.6 4.7 %shard_map.65 = (bf16[100,4,100]{2,1,0:T(4,128)(2,1)}, f32[100,1,400]{2,1,0:T(1,128)}) custom-call(s32[1]{0:T(128)} %bitcast.x_ref.refs_0_, f32[100,400]{1,0:T(8,128)S(1)} %get-tuple-element.15.refs_1_, bf16[128,384]{1,0:T(8,128)(2,1)S(1)} %slice_bitcast_fusion.1.m_ref.refs_2_, bf16[128,384]{1,0:T(8,128)(2,1)S(1)} %slice_bitcast_fusion.m_ref.refs_3_, ...), custom_call_target="tpu_custom_call" | custom-call | tf_op jit(solution)/shard_map/pallas_call | solution.py:340
  (36 shorter events, 4.2 us)
Async XLA Ops:
  1.5 1.8 copy-start
  1.6 1.8 copy-start.1

commit v10 on v9

--- a/solution.py
+++ b/solution.py
@@ -33,8 +33,9 @@
     tiles = [padded[8 * t : 8 * t + 8] for t in range(count)]
     lane = lax.broadcasted_iota(jnp.int32, (8, 128), 1)
     sub = lax.broadcasted_iota(jnp.int32, (8, 128), 0)
-
     none = jnp.where(lane >= 128, 1.0, 0.0)
+    even = sub % 2 == 0
+    start = sub - sub % 2
 
     def column(tile, j):
         return jnp.broadcast_to(tile[:, j : j + 1], (8, 128))
@@ -48,34 +49,48 @@
         step = lane - base
         columns = {t: [column(tiles[t], base + c) for c in range(width)] for t in range(own, count)}
         head = [value + none for value in columns[own]]
-        scales, leads = [], []
+        solves, leads = [], []
         tile = tiles[own]
-        for s in range(width):
-            scales.append(line(1.0 / head[s], s))
-            leads.append([line(head[c], s) if c > s else None for c in range(width)])
-            factor = jnp.where(sub > s, head[s] * scales[s], 0.0)
-            pivot = jnp.where(step == s, 1.0, line(tile, s))
-            tile = jnp.where((step == s) & (sub > s), 0.0, tile) - factor * pivot
-            for c in range(s + 1, width):
-                head[c] = head[c] - factor * leads[s][c]
+        for s in range(0, width, 2):
+            a, b, c = line(head[s], s), line(head[s + 1], s), line(head[s + 1], s + 1)
+            scale = 1.0 / (a * c - b * b)
+            solve = (a * scale, b * scale, c * scale)
+            solves.append(solve)
+            leads.append([(line(head[k], s), line(head[k], s + 1)) if k > s + 1 else None for k in range(width)])
+            if s + 2 < width:
+                below = sub > s + 1
+                first = jnp.where(below, head[s] * solve[2] - head[s + 1] * solve[1], 0.0)
+                second = jnp.where(below, head[s + 1] * solve[0] - head[s] * solve[1], 0.0)
+                pair = (step == s) | (step == s + 1)
+                top = jnp.where(pair, jnp.where(step == s, 1.0, 0.0), line(tile, s))
+                low = jnp.where(pair, jnp.where(step == s + 1, 1.0, 0.0), line(tile, s + 1))
+                tile = jnp.where(pair & below, 0.0, tile) - first * top - second * low
+                for k in range(s + 2, width):
+                    head[k] = head[k] - first * leads[-1][k][0] - second * leads[-1][k][1]
         tiles[own] = tile
-        reduced = jnp.where((step > sub) & (step < 8), 0.0, jnp.where(step == sub, 1.0, tile))
+        reduced = jnp.where((step >= start) & (step < 8), jnp.where(step == sub, 1.0, 0.0), tile)
         pivots = [line(reduced, s) for s in range(width)]
         for t in range(own + 1, count):
             col = columns[t]
             new = jnp.where((step >= 0) & (step < 8), 0.0, tiles[t])
-            for s in range(width):
-                factor = col[s] * scales[s]
-                new = new - factor * pivots[s]
-                for c in range(s + 1, width):
-                    col[c] = col[c] - factor * leads[s][c]
+            for s in range(0, width, 2):
+                a, b, c = solves[s // 2]
+                first = col[s] * c - col[s + 1] * b
+                second = col[s + 1] * a - col[s] * b
+                new = new - first * pivots[s] - second * pivots[s + 1]
+                for k in range(s + 2, width):
+                    col[k] = col[k] - first * leads[s // 2][k][0] - second * leads[s // 2][k][1]
             tiles[t] = new
     done = []
     for t in range(count):
         row = sub + 8 * t
-        diagonal = jnp.sum(jnp.where(lane == row, tiles[t], 0.0), axis=1, keepdims=True)
-        lower = jnp.where(lane < row, tiles[t], jnp.where(lane == row, 1.0, 0.0))
-        done.append(lower * lax.rsqrt(diagonal))
+        tile = tiles[t]
+        diagonal = jnp.sum(jnp.where(lane == row, tile, 0.0), axis=1, keepdims=True)
+        side = jnp.sum(jnp.where((lane == row - 1) & ~even, tile, 0.0), axis=1, keepdims=True)
+        lower = jnp.where(lane < start + 8 * t, tile, jnp.where(lane == row, 1.0, 0.0))
+        ratio = jnp.where(even[:, :1], 0.0, side / jnp.concatenate([diagonal[-1:], diagonal[:-1]], axis=0))
+        above = jnp.concatenate([lower[-1:], lower[:-1]], axis=0)
+        done.append((lower - ratio * above) * lax.rsqrt(diagonal - ratio * side))
     return jnp.concatenate(done, axis=0)[:size, :size]
 
 

time: 249 us -> 246 us (0.988)
  Pallas kernels: 24 us -> 21 us
    pallas_call x7, Pallas kernels: 24 us -> 21 us  [call(): pl.pallas_call(kernel, out_shape=outs, in_specs=specs, out_specs=[pl.Bloc...]
where the time goes in v10:
time: 246 us; the launch traced here: 245 us
  blocking collectives  220 us (89%)
  Pallas kernels  21 us (9%)
  local copies, waits for them, and re-layouts  2.92 us (1%)
    all_to_all x18, blocking collectives, exchanged(): lax.all_to_all(tiles, AXES, 0, 0, axis_index_groups=groups, tiled=True)  220 us
    pallas_call x7, Pallas kernels, call(): pl.pallas_call(kernel, out_shape=outs, in_specs=specs, out_specs=[pl.Bloc...  21 us

profile of v10, /device:TPU:7, one launch (start us, length us, event | category | flops | bytes accessed | tf_op | source)
XLA Modules:
  0.0 245.4 jit_solution(3155576412916572412)
XLA Ops:
  1.6 1.8 copy.12
  4.7 12.2 %all_to_all.90 = bf16[16,8,384]{2,1,0:T(8,128)(2,1)S(1)} all-to-all(bf16[16,8,384]{2,1,0:T(8,128)(2,1)S(1)} %bitcast.49), channel_id=1, replica_groups={{0,4,8,12,128,132,136,140,256,260,264,268,384,388,392,396},{16,20,24,28..., dimensions={0} | all-to-all | bytes 196608 | tf_op jit(solution)/shard_map/all_to_all | solution.py:404
  16.9 25.5 %all_to_all.91 = bf16[8,8,384]{2,1,0:T(8,128)(2,1)S(1)} all-to-all(bf16[8,8,384]{2,1,0:T(8,128)(2,1)S(1)} %broadcast_in_dim.39), channel_id=1, replica_groups={{3,19,35,51,79,95,111,127},{7,23,39,55,75,91,107,123},{11,27,43,59,71,8..., dimensions={0} | all-to-all | bytes 98304 | tf_op jit(solution)/shard_map/all_to_all | solution.py:404
  42.5 10.3 %all_to_all.92 = bf16[32,8,384]{2,1,0:T(8,128)(2,1)S(1)} all-to-all(bf16[32,8,384]{2,1,0:T(8,128)(2,1)S(1)} %broadcast_in_dim.40), channel_id=1, replica_groups={{3,7,11,15,131,135,139,143,259,263,267,271,387,391,395,399,2,6,10,14,13..., dimensions={0} | all-to-all | bytes 393216 | tf_op jit(solution)/shard_map/all_to_all | solution.py:404
  54.4 8.9 %all_to_all.93 = bf16[16,8,384]{2,1,0:T(8,128)(2,1)S(1)} all-to-all(bf16[16,8,384]{2,1,0:T(8,128)(2,1)S(1)} %bitcast.46), channel_id=1, replica_groups={{0,4,8,12,128,132,136,140,256,260,264,268,384,388,392,396},{16,20,24,28..., dimensions={0} | all-to-all | bytes 196608 | tf_op jit(solution)/shard_map/all_to_all | solution.py:404
  63.4 7.7 %all_to_all.94 = bf16[8,8,384]{2,1,0:T(8,128)(2,1)S(1)} all-to-all(bf16[8,8,384]{2,1,0:T(8,128)(2,1)S(1)} %broadcast_in_dim.41), channel_id=1, replica_groups={{2,18,34,50,78,94,110,126},{6,22,38,54,74,90,106,122},{10,26,42,58,70,8..., dimensions={0} | all-to-all | bytes 98304 | tf_op jit(solution)/shard_map/all_to_all | solution.py:404
  71.2 13.6 %all_to_all.95 = bf16[32,8,384]{2,1,0:T(8,128)(2,1)S(1)} all-to-all(bf16[32,8,384]{2,1,0:T(8,128)(2,1)S(1)} %broadcast_in_dim.42), channel_id=1, replica_groups={{2,6,10,14,130,134,138,142,258,262,266,270,386,390,394,398,1,5,9,13,129..., dimensions={0} | all-to-all | bytes 393216 | tf_op jit(solution)/shard_map/all_to_all | solution.py:404
  84.8 1.6 shard_map.61
  86.4 9.3 %all_to_all.96 = bf16[16,8,384]{2,1,0:T(8,128)(2,1)S(1)} all-to-all(bf16[16,8,384]{2,1,0:T(8,128)(2,1)S(1)} %bitcast.44), channel_id=1, replica_groups={{0,4,8,12,128,132,136,140,256,260,264,268,384,388,392,396},{16,20,24,28..., dimensions={0} | all-to-all | bytes 196608 | tf_op jit(solution)/shard_map/all_to_all | solution.py:404
  95.8 7.7 %all_to_all.97 = bf16[8,8,384]{2,1,0:T(8,128)(2,1)S(1)} all-to-all(bf16[8,8,384]{2,1,0:T(8,128)(2,1)S(1)} %broadcast_in_dim.43), channel_id=1, replica_groups={{1,17,33,49,77,93,109,125},{5,21,37,53,73,89,105,121},{9,25,41,57,69,85..., dimensions={0} | all-to-all | bytes 98304 | tf_op jit(solution)/shard_map/all_to_all | solution.py:404
  103.6 13.0 %all_to_all.98 = bf16[32,8,384]{2,1,0:T(8,128)(2,1)S(1)} all-to-all(bf16[32,8,384]{2,1,0:T(8,128)(2,1)S(1)} %broadcast_in_dim.44), channel_id=1, replica_groups={{1,5,9,13,129,133,137,141,257,261,265,269,385,389,393,397,0,4,8,12,128,..., dimensions={0} | all-to-all | bytes 393216 | tf_op jit(solution)/shard_map/all_to_all | solution.py:404
  116.6 4.7 %shard_map.62 = (bf16[128,384]{1,0:T(8,128)(2,1)S(1)}, f32[4,100,100]{2,1,0:T(8,128)S(1)}, f32[100,400]{1,0:T(8,128)S(1)}) custom-call(bf16[128,384]{1,0:T(8,128)(2,1)S(1)} %slice_bitcast_fusion.5.sketch_ref.upper_ref.before_ref.refs_7_, bf16[128,384]{1,0:T(8,128)(2,1)S(1)} %get-tuple-element.25.rest_ref, ...), custom_call_target="tpu_custom_call" | custom-call | tf_op jit(solution)/shard_map/pallas_call | solution.py:355
  121.3 9.3 %all_to_all.99 = bf16[16,8,384]{2,1,0:T(8,128)(2,1)S(1)} all-to-all(bf16[16,8,384]{2,1,0:T(8,128)(2,1)S(1)} %bitcast.47), channel_id=1, replica_groups={{0,4,8,12,128,132,136,140,256,260,264,268,384,388,392,396},{16,20,24,28..., dimensions={0} | all-to-all | bytes 196608 | tf_op jit(solution)/shard_map/all_to_all | solution.py:404
  130.7 7.7 %all_to_all.100 = bf16[8,8,384]{2,1,0:T(8,128)(2,1)S(1)} all-to-all(bf16[8,8,384]{2,1,0:T(8,128)(2,1)S(1)} %broadcast_in_dim.45), channel_id=1, replica_groups={{1,17,33,49,77,93,109,125},{5,21,37,53,73,89,105,121},{9,25,41,57,69,85..., dimensions={0} | all-to-all | bytes 98304 | tf_op jit(solution)/shard_map/all_to_all | solution.py:404
  138.4 13.0 %all_to_all.101 = bf16[32,8,384]{2,1,0:T(8,128)(2,1)S(1)} all-to-all(bf16[32,8,384]{2,1,0:T(8,128)(2,1)S(1)} %broadcast_in_dim.46), channel_id=1, replica_groups={{1,5,9,13,129,133,137,141,257,261,265,269,385,389,393,397,2,6,10,14,130..., dimensions={0} | all-to-all | bytes 393216 | tf_op jit(solution)/shard_map/all_to_all | solution.py:404
  151.5 4.1 %shard_map.63 = (bf16[128,384]{1,0:T(8,128)(2,1)S(1)}, f32[4,100,100]{2,1,0:T(8,128)S(1)}) custom-call(bf16[128,384]{1,0:T(8,128)(2,1)S(1)} %slice_bitcast_fusion.1.m_ref.refs_2_, bf16[128,384]{1,0:T(8,128)(2,1)S(1)} %slice_bitcast_fusion.4.sketch_ref.before_ref.refs_6_, bf16[4,400,400]{2,1,0:T(8,128)(2,1)S(1)} %bitcast.37, ...), custom_call_target="tpu_custom_call" | custom-call | tf_op jit(solution)/shard_map/pallas_call | solution.py:355
  155.5 9.3 %all_to_all.102 = bf16[16,8,384]{2,1,0:T(8,128)(2,1)S(1)} all-to-all(bf16[16,8,384]{2,1,0:T(8,128)(2,1)S(1)} %bitcast.50), channel_id=1, replica_groups={{0,4,8,12,128,132,136,140,256,260,264,268,384,388,392,396},{16,20,24,28..., dimensions={0} | all-to-all | bytes 196608 | tf_op jit(solution)/shard_map/all_to_all | solution.py:404
  164.9 7.7 %all_to_all.103 = bf16[8,8,384]{2,1,0:T(8,128)(2,1)S(1)} all-to-all(bf16[8,8,384]{2,1,0:T(8,128)(2,1)S(1)} %broadcast_in_dim.47), channel_id=1, replica_groups={{2,18,34,50,78,94,110,126},{6,22,38,54,74,90,106,122},{10,26,42,58,70,8..., dimensions={0} | all-to-all | bytes 98304 | tf_op jit(solution)/shard_map/all_to_all | solution.py:404
  172.7 31.7 %all_to_all.104 = bf16[32,8,384]{2,1,0:T(8,128)(2,1)S(1)} all-to-all(bf16[32,8,384]{2,1,0:T(8,128)(2,1)S(1)} %broadcast_in_dim.48), channel_id=1, replica_groups={{2,6,10,14,130,134,138,142,258,262,266,270,386,390,394,398,3,7,11,15,13..., dimensions={0} | all-to-all | bytes 393216 | tf_op jit(solution)/shard_map/all_to_all | solution.py:404
  204.4 4.0 %shard_map.64 = (bf16[128,384]{1,0:T(8,128)(2,1)S(1)}, f32[4,100,100]{2,1,0:T(8,128)S(1)}) custom-call(s32[1]{0:T(128)} %bitcast.x_ref.refs_0_, bf16[128,384]{1,0:T(8,128)(2,1)S(1)} %slice_bitcast_fusion.m_ref.refs_3_, bf16[128,384]{1,0:T(8,128)(2,1)S(1)} %slice_bitcast_fusion.5.sketch_ref.upper_ref.before_ref.refs_7_, bf16[4,400,400]{2,1,0:T(8,128)(2,1)S(1)} %bitcast.38, ...), custom_call_target="tpu_custom_call" | custom-call | tf_op jit(solution)/shard_map/pallas_call | solution.py:355
  208.4 9.0 %all_to_all.105 = bf16[16,8,384]{2,1,0:T(8,128)(2,1)S(1)} all-to-all(bf16[16,8,384]{2,1,0:T(8,128)(2,1)S(1)} %bitcast.48), channel_id=1, replica_groups={{0,4,8,12,128,132,136,140,256,260,264,268,384,388,392,396},{16,20,24,28..., dimensions={0} | all-to-all | bytes 196608 | tf_op jit(solution)/shard_map/all_to_all | solution.py:404
  217.4 15.5 %all_to_all.106 = bf16[8,8,384]{2,1,0:T(8,128)(2,1)S(1)} all-to-all(bf16[8,8,384]{2,1,0:T(8,128)(2,1)S(1)} %broadcast_in_dim.49), channel_id=1, replica_groups={{3,19,35,51,79,95,111,127},{7,23,39,55,75,91,107,123},{11,27,43,59,71,8..., dimensions={0} | all-to-all | bytes 98304 | tf_op jit(solution)/shard_map/all_to_all | solution.py:404
  233.0 8.7 %all_to_all.107 = bf16[16,8,384]{2,1,0:T(8,128)(2,1)S(1)} all-to-all(bf16[16,8,384]{2,1,0:T(8,128)(2,1)S(1)} %broadcast_in_dim.50), channel_id=1, replica_groups={{0,4,8,12,128,132,136,140,256,260,264,268,384,388,392,396},{16,20,24,28..., dimensions={0} | all-to-all | bytes 196608 | tf_op jit(solution)/shard_map/all_to_all | solution.py:404
  241.7 3.7 %shard_map.65 = (bf16[100,4,100]{2,1,0:T(4,128)(2,1)}, f32[100,1,400]{2,1,0:T(1,128)}) custom-call(s32[1]{0:T(128)} %bitcast.x_ref.refs_0_, f32[100,400]{1,0:T(8,128)S(1)} %get-tuple-element.15.refs_1_, bf16[128,384]{1,0:T(8,128)(2,1)S(1)} %slice_bitcast_fusion.1.m_ref.refs_2_, bf16[128,384]{1,0:T(8,128)(2,1)S(1)} %slice_bitcast_fusion.m_ref.refs_3_, ...), custom_call_target="tpu_custom_call" | custom-call | tf_op jit(solution)/shard_map/pallas_call | solution.py:355
  (36 shorter events, 4.2 us)
Async XLA Ops:
  1.5 1.8 copy-start
  1.6 1.8 copy-start.1

commit v11 on v10

--- a/solution.py
+++ b/solution.py
@@ -132,13 +132,12 @@
 
 
 def sketch_term(out_ref, core_ref, sketch_core_ref, partial_of):
-    total = rest = None
+    total = None
     for i in range(core_ref.shape[0]):
         partial = partial_of(core_ref[i]).astype(BF16)
-        term = dot(sketch_core_ref[i], partial[:MAIN], 1, 1)
-        end = dot(partial[MAIN:], sketch_core_ref[i], 1, 1)
-        total, rest = (term, end) if total is None else (total + term, rest + end)
-    write(out_ref, total, rest)
+        term = dot(sketch_core_ref[i], partial, 1, 1)
+        total = term if total is None else total + term
+    write(out_ref, total[:, :MAIN], total[:, MAIN:].T)
 
 
 def first_kernel(x_ref, core_ref, sketch_core_ref, right_ref, left_ref, out_ref, rest_ref):

time: 246 us -> 246 us (level)
  no operation moved by 1% of the time
where the time goes in v11:
time: 246 us; the launch traced here: 245 us
  blocking collectives  220 us (89%)
  Pallas kernels  21 us (9%)
  local copies, waits for them, and re-layouts  2.92 us (1%)
    all_to_all x18, blocking collectives, exchanged(): lax.all_to_all(tiles, AXES, 0, 0, axis_index_groups=groups, tiled=True)  220 us
    pallas_call x7, Pallas kernels, call(): pl.pallas_call(kernel, out_shape=outs, in_specs=specs, out_specs=[pl.Bloc...  21 us

profile of v11, /device:TPU:7, one launch (start us, length us, event | category | flops | bytes accessed | tf_op | source)
XLA Modules:
  0.0 245.5 jit_solution(907153496418704574)
XLA Ops:
  1.6 1.8 copy.12
  4.7 12.1 %all_to_all.90 = bf16[16,8,384]{2,1,0:T(8,128)(2,1)S(1)} all-to-all(bf16[16,8,384]{2,1,0:T(8,128)(2,1)S(1)} %bitcast.49), channel_id=1, replica_groups={{0,4,8,12,128,132,136,140,256,260,264,268,384,388,392,396},{16,20,24,28..., dimensions={0} | all-to-all | bytes 196608 | tf_op jit(solution)/shard_map/all_to_all | solution.py:403
  16.9 25.5 %all_to_all.91 = bf16[8,8,384]{2,1,0:T(8,128)(2,1)S(1)} all-to-all(bf16[8,8,384]{2,1,0:T(8,128)(2,1)S(1)} %broadcast_in_dim.39), channel_id=1, replica_groups={{3,19,35,51,79,95,111,127},{7,23,39,55,75,91,107,123},{11,27,43,59,71,8..., dimensions={0} | all-to-all | bytes 98304 | tf_op jit(solution)/shard_map/all_to_all | solution.py:403
  42.4 10.3 %all_to_all.92 = bf16[32,8,384]{2,1,0:T(8,128)(2,1)S(1)} all-to-all(bf16[32,8,384]{2,1,0:T(8,128)(2,1)S(1)} %broadcast_in_dim.40), channel_id=1, replica_groups={{3,7,11,15,131,135,139,143,259,263,267,271,387,391,395,399,2,6,10,14,13..., dimensions={0} | all-to-all | bytes 393216 | tf_op jit(solution)/shard_map/all_to_all | solution.py:403
  54.3 8.9 %all_to_all.93 = bf16[16,8,384]{2,1,0:T(8,128)(2,1)S(1)} all-to-all(bf16[16,8,384]{2,1,0:T(8,128)(2,1)S(1)} %bitcast.46), channel_id=1, replica_groups={{0,4,8,12,128,132,136,140,256,260,264,268,384,388,392,396},{16,20,24,28..., dimensions={0} | all-to-all | bytes 196608 | tf_op jit(solution)/shard_map/all_to_all | solution.py:403
  63.3 7.7 %all_to_all.94 = bf16[8,8,384]{2,1,0:T(8,128)(2,1)S(1)} all-to-all(bf16[8,8,384]{2,1,0:T(8,128)(2,1)S(1)} %broadcast_in_dim.41), channel_id=1, replica_groups={{2,18,34,50,78,94,110,126},{6,22,38,54,74,90,106,122},{10,26,42,58,70,8..., dimensions={0} | all-to-all | bytes 98304 | tf_op jit(solution)/shard_map/all_to_all | solution.py:403
  71.0 13.7 %all_to_all.95 = bf16[32,8,384]{2,1,0:T(8,128)(2,1)S(1)} all-to-all(bf16[32,8,384]{2,1,0:T(8,128)(2,1)S(1)} %broadcast_in_dim.42), channel_id=1, replica_groups={{2,6,10,14,130,134,138,142,258,262,266,270,386,390,394,398,1,5,9,13,129..., dimensions={0} | all-to-all | bytes 393216 | tf_op jit(solution)/shard_map/all_to_all | solution.py:403
  84.7 1.6 shard_map.61
  86.3 9.3 %all_to_all.96 = bf16[16,8,384]{2,1,0:T(8,128)(2,1)S(1)} all-to-all(bf16[16,8,384]{2,1,0:T(8,128)(2,1)S(1)} %bitcast.44), channel_id=1, replica_groups={{0,4,8,12,128,132,136,140,256,260,264,268,384,388,392,396},{16,20,24,28..., dimensions={0} | all-to-all | bytes 196608 | tf_op jit(solution)/shard_map/all_to_all | solution.py:403
  95.7 7.7 %all_to_all.97 = bf16[8,8,384]{2,1,0:T(8,128)(2,1)S(1)} all-to-all(bf16[8,8,384]{2,1,0:T(8,128)(2,1)S(1)} %broadcast_in_dim.43), channel_id=1, replica_groups={{1,17,33,49,77,93,109,125},{5,21,37,53,73,89,105,121},{9,25,41,57,69,85..., dimensions={0} | all-to-all | bytes 98304 | tf_op jit(solution)/shard_map/all_to_all | solution.py:403
  103.5 13.0 %all_to_all.98 = bf16[32,8,384]{2,1,0:T(8,128)(2,1)S(1)} all-to-all(bf16[32,8,384]{2,1,0:T(8,128)(2,1)S(1)} %broadcast_in_dim.44), channel_id=1, replica_groups={{1,5,9,13,129,133,137,141,257,261,265,269,385,389,393,397,0,4,8,12,128,..., dimensions={0} | all-to-all | bytes 393216 | tf_op jit(solution)/shard_map/all_to_all | solution.py:403
  116.5 4.7 %shard_map.62 = (bf16[128,384]{1,0:T(8,128)(2,1)S(1)}, f32[4,100,100]{2,1,0:T(8,128)S(1)}, f32[100,400]{1,0:T(8,128)S(1)}) custom-call(bf16[128,384]{1,0:T(8,128)(2,1)S(1)} %slice_bitcast_fusion.5.sketch_ref.upper_ref.before_ref.refs_7_, bf16[128,384]{1,0:T(8,128)(2,1)S(1)} %get-tuple-element.25.rest_ref, ...), custom_call_target="tpu_custom_call" | custom-call | tf_op jit(solution)/shard_map/pallas_call | solution.py:354
  121.2 9.3 %all_to_all.99 = bf16[16,8,384]{2,1,0:T(8,128)(2,1)S(1)} all-to-all(bf16[16,8,384]{2,1,0:T(8,128)(2,1)S(1)} %bitcast.47), channel_id=1, replica_groups={{0,4,8,12,128,132,136,140,256,260,264,268,384,388,392,396},{16,20,24,28..., dimensions={0} | all-to-all | bytes 196608 | tf_op jit(solution)/shard_map/all_to_all | solution.py:403
  130.6 7.7 %all_to_all.100 = bf16[8,8,384]{2,1,0:T(8,128)(2,1)S(1)} all-to-all(bf16[8,8,384]{2,1,0:T(8,128)(2,1)S(1)} %broadcast_in_dim.45), channel_id=1, replica_groups={{1,17,33,49,77,93,109,125},{5,21,37,53,73,89,105,121},{9,25,41,57,69,85..., dimensions={0} | all-to-all | bytes 98304 | tf_op jit(solution)/shard_map/all_to_all | solution.py:403
  138.4 13.0 %all_to_all.101 = bf16[32,8,384]{2,1,0:T(8,128)(2,1)S(1)} all-to-all(bf16[32,8,384]{2,1,0:T(8,128)(2,1)S(1)} %broadcast_in_dim.46), channel_id=1, replica_groups={{1,5,9,13,129,133,137,141,257,261,265,269,385,389,393,397,2,6,10,14,130..., dimensions={0} | all-to-all | bytes 393216 | tf_op jit(solution)/shard_map/all_to_all | solution.py:403
  151.4 4.1 %shard_map.63 = (bf16[128,384]{1,0:T(8,128)(2,1)S(1)}, f32[4,100,100]{2,1,0:T(8,128)S(1)}) custom-call(bf16[128,384]{1,0:T(8,128)(2,1)S(1)} %slice_bitcast_fusion.1.m_ref.refs_2_, bf16[128,384]{1,0:T(8,128)(2,1)S(1)} %slice_bitcast_fusion.4.sketch_ref.before_ref.refs_6_, bf16[4,400,400]{2,1,0:T(8,128)(2,1)S(1)} %bitcast.37, ...), custom_call_target="tpu_custom_call" | custom-call | tf_op jit(solution)/shard_map/pallas_call | solution.py:354
  155.5 9.3 %all_to_all.102 = bf16[16,8,384]{2,1,0:T(8,128)(2,1)S(1)} all-to-all(bf16[16,8,384]{2,1,0:T(8,128)(2,1)S(1)} %bitcast.50), channel_id=1, replica_groups={{0,4,8,12,128,132,136,140,256,260,264,268,384,388,392,396},{16,20,24,28..., dimensions={0} | all-to-all | bytes 196608 | tf_op jit(solution)/shard_map/all_to_all | solution.py:403
  164.8 7.7 %all_to_all.103 = bf16[8,8,384]{2,1,0:T(8,128)(2,1)S(1)} all-to-all(bf16[8,8,384]{2,1,0:T(8,128)(2,1)S(1)} %broadcast_in_dim.47), channel_id=1, replica_groups={{2,18,34,50,78,94,110,126},{6,22,38,54,74,90,106,122},{10,26,42,58,70,8..., dimensions={0} | all-to-all | bytes 98304 | tf_op jit(solution)/shard_map/all_to_all | solution.py:403
  172.6 31.9 %all_to_all.104 = bf16[32,8,384]{2,1,0:T(8,128)(2,1)S(1)} all-to-all(bf16[32,8,384]{2,1,0:T(8,128)(2,1)S(1)} %broadcast_in_dim.48), channel_id=1, replica_groups={{2,6,10,14,130,134,138,142,258,262,266,270,386,390,394,398,3,7,11,15,13..., dimensions={0} | all-to-all | bytes 393216 | tf_op jit(solution)/shard_map/all_to_all | solution.py:403
  204.5 4.0 %shard_map.64 = (bf16[128,384]{1,0:T(8,128)(2,1)S(1)}, f32[4,100,100]{2,1,0:T(8,128)S(1)}) custom-call(s32[1]{0:T(128)} %bitcast.x_ref.refs_0_, bf16[128,384]{1,0:T(8,128)(2,1)S(1)} %slice_bitcast_fusion.m_ref.refs_3_, bf16[128,384]{1,0:T(8,128)(2,1)S(1)} %slice_bitcast_fusion.5.sketch_ref.upper_ref.before_ref.refs_7_, bf16[4,400,400]{2,1,0:T(8,128)(2,1)S(1)} %bitcast.38, ...), custom_call_target="tpu_custom_call" | custom-call | tf_op jit(solution)/shard_map/pallas_call | solution.py:354
  208.5 9.0 %all_to_all.105 = bf16[16,8,384]{2,1,0:T(8,128)(2,1)S(1)} all-to-all(bf16[16,8,384]{2,1,0:T(8,128)(2,1)S(1)} %bitcast.48), channel_id=1, replica_groups={{0,4,8,12,128,132,136,140,256,260,264,268,384,388,392,396},{16,20,24,28..., dimensions={0} | all-to-all | bytes 196608 | tf_op jit(solution)/shard_map/all_to_all | solution.py:403
  217.6 15.5 %all_to_all.106 = bf16[8,8,384]{2,1,0:T(8,128)(2,1)S(1)} all-to-all(bf16[8,8,384]{2,1,0:T(8,128)(2,1)S(1)} %broadcast_in_dim.49), channel_id=1, replica_groups={{3,19,35,51,79,95,111,127},{7,23,39,55,75,91,107,123},{11,27,43,59,71,8..., dimensions={0} | all-to-all | bytes 98304 | tf_op jit(solution)/shard_map/all_to_all | solution.py:403
  233.1 8.7 %all_to_all.107 = bf16[16,8,384]{2,1,0:T(8,128)(2,1)S(1)} all-to-all(bf16[16,8,384]{2,1,0:T(8,128)(2,1)S(1)} %broadcast_in_dim.50), channel_id=1, replica_groups={{0,4,8,12,128,132,136,140,256,260,264,268,384,388,392,396},{16,20,24,28..., dimensions={0} | all-to-all | bytes 196608 | tf_op jit(solution)/shard_map/all_to_all | solution.py:403
  241.8 3.7 %shard_map.65 = (bf16[100,4,100]{2,1,0:T(4,128)(2,1)}, f32[100,1,400]{2,1,0:T(1,128)}) custom-call(s32[1]{0:T(128)} %bitcast.x_ref.refs_0_, f32[100,400]{1,0:T(8,128)S(1)} %get-tuple-element.15.refs_1_, bf16[128,384]{1,0:T(8,128)(2,1)S(1)} %slice_bitcast_fusion.1.m_ref.refs_2_, bf16[128,384]{1,0:T(8,128)(2,1)S(1)} %slice_bitcast_fusion.m_ref.refs_3_, ...), custom_call_target="tpu_custom_call" | custom-call | tf_op jit(solution)/shard_map/pallas_call | solution.py:354
  (36 shorter events, 4.2 us)
Async XLA Ops:
  1.5 1.8 copy-start
  1.6 1.8 copy-start.1
